TPU v7x, 32 devices: a whole 2x2x4 slice. The times are simulated.
32 devices in a mesh: fsdp: 8 (over z, x), ctx: 2 (over y), tp: 2 (over core).
Axes of the slice: x: 2, y: 2, z: 4, core: 2. Of those that a mesh axis runs over, the one named last changes fastest.
Arguments:
- hidden_in: bfloat16 [1024, 8, 768], P('ctx', 'fsdp'), may hold values from -6 to 6
- first_values: bfloat16 [1024, 8, 384], P('ctx', 'fsdp', 'tp'), may hold values from -6 to 6
- span_table: int32 [2, 2], replicated, may hold values from 0 to 3, as said below
- w_query: bfloat16 [768, 768], P('fsdp', 'tp'), may hold values from -0.21875 to 0.21875
- w_key: bfloat16 [768, 768], P('fsdp', 'tp'), may hold values from -0.21875 to 0.21875
- w_value: bfloat16 [768, 384], P('fsdp', 'tp'), may hold values from -0.21875 to 0.21875
- w_out: bfloat16 [768, 768], P('fsdp', 'tp'), may hold values from -3 to 3
- w_up: bfloat16 [768, 3072], P('fsdp', 'tp'), may hold values from -0.21875 to 0.21875
- w_down: bfloat16 [768, 3072], P('fsdp', 'tp'), may hold values from -0.109375 to 0.109375
- gain_attn: bfloat16 [768], P('fsdp'), may hold values from 0.5 to 1.5
- shift_attn: bfloat16 [768], P('fsdp'), may hold values from -1.5 to 1.5
- gain_mlp: bfloat16 [768], P('fsdp'), may hold values from 0.5 to 1.5
- shift_mlp: bfloat16 [768], P('fsdp'), may hold values from -1.5 to 1.5
- cotangent: bfloat16 [1024, 8, 768], P('ctx', 'fsdp'), may hold values from -6 to 6
Outputs:
- out_hidden: float32 [1024, 8, 768], P('ctx', 'fsdp')
- grad_hidden: float32 [1024, 8, 768], P('ctx', 'fsdp')
- grad_first: float32 [1024, 8, 384], P('ctx', 'fsdp', 'tp')
- grad_query: float32 [768, 768], P('fsdp', 'tp')
- grad_key: float32 [768, 768], P('fsdp', 'tp')
- grad_value: float32 [768, 384], P('fsdp', 'tp')
- grad_outproj: float32 [768, 768], P('fsdp', 'tp')
- grad_up: float32 [768, 3072], P('fsdp', 'tp')
- grad_down: float32 [768, 3072], P('fsdp', 'tp')
- grad_gain_attn: float32 [768], P('fsdp')
- grad_shift_attn: float32 [768], P('fsdp')
- grad_gain_mlp: float32 [768], P('fsdp')
- grad_shift_mlp: float32 [768], P('fsdp')
Inputs may be any that keep to these rules, and one draw needn't show every extreme that they name: `span_table`: every span number appears exactly once in the table.
All inputs are finite; a program needn't handle non-finite values.
Results may differ from a plain program's by a relative error of at most 0.02.
Values may be sent and summed in bfloat16 or wider, within the bound.
No kernel may reach another device: no remote copies, remote signals or barrier semaphores. Data moves between devices by JAX's collectives and lax.ppermute only.
A program may use at most 128 MiB of HBM per device.

v0:
```python
import jax
import jax.numpy as jnp
from jax import lax
from jax.sharding import PartitionSpec as P

HEADS = 12
HEAD_DIM = 64


eps_norm = 1e-05
big_negative = -1e30
gelu_coef = 0.7978845608028654
cube_coef = 0.044715


def passed_along(value, axis, steps):
    count = lax.axis_size(axis)
    pairs = [(source, (source + steps) % count) for source in range(count)]
    return lax.ppermute(value, axis, pairs)


def normalize_rows(values):
    mean = jnp.mean(values, axis=-1, keepdims=True)
    centred = values - mean
    inverse = lax.rsqrt(jnp.mean(centred * centred, axis=-1, keepdims=True) + eps_norm)
    return (centred * inverse, inverse)


def normalize_back(d_norm, unit, inverse, gain):
    scaled = d_norm * gain
    inner = (
        scaled
        - jnp.mean(scaled, axis=-1, keepdims=True)
        - unit * jnp.mean(scaled * unit, axis=-1, keepdims=True)
    )
    return inverse * inner


def gelu_forward(values):
    return (
        0.5 * values * (1.0 + jnp.tanh(gelu_coef * (values + cube_coef * values * values * values)))
    )


def gelu_slope(values):
    tanh_val = jnp.tanh(gelu_coef * (values + cube_coef * values * values * values))
    return 0.5 * (1.0 + tanh_val) + 0.5 * values * (1.0 - tanh_val * tanh_val) * gelu_coef * (
        1.0 + 3.0 * cube_coef * values * values
    )


def contract_rows(left, right):
    return lax.dot_general(
        left, right, (((0,), (0,)), ((), ())), preferred_element_type=jnp.float32
    )


def contract_cols(left, right):
    return lax.dot_general(
        left, right, (((1,), (1,)), ((), ())), preferred_element_type=jnp.float32
    )


def block_scores(query, keys, q_places, k_places, scale):
    scores = jnp.einsum("qshe,kshe->shqk", query, keys, preferred_element_type=jnp.float32) * scale
    allowed = k_places[None, None, None, :] <= q_places[None, None, :, None]
    return (jnp.where(allowed, scores, big_negative), allowed)


def absorb_block(state, query, q_places, k_block, v_block, p_block, scale):
    top, total, summed = state
    scores, allowed = block_scores(query, k_block, q_places, p_block, scale)
    new_top = jnp.maximum(top, jnp.max(scores, axis=-1))
    factor = jnp.exp(top - new_top)
    weights = jnp.where(allowed, jnp.exp(scores - new_top[..., None]), 0.0)
    total = total * factor + jnp.sum(weights, axis=-1)
    update = jnp.einsum(
        "shqk,kshe->qshe", weights.astype(jnp.bfloat16), v_block, preferred_element_type=jnp.float32
    )
    summed = summed * jnp.transpose(factor, (2, 0, 1))[..., None] + update
    return (new_top, total, summed)


def make_absorb(query, q_places, places_all, scale):
    rows, seqs, heads, width = query.shape

    def absorb(carry, piece, start):
        keys, values = piece
        pairs = keys.shape[0] // rows
        k_pairs = keys.reshape(pairs, rows, seqs, heads, width)
        v_pairs = values.reshape(pairs, rows, seqs, heads, width)
        p_pairs = places_all.reshape(pairs, rows)

        def one_pair(state, item):
            k_pair, v_pair, p_pair = item
            return (absorb_block(state, query, q_places, k_pair, v_pair, p_pair, scale), None)

        carry, _ = lax.scan(one_pair, carry, (k_pairs, v_pairs, p_pairs))
        return carry

    return absorb


def grad_block(query, d_mixed, delta, log_total, q_places, k_block, v_block, p_block, scale):
    scores, allowed = block_scores(query, k_block, q_places, p_block, scale)
    weights = jnp.where(allowed, jnp.exp(scores - log_total[..., None]), 0.0)
    d_weights = jnp.einsum("qshe,kshe->shqk", d_mixed, v_block, preferred_element_type=jnp.float32)
    d_scores = (weights * (d_weights - delta[..., None])).astype(jnp.bfloat16)
    part_query = jnp.einsum(
        "shqk,kshe->qshe", d_scores, k_block, preferred_element_type=jnp.float32
    )
    part_key = jnp.einsum("shqk,qshe->kshe", d_scores, query, preferred_element_type=jnp.float32)
    part_value = jnp.einsum(
        "shqk,qshe->kshe", weights.astype(jnp.bfloat16), d_mixed, preferred_element_type=jnp.float32
    )
    return (part_query, part_key, part_value)


def grad_pair(query, d_mixed, delta, log_total, q_places, k_shard, v_shard, p_shard, scale):
    return grad_block(query, d_mixed, delta, log_total, q_places, k_shard, v_shard, p_shard, scale)


def local(
    hidden_in,
    first_values,
    span_table,
    w_query,
    w_key,
    w_value,
    w_out,
    w_up,
    w_down,
    gain_attn,
    shift_attn,
    gain_mlp,
    shift_mlp,
    cotangent,
):
    rows, seqs, width = hidden_in.shape
    count = rows * seqs
    ranks = lax.axis_size("ctx")
    rank = lax.axis_index("ctx")
    span_rows = rows // 2
    local_heads = HEADS // lax.axis_size("tp")
    head_cols = local_heads * HEAD_DIM
    scale = HEAD_DIM ** (-0.5)
    places_all = (
        jnp.repeat(span_table.reshape(-1), span_rows) * span_rows
        + jnp.arange(ranks * rows, dtype=jnp.int32) % span_rows
    )
    q_places = lax.dynamic_slice_in_dim(places_all, rank * rows, rows)
    x_rows = hidden_in.reshape(count, width).astype(jnp.float32)
    unit_one, inverse_one = normalize_rows(x_rows)
    wq_full, wk_full, wv_full, wo_full, gain_one, shift_one = (
        lax.all_gather(w_query, "fsdp", axis=0, tiled=True),
        lax.all_gather(w_key, "fsdp", axis=0, tiled=True),
        lax.all_gather(w_value, "fsdp", axis=0, tiled=True),
        lax.all_gather(w_out, "fsdp", axis=0, tiled=True),
        lax.all_gather(gain_attn, "fsdp", axis=0, tiled=True),
        lax.all_gather(shift_attn, "fsdp", axis=0, tiled=True),
    )
    gain_one = gain_one.astype(jnp.float32)
    h_one = (unit_one * gain_one + shift_one.astype(jnp.float32)).astype(jnp.bfloat16)
    query = jnp.dot(h_one, wq_full, preferred_element_type=jnp.float32).astype(jnp.bfloat16)
    keys = jnp.dot(h_one, wk_full, preferred_element_type=jnp.float32).astype(jnp.bfloat16)
    fresh = jnp.dot(h_one, wv_full, preferred_element_type=jnp.float32).astype(jnp.bfloat16)
    fresh_heads = fresh.reshape(rows, seqs, local_heads // 2, HEAD_DIM)
    reused_heads = first_values.reshape(rows, seqs, local_heads // 2, HEAD_DIM)
    values = jnp.stack([fresh_heads, reused_heads], axis=3).reshape(rows, seqs, head_cols)
    keys_sent = keys.reshape(rows, seqs, head_cols)
    query4 = query.reshape(rows, seqs, local_heads, HEAD_DIM)
    absorb = make_absorb(query4, q_places, places_all, scale)
    start_state = (
        jnp.full((seqs, local_heads, rows), big_negative, jnp.float32),
        jnp.zeros((seqs, local_heads, rows), jnp.float32),
        jnp.zeros((rows, seqs, local_heads, HEAD_DIM), jnp.float32),
    )
    top, total, summed = absorb(
        start_state,
        (
            lax.all_gather(keys_sent, "ctx", axis=0, tiled=True),
            lax.all_gather(values, "ctx", axis=0, tiled=True),
        ),
        jnp.int32(0),
    )
    mixed_exact = summed / jnp.transpose(total, (2, 0, 1))[..., None]
    log_total = top + jnp.log(total)
    mixed = mixed_exact.reshape(count, head_cols).astype(jnp.bfloat16)
    resid = x_rows + lax.psum(contract_cols(mixed, wo_full).astype(jnp.bfloat16), "tp").astype(
        jnp.float32
    )
    unit_two, inverse_two = normalize_rows(resid)
    wu_full, wd_full, gain_two, shift_two = (
        lax.all_gather(w_up, "fsdp", axis=0, tiled=True),
        lax.all_gather(w_down, "fsdp", axis=0, tiled=True),
        lax.all_gather(gain_mlp, "fsdp", axis=0, tiled=True),
        lax.all_gather(shift_mlp, "fsdp", axis=0, tiled=True),
    )
    gain_two = gain_two.astype(jnp.float32)
    h_two = (unit_two * gain_two + shift_two.astype(jnp.float32)).astype(jnp.bfloat16)
    upper = jnp.dot(h_two, wu_full, preferred_element_type=jnp.float32)
    act = gelu_forward(upper).astype(jnp.bfloat16)
    out_rows = resid + lax.psum(contract_cols(act, wd_full).astype(jnp.bfloat16), "tp").astype(
        jnp.float32
    )
    d_out = cotangent.reshape(count, width)
    grad_down = contract_rows(d_out, act)
    d_act = jnp.dot(d_out, wd_full, preferred_element_type=jnp.float32)
    d_upper = (d_act * gelu_slope(upper)).astype(jnp.bfloat16)
    grad_up = contract_rows(h_two, d_upper)
    d_two = lax.psum(contract_cols(d_upper, wu_full).astype(jnp.bfloat16), "tp").astype(jnp.float32)
    grad_gain_mlp = jnp.sum(d_two * unit_two, axis=0)
    grad_shift_mlp = jnp.sum(d_two, axis=0)
    d_resid = d_out.astype(jnp.float32) + normalize_back(d_two, unit_two, inverse_two, gain_two)
    d_branch = d_resid.astype(jnp.bfloat16)
    grad_outproj = contract_rows(d_branch, mixed)
    d_mixed = jnp.dot(d_branch, wo_full, preferred_element_type=jnp.float32).astype(jnp.bfloat16)
    d_mixed4 = d_mixed.reshape(rows, seqs, local_heads, HEAD_DIM)
    delta = jnp.transpose(jnp.sum(d_mixed4.astype(jnp.float32) * mixed_exact, axis=-1), (1, 2, 0))
    zero_query = jnp.zeros((rows, seqs, local_heads, HEAD_DIM), jnp.float32)
    zero_keys = jnp.zeros((rows, seqs, head_cols), jnp.float32)

    def visit(step, state):
        moving_k, moving_v, acc_k, acc_v, acc_q = state
        source = (rank - step) % ranks
        p_block = lax.dynamic_slice_in_dim(places_all, source * rows, rows)
        part_q, part_k, part_v = grad_pair(
            query4,
            d_mixed4,
            delta,
            log_total,
            q_places,
            moving_k.reshape(rows, seqs, local_heads, HEAD_DIM),
            moving_v.reshape(rows, seqs, local_heads, HEAD_DIM),
            p_block,
            scale,
        )
        acc_k = acc_k + part_k.reshape(rows, seqs, head_cols)
        acc_v = acc_v + part_v.reshape(rows, seqs, head_cols)
        moving_k, moving_v = passed_along((moving_k, moving_v), "ctx", 1)
        acc_k, acc_v = (
            passed_along(acc_k.astype(jnp.bfloat16), "ctx", 1).astype(acc_k.dtype),
            passed_along(acc_v.astype(jnp.bfloat16), "ctx", 1).astype(acc_v.dtype),
        )
        return (moving_k, moving_v, acc_k, acc_v, acc_q + part_q)

    final_state = lax.fori_loop(
        0, ranks, visit, (keys_sent, values, zero_keys, zero_keys, zero_query)
    )
    d_keys = final_state[2]
    d_values = final_state[3]
    d_query = final_state[4]
    d_query_low = (d_query * scale).reshape(count, head_cols).astype(jnp.bfloat16)
    d_keys_low = (d_keys * scale).reshape(count, head_cols).astype(jnp.bfloat16)
    split_values = d_values.reshape(rows, seqs, local_heads // 2, 2, HEAD_DIM)
    d_fresh = split_values[:, :, :, 0, :].reshape(count, head_cols // 2).astype(jnp.bfloat16)
    grad_first = split_values[:, :, :, 1, :].reshape(rows, seqs, head_cols // 2)
    grad_query = contract_rows(h_one, d_query_low)
    grad_key = contract_rows(h_one, d_keys_low)
    grad_value = contract_rows(h_one, d_fresh)
    d_part = (
        contract_cols(d_query_low, wq_full)
        + contract_cols(d_keys_low, wk_full)
        + contract_cols(d_fresh, wv_full)
    )
    d_one = lax.psum(d_part.astype(jnp.bfloat16), "tp").astype(jnp.float32)
    grad_gain_attn = jnp.sum(d_one * unit_one, axis=0)
    grad_shift_attn = jnp.sum(d_one, axis=0)
    d_input = d_resid + normalize_back(d_one, unit_one, inverse_one, gain_one)
    shared = (
        lax.psum_scatter(
            grad_query.astype(jnp.bfloat16), "fsdp", scatter_dimension=0, tiled=True
        ).astype(jnp.float32),
        lax.psum_scatter(
            grad_key.astype(jnp.bfloat16), "fsdp", scatter_dimension=0, tiled=True
        ).astype(jnp.float32),
        lax.psum_scatter(
            grad_value.astype(jnp.bfloat16), "fsdp", scatter_dimension=0, tiled=True
        ).astype(jnp.float32),
        lax.psum_scatter(
            grad_outproj.astype(jnp.bfloat16), "fsdp", scatter_dimension=0, tiled=True
        ).astype(jnp.float32),
        lax.psum_scatter(
            grad_up.astype(jnp.bfloat16), "fsdp", scatter_dimension=0, tiled=True
        ).astype(jnp.float32),
        lax.psum_scatter(
            grad_down.astype(jnp.bfloat16), "fsdp", scatter_dimension=0, tiled=True
        ).astype(jnp.float32),
        lax.psum_scatter(
            grad_gain_attn.astype(jnp.bfloat16), "fsdp", scatter_dimension=0, tiled=True
        ).astype(jnp.float32),
        lax.psum_scatter(
            grad_shift_attn.astype(jnp.bfloat16), "fsdp", scatter_dimension=0, tiled=True
        ).astype(jnp.float32),
        lax.psum_scatter(
            grad_gain_mlp.astype(jnp.bfloat16), "fsdp", scatter_dimension=0, tiled=True
        ).astype(jnp.float32),
        lax.psum_scatter(
            grad_shift_mlp.astype(jnp.bfloat16), "fsdp", scatter_dimension=0, tiled=True
        ).astype(jnp.float32),
    )
    summed_grads = (
        lax.psum(shared[0].astype(jnp.bfloat16), "ctx").astype(jnp.float32),
        lax.psum(shared[1].astype(jnp.bfloat16), "ctx").astype(jnp.float32),
        lax.psum(shared[2].astype(jnp.bfloat16), "ctx").astype(jnp.float32),
        lax.psum(shared[3].astype(jnp.bfloat16), "ctx").astype(jnp.float32),
        lax.psum(shared[4].astype(jnp.bfloat16), "ctx").astype(jnp.float32),
        lax.psum(shared[5].astype(jnp.bfloat16), "ctx").astype(jnp.float32),
        lax.psum(shared[6].astype(jnp.bfloat16), "ctx").astype(jnp.float32),
        lax.psum(shared[7].astype(jnp.bfloat16), "ctx").astype(jnp.float32),
        lax.psum(shared[8].astype(jnp.bfloat16), "ctx").astype(jnp.float32),
        lax.psum(shared[9].astype(jnp.bfloat16), "ctx").astype(jnp.float32),
    )
    return (
        out_rows.reshape(rows, seqs, width),
        d_input.reshape(rows, seqs, width),
        grad_first,
        summed_grads[0],
        summed_grads[1],
        summed_grads[2],
        summed_grads[3],
        summed_grads[4],
        summed_grads[5],
        summed_grads[6],
        summed_grads[7],
        summed_grads[8],
        summed_grads[9],
    )


def solution(mesh):
    return jax.shard_map(
        local,
        mesh=mesh,
        in_specs=(
            P("ctx", "fsdp", None),
            P("ctx", "fsdp", "tp"),
            P(),
            P("fsdp", "tp"),
            P("fsdp", "tp"),
            P("fsdp", "tp"),
            P("fsdp", "tp"),
            P("fsdp", "tp"),
            P("fsdp", "tp"),
            P("fsdp"),
            P("fsdp"),
            P("fsdp"),
            P("fsdp"),
            P("ctx", "fsdp", None),
        ),
        out_specs=(
            P("ctx", "fsdp", None),
            P("ctx", "fsdp", None),
            P("ctx", "fsdp", "tp"),
            P("fsdp", "tp"),
            P("fsdp", "tp"),
            P("fsdp", "tp"),
            P("fsdp", "tp"),
            P("fsdp", "tp"),
            P("fsdp", "tp"),
            P("fsdp"),
            P("fsdp"),
            P("fsdp"),
            P("fsdp"),
        ),
        check_vma=False,
    )
```

profile of v0, /device:TPU:0, one launch (start us, length us, event | category | flops | bytes accessed | tf_op | source)
XLA Modules:
  0.0 905.0 jit_solution(15849868233037522959)
XLA Ops:
  14.2 23.3 %all-reduce.9 = (bf16[768]{0:T(1024)(128)(2,1)S(1)}, bf16[768]{0:T(1024)(128)(2,1)S(1)}, bf16[768]{0:T(1024)(128)(2,1)S(1)}, bf16[768]{0:T(1024)(128)(2,1)S(1)}) all-reduce(bf16[768]{0:T(1024)(128)(2,1)S(1)} %dynamic-update-slice.3, bf16[768]{0:T(1024)(128)(2,1)S(1)} %dynamic-update-slice.2, ...), channel_id=1, replica_groups=mesh['fsdp'=8,'ctx'=2,'tp'=2] {'fsdp'}, use_global_device_ids=true, to_apply=%add.3 | all-reduce | flops 3072 | bytes 12288
  37.6 31.2 %all_gather.41 = bf16[768,192]{1,0:T(8,128)(2,1)S(1)} all-gather(bf16[96,192]{1,0:T(8,128)(2,1)S(1)} %copy-done.32), channel_id=1, replica_groups=mesh['fsdp'=8,'ctx'=2,'tp'=2] {'fsdp'}, dimensions={0}, use_global_device_ids=true | all-gather | bytes 331776 | tf_op jit(solution)/shard_map/all_gather | solution.py:157
  70.4 31.6 %all_gather.40 = bf16[768,384]{1,0:T(8,128)(2,1)S(1)} all-gather(bf16[96,384]{1,0:T(8,128)(2,1)S(1)} %copy-done.29), channel_id=1, replica_groups=mesh['fsdp'=8,'ctx'=2,'tp'=2] {'fsdp'}, dimensions={0}, use_global_device_ids=true | all-gather | bytes 663552 | tf_op jit(solution)/shard_map/all_gather | solution.py:155
  102.9 31.5 %all_gather.38 = bf16[768,384]{1,0:T(8,128)(2,1)S(1)} all-gather(bf16[96,384]{1,0:T(8,128)(2,1)S(1)} %copy-done.30), channel_id=1, replica_groups=mesh['fsdp'=8,'ctx'=2,'tp'=2] {'fsdp'}, dimensions={0}, use_global_device_ids=true | all-gather | bytes 663552 | tf_op jit(solution)/shard_map/all_gather | solution.py:156
  136.1 31.3 %all_gather.43 = bf16[768,384]{1,0:T(8,128)(2,1)S(1)} all-gather(bf16[96,384]{1,0:T(8,128)(2,1)S(1)} %copy-done.31), channel_id=1, replica_groups=mesh['fsdp'=8,'ctx'=2,'tp'=2] {'fsdp'}, dimensions={0}, use_global_device_ids=true | all-gather | bytes 663552 | tf_op jit(solution)/shard_map/all_gather | solution.py:158
  167.4 8.5 all-gather
  180.0 10.2 %all_gather.42 = bf16[1024,1,384]{0,2,1:T(8,128)(2,1)} all-gather(bf16[512,1,384]{0,2,1:T(8,128)(2,1)} %bitcast.5), channel_id=1, replica_groups=mesh['fsdp'=8,'ctx'=2,'tp'=2] {'ctx'}, dimensions={0}, use_global_device_ids=true | all-gather | bytes 1179648 | tf_op jit(solution)/shard_map/all_gather | solution.py:182
  190.2 3.2 reshape.436
  193.4 2.1 copy.50
  195.6 10.1 %while.39 = (s32[]{:T(128)}, f32[1,6,512]{2,1,0:T(8,128)S(1)}, f32[1,6,512]{2,1,0:T(8,128)S(1)}, f32[512,1,6,64]{0,3,2,1:T(8,128)S(1)}, s32[2,512]{1,0:T(2,128)S...) while((s32[]{:T(128)}, f32[1,6,512]{2,1,0:T(8,128)S(1)}, ...), condition=%wide.region_5.6_spmd.clone, body=%wide.region_2.5_spmd.clone.sunk | while | flops 423970816 | bytes 26034344 | solution.py:98
  198.6 2.0 fusion.157
  203.7 2.0 fusion.157
  209.6 13.2 %all-reduce.18.cloned.1.call-done = bf16[512,768]{1,0:T(8,128)(2,1)} async-done(((bf16[512,768]{1,0:T(8,128)(2,1)}), bf16[512,768]{1,0:T(8,128)(2,1)}) %all-reduce.18.cloned.1.call-update) | async-done | bytes 786448 | tf_op jit(solution)/shard_map/psum | solution.py:189
  224.7 33.3 %all-gather.4.cloned.1.call-done = bf16[768,1536]{1,0:T(8,128)(2,1)} async-done(((bf16[96,1536]{1,0:T(8,128)(2,1)}), bf16[768,1536]{1,0:T(8,128)(2,1)}) %all-gather.4.cloned.1.call-update) | async-done | bytes 2359312 | tf_op jit(solution)/shard_map/all_gather | solution.py:194
  258.0 4.8 fusion.85
  262.9 47.5 %all-gather.6.cloned.1.call-done = bf16[768,1536]{1,0:T(8,128)(2,1)} async-done(((bf16[96,1536]{1,0:T(8,128)(2,1)}), bf16[768,1536]{1,0:T(8,128)(2,1)}) %all-gather.6.cloned.1.call-update) | async-done | bytes 2359312 | tf_op jit(solution)/shard_map/all_gather | solution.py:195
  310.3 5.6 fusion.46
  317.1 2.3 convolution_convert_fusion.2
  319.7 5.5 convolution_convert_fusion.3
  325.2 11.9 %all-reduce.20.cloned.1.call-done = bf16[512,768]{1,0:T(8,128)(2,1)} async-done(((bf16[512,768]{1,0:T(8,128)(2,1)}), bf16[512,768]{1,0:T(8,128)(2,1)}) %all-reduce.20.cloned.1.call-update) | async-done | bytes 786448 | tf_op jit(solution)/shard_map/psum | solution.py:211
  337.1 2.7 fusion.70
  341.8 97.1 %while.40 = (s32[]{:T(128)}, bf16[512,1,384]{0,2,1:T(8,128)(2,1)}, bf16[512,1,384]{0,2,1:T(8,128)(2,1)}, f32[512,1,384]{0,2,1:T(8,128)}, f32[512,1,384]{0,2,1:T(...) while((s32[]{:T(128)}, bf16[512,1,384]{0,2,1:T(8,128)(2,1)}, ...), condition=%wide.region_15.16_spmd.clone, body=%wide.region_14.15_spmd.clone.sunk | while | flops 1027735552 | bytes 58831576 | solution.py:247
  341.8 1.9 copy.88
  343.7 1.8 copy.87
  345.8 2.0 fusion.168
  347.9 3.9 multiply_convert_fusion.7
  353.8 1.8 collective-permute-start.2
  355.6 2.8 fusion.171
  359.6 1.8 collective-permute-start
  361.7 3.0 fusion.173
  366.1 2.0 convert_element_type.523
  368.1 6.4 collective-permute-done.3
  374.6 2.0 convert_element_type.524
  376.5 6.4 collective-permute-done
  383.0 7.8 collective-permute-done.1
  390.8 1.9 copy.88
  394.8 2.0 fusion.168
  396.8 3.9 multiply_convert_fusion.7
  404.6 2.8 fusion.171
  410.6 3.2 fusion.173
  415.1 2.0 convert_element_type.523
  417.1 6.4 collective-permute-done.3
  423.5 2.0 convert_element_type.524
  425.5 6.4 collective-permute-done
  432.0 6.9 collective-permute-done.1
  447.3 5.1 fusion.45
  452.4 4.3 copy.57
  459.7 2.7 convolution_convert_fusion.7
  464.3 4.8 convolution_convert_fusion.1
  473.7 2.0 fusion.72
  475.7 21.9 %all-reduce.8 = (bf16[768]{0:T(1024)(128)(2,1)S(1)}, bf16[768]{0:T(1024)(128)(2,1)S(1)}, bf16[768]{0:T(1024)(128)(2,1)S(1)}, bf16[768]{0:T(1024)(128)(2,1)S(1)}) all-reduce(bf16[768]{0:T(1024)(128)(2,1)S(1)} %get-tuple-element.558, bf16[768]{0:T(1024)(128)(2,1)S(1)} %reduce_sum.147, ...), channel_id=9, replica_groups=mesh['fsdp'=8,'ctx'=2,'tp'=2] {'fsdp'}, use_global_device_ids=true, to_apply=%region_32.33.clone | all-reduce | flops 3072 | bytes 12288
  497.9 14.0 %reduce-scatter.13.cloned.1.call-done = bf16[96,192]{1,0:T(8,128)(2,1)} async-done(((bf16[768,192]{1,0:T(8,128)(2,1)}), bf16[96,192]{1,0:T(8,128)(2,1)}) %reduce-scatter.13.cloned.1.call-update) | async-done | bytes 36880 | tf_op jit(solution)/shard_map/reduce_scatter | solution.py:277
  511.9 9.4 %all-reduce.11 = (bf16[96,192]{1,0:T(8,128)(2,1)S(1)}, bf16[96]{0:T(256)(128)(2,1)S(1)}, bf16[96]{0:T(256)(128)(2,1)S(1)}, bf16[96]{0:T(256)(128)(2,1)S(1)}, bf16[96]{0:T(256)(128)(2,1)S(1)}) all-reduce(bf16[96,192]{1,0:T(8,128)(2,1)} %reduce-scatter.13.cloned.1.call-done, ...), channel_id=1, replica_groups=mesh['fsdp'=8,'ctx'=2,'tp'=2] {'ctx'}, use_global_device_ids=true, to_apply=%region_24.25 | all-reduce | flops 18816 | bytes 75264 | tf_op jit(solution)/shard_map/psum | solution.py:305
  523.4 60.8 %reduce-scatter.19.cloned.1.call-done = bf16[96,1536]{1,0:T(8,128)(2,1)} async-done(((bf16[768,1536]{1,0:T(8,128)(2,1)}), bf16[96,1536]{1,0:T(8,128)(2,1)}) %reduce-scatter.19.cloned.1.call-update) | async-done | bytes 294928
  584.2 1.9 copy.58
  586.1 64.0 %reduce-scatter.15.cloned.1.call-done = bf16[96,384]{1,0:T(8,128)(2,1)} async-done(((bf16[768,384]{1,0:T(8,128)(2,1)}), bf16[96,384]{1,0:T(8,128)(2,1)}) %reduce-scatter.15.cloned.1.call-update) | async-done | bytes 73744 | tf_op jit(solution)/shard_map/reduce_scatter | solution.py:280
  650.1 65.7 %reduce-scatter.9.cloned.1.call-done = bf16[96,384]{1,0:T(8,128)(2,1)} async-done(((bf16[768,384]{1,0:T(8,128)(2,1)}), bf16[96,384]{1,0:T(8,128)(2,1)}) %reduce-scatter.9.cloned.1.call-update) | async-done | bytes 73744 | tf_op jit(solution)/shard_map/reduce_scatter | solution.py:271
  715.8 65.6 %reduce-scatter.11.cloned.1.call-done = bf16[96,384]{1,0:T(8,128)(2,1)} async-done(((bf16[768,384]{1,0:T(8,128)(2,1)}), bf16[96,384]{1,0:T(8,128)(2,1)}) %reduce-scatter.11.cloned.1.call-update) | async-done | bytes 73744 | tf_op jit(solution)/shard_map/reduce_scatter | solution.py:274
  781.4 72.2 %reduce-scatter.17.cloned.1.call-done = bf16[96,1536]{1,0:T(8,128)(2,1)} async-done(((bf16[768,1536]{1,0:T(8,128)(2,1)}), bf16[96,1536]{1,0:T(8,128)(2,1)}) %reduce-scatter.17.cloned.1.call-update) | async-done | bytes 294928 | tf_op jit(solution)/shard_map/reduce_scatter | solution.py:283
  853.6 2.1 fusion.64
  855.8 2.8 copy.54
  859.2 2.8 copy.53
  861.9 28.2 %all-reduce.24.cloned.1.call-done = (bf16[96,1536]{0,1:T(8,128)(2,1)}, bf16[96,384]{1,0:T(8,128)(2,1)}, bf16[96,384]{1,0:T(8,128)(2,1)}, bf16[96,384]{1,0:T(8,128)(2,1)}, bf16[96,1536]{1,0:T(8,128)(2,1)}) async-done(((bf16[96,1536]{0,1:T(8,128)(2,1)}, bf16[96,384]{1,0:T(8,128)(2,1)}, bf16[96,384]{1,0:T(8,128)(2,1)}, bf16[96,384]{1,0:T(8,128)(2,1)}, bf16[96,1536]{1,0:T(8,128)(2,1)}), ...) | async-done | bytes 811024 | tf_op jit(solution)/shard_map/psum | solution.py:308
  894.8 2.0 copy.55
  (272 shorter events, 70.0 us)
Async XLA Ops:
  8.0 4.0 copy-start.52
  8.0 60.8 %copy-start = (bf16[512,1,768]{2,0,1:T(8,128)(2,1)S(1)}, bf16[512,1,768]{2,0,1:T(8,128)(2,1)}, u32[]{:S(2)}) copy-start(bf16[512,1,768]{2,0,1:T(8,128)(2,1)} %param.18) | copy-start | bytes 2359300
  8.0 5.2 copy-start.54
  8.0 5.5 copy-start.55
  8.1 5.7 copy-start.56
  8.1 5.9 copy-start.57
  8.1 29.5 %copy-start.32 = (bf16[96,192]{1,0:T(8,128)(2,1)S(1)}, bf16[96,192]{1,0:T(8,128)(2,1)}, u32[]{:S(2)}) copy-start(bf16[96,192]{1,0:T(8,128)(2,1)} %param.23) | copy-start | bytes 110596
  8.1 214.7 %all-reduce.18.cloned.1.call-start = ((), (), s32[]{:S(2)}) async-start(), calls=%async_computation.6 | async-start | bytes 1572864 | tf_op jit(solution)/shard_map/psum | solution.py:189
  10.4 124.0 %copy-start.35 = (f32[512]{0:T(512)}, f32[512]{0:T(512)S(1)}, u32[]{:S(2)}) copy-start(f32[512]{0:T(512)S(1)} %broadcast_multiply_fusion.5) | copy-start | bytes 6148
  11.9 122.5 %copy-start.39 = (f32[512]{0:T(512)}, f32[512]{0:T(512)S(1)}, u32[]{:S(2)}) copy-start(f32[512]{0:T(512)S(1)} %add_rsqrt_fusion.1) | copy-start | bytes 6148
  11.9 57.7 %copy-start.28 = (bf16[512,1,192]{0,2,1:T(8,128)(2,1)S(1)}, bf16[512,1,192]{0,2,1:T(8,128)(2,1)}, u32[]{:S(2)}) copy-start(bf16[512,1,192]{0,2,1:T(8,128)(2,1)} %param.19) | copy-start | bytes 589828
  37.6 96.8 %copy-start.47 = (f32[768]{0:T(1024)}, f32[768]{0:T(1024)S(1)}, u32[]{:S(2)}) copy-start(f32[768]{0:T(1024)S(1)} %convert_element_type.268) | copy-start | bytes 9220
  136.1 31.3 %copy-start.20 = (bf16[512,384]{1,0:T(8,128)(2,1)}, bf16[512,384]{1,0:T(8,128)(2,1)S(1)}, u32[]{:S(2)}) copy-start(bf16[512,384]{1,0:T(8,128)(2,1)S(1)} %convolution_convert_fusion.11) | copy-start | bytes 1179652
  205.8 2.7 copy-start.11
  205.8 2.8 copy-start.21
  207.3 50.7 %all-gather.4.cloned.1.call-start = ((), (), s32[]{:S(2)}) async-start(), calls=%async_computation.7 | async-start | bytes 2654208 | tf_op jit(solution)/shard_map/all_gather | solution.py:194
  207.9 102.4 %all-gather.6.cloned.1.call-start = ((), (), s32[]{:S(2)}) async-start(), calls=%async_computation.8 | async-start | bytes 2654208 | tf_op jit(solution)/shard_map/all_gather | solution.py:195
  208.5 128.6 %all-reduce.20.cloned.1.call-start = ((), (), s32[]{:S(2)}) async-start(), calls=%async_computation.9 | async-start | bytes 1572864 | tf_op jit(solution)/shard_map/psum | solution.py:211
  208.6 49.5 %copy-start.50 = (f32[768]{0:T(1024)}, f32[768]{0:T(1024)S(1)}, u32[]{:S(2)}) copy-start(f32[768]{0:T(1024)S(1)} %convert_element_type.278) | copy-start | bytes 9220
  224.3 115.6 %copy-start.33 = (f32[512]{0:T(512)}, f32[512]{0:T(512)S(1)}, u32[]{:S(2)}) copy-start(f32[512]{0:T(512)S(1)} %broadcast_multiply_fusion.4) | copy-start | bytes 6148
  224.7 115.2 %copy-start.37 = (f32[512]{0:T(512)}, f32[512]{0:T(512)S(1)}, u32[]{:S(2)}) copy-start(f32[512]{0:T(512)S(1)} %add_rsqrt_fusion) | copy-start | bytes 6148
  310.3 6.8 copy-start.53
  319.4 152.9 %all-reduce.22.cloned.1.call-start = ((), (), s32[]{:S(2)}) async-start(), calls=%async_computation.16 | async-start | bytes 3145728 | tf_op jit(solution)/shard_map/psum | solution.py:203
  337.1 2.8 copy-start.10
  337.1 2.8 copy-start.25
  341.8 6.0 copy-start.17
  341.8 6.0 copy-start.42
  341.8 6.0 copy-start.44
  353.8 4.6 copy-start.4
  353.8 12.3 %collective-permute-start.2 = (bf16[512,1,384]{0,2,1:T(8,128)(2,1)}, bf16[512,1,384]{0,2,1:T(8,128)(2,1)}, u32[]{:S(2)}, u32[]{:S(2)}) collective-permute-start(bf16[512,1,384]{0,2,1:T(8,128)(2,1)} %fusion.170), channel_id=1, source_target_pairs={{0,2},{2,0},{1,3},{3,1},{4,6},{6,4},{5,7},{7,5},{8,10},{10,8},{9,1... | collective-permute-start | bytes 1179656 | tf_op jit(solution)/shard_map/while/body/eval_jaxpr/ppermute | solution.py:19
  359.4 15.2 %collective-permute-start.3 = (bf16[512,1,384]{0,2,1:T(8,128)(2,1)}, bf16[512,1,384]{0,2,1:T(8,128)(2,1)}, u32[]{:S(2)}, u32[]{:S(2)}) collective-permute-start(bf16[512,1,384]{0,2,1:T(8,128)(2,1)} %fusion.172), channel_id=1, source_target_pairs={{0,2},{2,0},{1,3},{3,1},{4,6},{6,4},{5,7},{7,5},{8,10},{10,8},{9,1... | collective-permute-start | bytes 1179656 | tf_op jit(solution)/shard_map/while/body/eval_jaxpr/ppermute | solution.py:19
  359.6 23.4 %collective-permute-start = (bf16[512,1,384]{0,2,1:T(8,128)(2,1)}, bf16[512,1,384]{0,2,1:T(8,128)(2,1)}, u32[]{:S(2)}, u32[]{:S(2)}) collective-permute-start(bf16[512,1,384]{0,2,1:T(8,128)(2,1)} %copy.87), channel_id=1, source_target_pairs={{0,2},{2,0},{1,3},{3,1},{4,6},{6,4},{5,7},{7,5},{8,10},{10,8},{9,1... | collective-permute-start | bytes 1179656 | tf_op jit(solution)/shard_map/while/body/eval_jaxpr/ppermute | solution.py:19
  361.4 29.3 %collective-permute-start.1 = (bf16[512,1,384]{0,2,1:T(8,128)(2,1)}, bf16[512,1,384]{0,2,1:T(8,128)(2,1)}, u32[]{:S(2)}, u32[]{:S(2)}) collective-permute-start(bf16[512,1,384]{0,2,1:T(8,128)(2,1)} %copy.88), channel_id=1, source_target_pairs={{0,2},{2,0},{1,3},{3,1},{4,6},{6,4},{5,7},{7,5},{8,10},{10,8},{9,1... | collective-permute-start | bytes 1179656 | tf_op jit(solution)/shard_map/while/body/eval_jaxpr/ppermute | solution.py:19
  364.6 26.1 %copy-start.18 = (bf16[512,1,6,64]{0,3,2,1:T(8,128)(2,1)S(1)}, bf16[512,1,6,64]{0,3,2,1:T(8,128)(2,1)}, u32[]{:S(2)}) copy-start(bf16[512,1,6,64]{0,3,2,1:T(8,128)(2,1)} %copy-done.17) | copy-start | bytes 1179652 | tf_op jit(solution)/shard_map/while
  364.6 26.1 %copy-start.43 = (f32[1,6,512]{2,1,0:T(8,128)S(1)}, f32[1,6,512]{2,1,0:T(8,128)}, u32[]{:S(2)}) copy-start(f32[1,6,512]{2,1,0:T(8,128)} %copy-done.42) | copy-start | bytes 36868 | tf_op jit(solution)/shard_map/while
  364.6 26.1 %copy-start.45 = (f32[1,6,512]{2,1,0:T(8,128)S(1)}, f32[1,6,512]{2,1,0:T(8,128)}, u32[]{:S(2)}) copy-start(f32[1,6,512]{2,1,0:T(8,128)} %copy-done.44) | copy-start | bytes 36868 | tf_op jit(solution)/shard_map/while
  390.8 6.0 copy-start.17
  390.8 6.0 copy-start.42
  390.8 6.0 copy-start.44
  402.8 4.6 copy-start.4
  402.8 12.3 %collective-permute-start.2 = (bf16[512,1,384]{0,2,1:T(8,128)(2,1)}, bf16[512,1,384]{0,2,1:T(8,128)(2,1)}, u32[]{:S(2)}, u32[]{:S(2)}) collective-permute-start(bf16[512,1,384]{0,2,1:T(8,128)(2,1)} %fusion.170), channel_id=1, source_target_pairs={{0,2},{2,0},{1,3},{3,1},{4,6},{6,4},{5,7},{7,5},{8,10},{10,8},{9,1... | collective-permute-start | bytes 1179656 | tf_op jit(solution)/shard_map/while/body/eval_jaxpr/ppermute | solution.py:19
  408.3 15.2 %collective-permute-start.3 = (bf16[512,1,384]{0,2,1:T(8,128)(2,1)}, bf16[512,1,384]{0,2,1:T(8,128)(2,1)}, u32[]{:S(2)}, u32[]{:S(2)}) collective-permute-start(bf16[512,1,384]{0,2,1:T(8,128)(2,1)} %fusion.172), channel_id=1, source_target_pairs={{0,2},{2,0},{1,3},{3,1},{4,6},{6,4},{5,7},{7,5},{8,10},{10,8},{9,1... | collective-permute-start | bytes 1179656 | tf_op jit(solution)/shard_map/while/body/eval_jaxpr/ppermute | solution.py:19
  408.6 23.4 %collective-permute-start = (bf16[512,1,384]{0,2,1:T(8,128)(2,1)}, bf16[512,1,384]{0,2,1:T(8,128)(2,1)}, u32[]{:S(2)}, u32[]{:S(2)}) collective-permute-start(bf16[512,1,384]{0,2,1:T(8,128)(2,1)} %copy.87), channel_id=1, source_target_pairs={{0,2},{2,0},{1,3},{3,1},{4,6},{6,4},{5,7},{7,5},{8,10},{10,8},{9,1... | collective-permute-start | bytes 1179656 | tf_op jit(solution)/shard_map/while/body/eval_jaxpr/ppermute | solution.py:19
  410.4 28.5 %collective-permute-start.1 = (bf16[512,1,384]{0,2,1:T(8,128)(2,1)}, bf16[512,1,384]{0,2,1:T(8,128)(2,1)}, u32[]{:S(2)}, u32[]{:S(2)}) collective-permute-start(bf16[512,1,384]{0,2,1:T(8,128)(2,1)} %copy.88), channel_id=1, source_target_pairs={{0,2},{2,0},{1,3},{3,1},{4,6},{6,4},{5,7},{7,5},{8,10},{10,8},{9,1... | collective-permute-start | bytes 1179656 | tf_op jit(solution)/shard_map/while/body/eval_jaxpr/ppermute | solution.py:19
  413.8 25.0 %copy-start.18 = (bf16[512,1,6,64]{0,3,2,1:T(8,128)(2,1)S(1)}, bf16[512,1,6,64]{0,3,2,1:T(8,128)(2,1)}, u32[]{:S(2)}) copy-start(bf16[512,1,6,64]{0,3,2,1:T(8,128)(2,1)} %copy-done.17) | copy-start | bytes 1179652 | tf_op jit(solution)/shard_map/while
  413.9 25.0 %copy-start.43 = (f32[1,6,512]{2,1,0:T(8,128)S(1)}, f32[1,6,512]{2,1,0:T(8,128)}, u32[]{:S(2)}) copy-start(f32[1,6,512]{2,1,0:T(8,128)} %copy-done.42) | copy-start | bytes 36868 | tf_op jit(solution)/shard_map/while
  413.9 25.0 %copy-start.45 = (f32[1,6,512]{2,1,0:T(8,128)S(1)}, f32[1,6,512]{2,1,0:T(8,128)}, u32[]{:S(2)}) copy-start(f32[1,6,512]{2,1,0:T(8,128)} %copy-done.44) | copy-start | bytes 36868 | tf_op jit(solution)/shard_map/while
  438.9 2.3 copy-start.14
  444.7 2.6 copy-start.26
  444.7 67.2 %reduce-scatter.13.cloned.1.call-start = ((), (), s32[]{:S(2)}) async-start(), calls=%async_computation.12 | async-start | bytes 442368 | tf_op jit(solution)/shard_map/reduce_scatter | solution.py:277
  447.2 136.9 %reduce-scatter.19.cloned.1.call-start = ((), (), s32[]{:S(2)}) async-start(), calls=%async_computation.15 | async-start | bytes 2654208
  456.7 193.4 %reduce-scatter.15.cloned.1.call-start = ((), (), s32[]{:S(2)}) async-start(), calls=%async_computation.13 | async-start | bytes 663552 | tf_op jit(solution)/shard_map/reduce_scatter | solution.py:280
  459.6 2.9 copy-start.41
  459.6 2.9 copy-start.49
  459.7 256.2 %reduce-scatter.9.cloned.1.call-start = ((), (), s32[]{:S(2)}) async-start(), calls=%async_computation.10 | async-start | bytes 663552 | tf_op jit(solution)/shard_map/reduce_scatter | solution.py:271
  462.4 1.9 copy-start.34
  462.4 1.9 copy-start.38
  462.4 1.9 copy-start.51
  462.5 318.9 %reduce-scatter.11.cloned.1.call-start = ((), (), s32[]{:S(2)}) async-start(), calls=%async_computation.11 | async-start | bytes 663552 | tf_op jit(solution)/shard_map/reduce_scatter | solution.py:274
  464.2 389.3 %reduce-scatter.17.cloned.1.call-start = ((), (), s32[]{:S(2)}) async-start(), calls=%async_computation.14 | async-start | bytes 2654208 | tf_op jit(solution)/shard_map/reduce_scatter | solution.py:283
  469.2 421.0 %all-reduce.24.cloned.1.call-start = ((), (), s32[]{:S(2)}) async-start(), calls=%async_computation.17 | async-start | bytes 1818624 | tf_op jit(solution)/shard_map/psum | solution.py:308
  471.1 4.7 copy-start.46
  473.7 380.0 %copy-start.9 = (bf16[512,768]{1,0:T(8,128)(2,1)S(1)}, bf16[512,768]{1,0:T(8,128)(2,1)}, u32[]{:S(2)}) copy-start(bf16[512,768]{1,0:T(8,128)(2,1)} %all-reduce.18.cloned.1.call-done) | copy-start | bytes 2359300
  890.1 6.7 copy-start.27
  (24 other events, 28.7 us)
Sparse Core Ops, SparseCore 0:
  207.4 15.2 all-reduce.17
  319.6 17.4 all-reduce.19
  444.8 21.5 all-reduce.21
  853.7 36.3 all-reduce.23
Sparse Core Ops, SparseCore 1:
  210.0 48.0 all-gather.3
  260.1 50.2 all-gather.5
  448.4 63.4 reduce-scatter.12
  515.4 68.7 reduce-scatter.18
  588.1 62.0 reduce-scatter.14
  654.0 61.8 reduce-scatter.8
  719.6 61.8 reduce-scatter.10
  784.8 68.8 reduce-scatter.16
where the time goes:
time: 912 us; the launch traced here: 905 us
  waiting for transfers between devices  521 us (57%)
  blocking collectives  199 us (22%)
  matrix products  73.1 us (8%)
  local copies, waits for them, and re-layouts  43.8 us (5%)
  other arithmetic  41.2 us (5%)
  between operations  17.6 us (2%)
  starting transfers between devices  9.23 us (1%)
    reduce_scatter x1, waiting for transfers between devices, local(): lax.psum_scatter(grad_up.astype(jnp.bfloat16), 'fsdp', scatter_dimension=...  72.2 us
    reduce_scatter x1, waiting for transfers between devices, local(): lax.psum_scatter(grad_query.astype(jnp.bfloat16), 'fsdp', scatter_dimensi...  65.7 us
    reduce_scatter x1, waiting for transfers between devices, local(): lax.psum_scatter(grad_key.astype(jnp.bfloat16), 'fsdp', scatter_dimension...  65.6 us
    reduce_scatter x1, waiting for transfers between devices, local(): lax.psum_scatter(grad_outproj.astype(jnp.bfloat16), 'fsdp', scatter_dimen...  64 us
    unnamed x13, waiting for transfers between devices  62 us
    all_gather x1, waiting for transfers between devices, local(): lax.all_gather(w_down, 'fsdp', axis=0, tiled=True)  47.5 us
    unnamed x2, blocking collectives  45.2 us
    ppermute x8, waiting for transfers between devices, passed_along(): return lax.ppermute(value, axis, pairs)  43.2 us
  transfers between devices with their start and end apart: 20, of which 19 were waited for; matrix products, arithmetic and copies ran while one was open for 8% of the time, Pallas kernels for 0%

commit v1 on v0

--- a/solution.py
+++ b/solution.py
@@ -1,10 +1,14 @@
 import jax
 import jax.numpy as jnp
 from jax import lax
+from jax.experimental import pallas as pl
+from jax.experimental.pallas import tpu as pltpu
 from jax.sharding import PartitionSpec as P
 
 HEADS = 12
 HEAD_DIM = 64
+low = jnp.bfloat16
+wide = jnp.float32
 
 
 eps_norm = 1e-05
@@ -120,7 +124,7 @@
     return grad_block(query, d_mixed, delta, log_total, q_places, k_shard, v_shard, p_shard, scale)
 
 
-def local(
+def local_ring(
     hidden_in,
     first_values,
     span_table,
@@ -328,40 +332,648 @@
     )
 
 
+def swap_fsdp(value, flip):
+    count = lax.axis_size("fsdp")
+    return lax.ppermute(value, "fsdp", [(i, i ^ flip) for i in range(count)])
+
+
+def swap_tp(value):
+    return lax.ppermute(value, "tp", [(0, 1), (1, 0)])
+
+
+def swap_ctx(value):
+    return lax.ppermute(value, "ctx", [(0, 1), (1, 0)])
+
+
+def gather_blocks(shard):
+    count = lax.axis_size("fsdp")
+    blocks = {0: shard}
+    for k in range(1, count // 2):
+        blocks[2 * k] = swap_fsdp(shard, 2 * k)
+    for k in range(count // 2):
+        blocks[2 * k + 1] = swap_fsdp(blocks[2 * k], 1)
+    return [blocks[m] for m in range(count)]
+
+
+def matmul(left, right, left_dim, right_dim):
+    return lax.dot_general(left, right, (((left_dim,), (right_dim,)), ((), ())), preferred_element_type=wide)
+
+
+def shapes(*pairs):
+    return tuple(jax.ShapeDtypeStruct(shape, dtype) for shape, dtype in pairs)
+
+
+def parity_heads(block, odd):
+    count = block.shape[1] // HEAD_DIM
+    return jnp.concatenate([block[:, j * HEAD_DIM : (j + 1) * HEAD_DIM] for j in range(odd, count, 2)], axis=1)
+
+
+def woven_heads(even, odd):
+    count = even.shape[1] // HEAD_DIM
+    parts = []
+    for i in range(count):
+        parts += [even[:, i * HEAD_DIM : (i + 1) * HEAD_DIM], odd[:, i * HEAD_DIM : (i + 1) * HEAD_DIM]]
+    return jnp.concatenate(parts, axis=1)
+
+
+def pack_attn_kernel(wq, wk, wv, g0, g1, g2, g3, out):
+    rank = lax.axis_index("ctx")
+    shard = wq.shape[0]
+
+    def pick(ref):
+        block = ref[...].astype(wide)
+        return jnp.where(rank == 0, parity_heads(block, 0), parity_heads(block, 1))
+
+    gains = jnp.concatenate([g[...].astype(wide) for g in (g0, g1, g2, g3)] + [jnp.zeros((4, shard), wide)], axis=0)
+    gains = jnp.concatenate([gains, jnp.zeros((8, 128 - shard), wide)], axis=1).T[:shard]
+    pad = jnp.zeros((shard, HEAD_DIM - 8), wide)
+    out[...] = jnp.concatenate([pick(wq), pick(wk), wv[...].astype(wide), gains, pad], axis=1).astype(low)
+
+
+def pack_late_kernel(wo, wu, wd, out_up, out_down):
+    rank = lax.axis_index("ctx")
+    cols, units = wo.shape[1], wu.shape[1] // 2
+    block = wo[...].astype(wide)
+    even, odd = parity_heads(block, 0), parity_heads(block, 1)
+    own = jnp.where(rank == 0, even, odd)
+    other = jnp.where(rank == 0, odd, even)
+    out_up[:, :cols] = jnp.concatenate([own, other], axis=1).astype(low)
+    out_up[:, cols:] = jnp.where(rank == 0, wu[:, :units], wu[:, units:])
+    out_down[...] = jnp.where(rank == 0, wd[:, :units], wd[:, units:])
+
+
+def place_blocks(blocks, store):
+    me = lax.axis_index("fsdp")
+    for m, block in enumerate(blocks):
+        rows = block.shape[0]
+        store(pl.ds(pl.multiple_of((me ^ m) * rows, 32), rows), block)
+
+
+def row_norm(values):
+    mean = jnp.mean(values, axis=-1, keepdims=True)
+    centred = values - mean
+    inverse = lax.rsqrt(jnp.mean(centred * centred, axis=-1, keepdims=True) + eps_norm)
+    return centred * inverse, inverse
+
+
+def quarter_of_place(table):
+    rank, side = lax.axis_index("ctx"), lax.axis_index("tp")
+    held = [table[rank ^ (q // 2), side ^ (q % 2)] for q in range(4)]
+    return [sum(jnp.where(held[q] == p, q, 0) for q in range(4)) for p in range(4)]
+
+
+def attn_kernel(table, hid, across, across2, b0, b1, b2, b3, b4, b5, b6, b7, first, first_far,
+                x_out, h_out, w_out, gains_out, qkv_out, mix_out, low_out, lse_out, keys_scr):
+    rank, side = lax.axis_index("ctx"), lax.axis_index("tp")
+    span = across.shape[0]
+    cols = first.shape[0]
+    heads = cols // HEAD_DIM
+
+    def store(where, block):
+        w_out[where, :] = block[...]
+
+    place_blocks((b0, b1, b2, b3, b4, b5, b6, b7), store)
+    gains = w_out[:, 512:640].astype(wide).T[64:72]
+    gains_out[...] = gains
+    gain, shift = gains[0:1], gains[1:2]
+    x_out[0] = hid[pl.ds(pl.multiple_of(side * span, span), span), :]
+    x_out[1] = hid[pl.ds(pl.multiple_of((1 - side) * span, span), span), :]
+    x_out[2] = across[...]
+    x_out[3] = across2[...]
+    step = 64
+
+    def norm_chunk(i, carry):
+        for q in range(4):
+            where = pl.ds(pl.multiple_of(i * step, step), step)
+            unit, _ = row_norm(x_out[q, where, :].astype(wide))
+            h_out[q, where, :] = (unit * gain + shift).astype(low)
+        return carry
+
+    lax.fori_loop(0, span // step, norm_chunk, 0)
+    w_turned = w_out[:, : 3 * cols].T
+    for q in range(4):
+        qkv_out[q] = matmul(w_turned, h_out[q], 1, 1).astype(low)
+
+    @pl.when(rank == 1)
+    def _():
+        for q in range(4):
+            ref = first if q < 2 else first_far
+            half = side if q % 2 == 0 else 1 - side
+            qkv_out[q, 2 * cols :, :] = jnp.where(half == 0, ref[:, :span], ref[:, span:])
+
+    order = quarter_of_place(table)
+    below = lax.broadcasted_iota(jnp.int32, (span, span), 0) <= lax.broadcasted_iota(jnp.int32, (span, span), 1)
+    lse_out[...] = jnp.zeros_like(lse_out)
+
+    for h in range(heads):
+        base = h * HEAD_DIM
+        for p in range(4):
+            keys_scr[p] = qkv_out[order[p], cols + base : cols + base + HEAD_DIM, :].T
+        for qp in range(4):
+            query = qkv_out[order[qp], base : base + HEAD_DIM, :] * low(HEAD_DIM ** -0.5)
+            scores = [matmul(keys_scr[kp], query, 1, 0) for kp in range(qp + 1)]
+            scores[qp] = jnp.where(below, scores[qp], big_negative)
+            top = jnp.max(scores[0], axis=0, keepdims=True)
+            for s in scores[1:]:
+                top = jnp.maximum(top, jnp.max(s, axis=0, keepdims=True))
+            total = jnp.zeros((1, span), wide)
+            mixed = jnp.zeros((HEAD_DIM, span), wide)
+            for kp in range(qp + 1):
+                weights = jnp.exp(scores[kp] - top)
+                total = total + jnp.sum(weights, axis=0, keepdims=True)
+                value = qkv_out[order[kp], 2 * cols + base : 2 * cols + base + HEAD_DIM, :]
+                mixed = mixed + matmul(value, weights.astype(low), 1, 0)
+            mixed = mixed / total
+            mix_out[order[qp], base : base + HEAD_DIM, :] = mixed
+            low_out[order[qp], base : base + HEAD_DIM, :] = mixed.astype(low)
+            lse_out[order[qp], h : h + 1, :] = top + jnp.log(total)
+
+
+def place_up_kernel(b0, b1, b2, b3, b4, b5, b6, b7, wo_out, wu_out):
+    cols = wo_out.shape[1]
+
+    def store(where, block):
+        wo_out[where, :] = block[:, :cols]
+        wu_out[where, :] = block[:, cols:]
+
+    place_blocks((b0, b1, b2, b3, b4, b5, b6, b7), store)
+
+
+def place_down_kernel(b0, b1, b2, b3, b4, b5, b6, b7, cot, across, across2, wd_out, cot_out):
+    side = lax.axis_index("tp")
+    span = across.shape[0]
+
+    def store(where, block):
+        wd_out[where, :] = block[...]
+
+    place_blocks((b0, b1, b2, b3, b4, b5, b6, b7), store)
+    cot_out[0] = cot[pl.ds(pl.multiple_of(side * span, span), span), :]
+    cot_out[1] = cot[pl.ds(pl.multiple_of((1 - side) * span, span), span), :]
+    cot_out[2] = across[...]
+    cot_out[3] = across2[...]
+
+
+def mlp_kernel(x, mix0, mix1, mix2, mix3, wo_own, wo_side, wu, wd, gains, cot,
+               resid_out, act_out, h_out, dup_out, keep_out, send_out):
+    q = pl.program_id(0)
+    mixed = jnp.concatenate([mix0[0], mix1[0], mix2[0], mix3[0]], axis=0).T
+    half = wo_own.shape[1]
+    proj = matmul(mixed[:, :half], wo_own[...], 1, 1) + matmul(mixed[:, half:], wo_side[...], 1, 1)
+    resid = x[0].astype(wide) + proj
+
+    @pl.when(q < 2)
+    def _():
+        resid_out[0] = resid
+
+    unit, _ = row_norm(resid)
+    h_two = (unit * gains[2:3, :] + gains[3:4, :]).astype(low)
+    h_out[0] = h_two
+    upper = matmul(h_two, wu[...], 1, 0)
+    square = upper * upper
+    tanh = jnp.tanh(gelu_coef * upper * (1.0 + cube_coef * square))
+    act_out[0] = (0.5 * upper * (1.0 + tanh)).astype(low)
+    slope = 0.5 * (1.0 + tanh) + 0.5 * upper * (1.0 - tanh * tanh) * gelu_coef * (1.0 + 3.0 * cube_coef * square)
+    d_act = matmul(cot[0], wd[...], 1, 0)
+    d_upper = (d_act * slope).astype(low)
+    dup_out[0] = d_upper
+    part = matmul(d_upper, wu[...], 1, 1).astype(low)
+
+    @pl.when(q % 2 == 0)
+    def _():
+        keep_out[0] = part
+
+    @pl.when(q % 2 == 1)
+    def _():
+        send_out[0] = part
+
+
+def scatter_slots(value, keep, send, lanes):
+    me = lax.axis_index("fsdp")
+    rows = keep.shape[1]
+    for k in range(keep.shape[0]):
+        base = (me >> 1) ^ k
+        keep[k, :, lanes] = value[pl.ds(pl.multiple_of((base * 2 + (me & 1)) * rows, 32), rows), :].astype(low)
+        send[k, :, lanes] = value[pl.ds(pl.multiple_of((base * 2 + ((me & 1) ^ 1)) * rows, 32), rows), :].astype(low)
+
+
+def mlp_grad_kernel(cot, act, h_two, d_upper, wd, keep_out, send_out, out_keep, out_send, grad):
+    units = act.shape[2]
+    width = cot.shape[2]
+    for left, right, first in ((h_two, d_upper, 0), (cot, act, units)):
+        total = matmul(left[0], right[0], 0, 0)
+        for q in range(1, 4):
+            total = total + matmul(left[q], right[q], 0, 0)
+        grad[...] = total
+        scatter_slots(grad, keep_out, send_out, slice(first, first + units))
+    for q in range(4):
+        part = matmul(act[q], wd[...], 1, 1).astype(low)
+        (out_keep if q % 2 == 0 else out_send)[q // 2] = part
+
+
+def norm_back(d_norm, unit, inverse, gain):
+    scaled = d_norm * gain
+    inner = scaled - jnp.mean(scaled, axis=-1, keepdims=True) - unit * jnp.mean(scaled * unit, axis=-1, keepdims=True)
+    return inverse * inner
+
+
+def branch_kernel(keep, got, far, resid, cot, gains, d_resid_out, low_out, sums_out):
+    d_two = keep[0].astype(wide) + got[0].astype(wide) + far[...].astype(wide)
+    unit, inverse = row_norm(resid[0])
+    sums_out[...] = jnp.zeros_like(sums_out)
+    sums_out[0:1, :] = jnp.sum(d_two * unit, axis=0, keepdims=True)
+    sums_out[1:2, :] = jnp.sum(d_two, axis=0, keepdims=True)
+    d_resid = cot[0].astype(wide) + norm_back(d_two, unit, inverse, gains[2:3, :])
+    d_resid_out[...] = d_resid
+    low_out[...] = d_resid.astype(low)
+
+
+def attn_back_kernel(table, br0, br1, br2, br3, wo, qkv, mix, lse, low_mix, d_out, d_first, keep_out, send_out,
+                     dm_scr, keys_scr, values_scr, dq_scr, grad):
+    rank = lax.axis_index("ctx")
+    span = qkv.shape[2]
+    cols = mix.shape[1]
+    heads = cols // HEAD_DIM
+    wo_turned = wo[:, :cols].T
+    branches = (br0, br1, br2, br3)
+    turned = jnp.zeros((cols, wo.shape[0]), wide)
+    for q in range(4):
+        dm_scr[q] = matmul(wo_turned, branches[q][...], 1, 1).astype(low)
+        turned = turned + matmul(low_mix[q], branches[q][...], 1, 0)
+    grad[...] = turned.T
+    scatter_slots(grad, keep_out, send_out, slice(0, cols))
+    order = quarter_of_place(table)
+    below = lax.broadcasted_iota(jnp.int32, (span, span), 0) <= lax.broadcasted_iota(jnp.int32, (span, span), 1)
+    root = low(HEAD_DIM ** -0.5)
+    for h in range(heads):
+        base = h * HEAD_DIM
+        mine = slice(base, base + HEAD_DIM)
+        delta = []
+        for p in range(4):
+            keys_scr[p] = qkv[order[p], cols + base : cols + base + HEAD_DIM, :].T
+            values_scr[p] = qkv[order[p], 2 * cols + base : 2 * cols + base + HEAD_DIM, :].T
+            delta.append(jnp.sum(dm_scr[order[p], mine, :].astype(wide) * mix[order[p], mine, :], axis=0, keepdims=True))
+        for kp in range(4):
+            d_key = jnp.zeros((HEAD_DIM, span), wide)
+            d_value = jnp.zeros((HEAD_DIM, span), wide)
+            key = qkv[order[kp], cols + base : cols + base + HEAD_DIM, :]
+            for qp in range(kp, 4):
+                query = qkv[order[qp], mine, :] * root
+                d_mixed = dm_scr[order[qp], mine, :]
+                weights = jnp.exp(matmul(keys_scr[kp], query, 1, 0) - lse[order[qp], h : h + 1, :])
+                if kp == qp:
+                    weights = jnp.where(below, weights, 0.0)
+                d_weights = matmul(values_scr[kp], d_mixed, 1, 0)
+                d_scores = (weights * (d_weights - delta[qp])).astype(low)
+                d_value = d_value + matmul(d_mixed, weights.astype(low), 1, 1)
+                d_key = d_key + matmul(query, d_scores, 1, 1)
+                d_query = matmul(key, d_scores, 1, 0)
+                dq_scr[qp] = d_query if kp == 0 else dq_scr[qp] + d_query
+            d_out[order[kp], cols + base : cols + base + HEAD_DIM, :] = d_key.astype(low)
+            d_first[order[kp], mine, :] = d_value
+            d_out[order[kp], 2 * cols + base : 2 * cols + base + HEAD_DIM, :] = jnp.where(rank == 0, d_value, 0.0).astype(low)
+        for qp in range(4):
+            d_out[order[qp], mine, :] = (dq_scr[qp] * HEAD_DIM ** -0.5).astype(low)
+
+
+def d_one_kernel(d_qkv, w, x, keep_out, send_out, sums_out):
+    q = pl.program_id(0)
+    wide_cols = d_qkv.shape[1]
+    part = matmul(d_qkv[0].T, w[:, :wide_cols], 1, 1)
+    unit, _ = row_norm(x[0].astype(wide))
+
+    @pl.when(q == 0)
+    def _():
+        sums_out[...] = jnp.zeros_like(sums_out)
+
+    sums_out[0:1, :] += jnp.sum(part * unit, axis=0, keepdims=True)
+    sums_out[1:2, :] += jnp.sum(part, axis=0, keepdims=True)
+
+    @pl.when(q % 2 == 0)
+    def _():
+        keep_out[0] = part.astype(low)
+
+    @pl.when(q % 2 == 1)
+    def _():
+        send_out[0] = part.astype(low)
+
+
+def attn_grad_kernel(d_qkv, h_one, sums_one, sums_two, side_one, side_two, keep_out, send_out, grad):
+    cols = d_qkv.shape[1]
+    width = h_one.shape[2]
+    turned = matmul(d_qkv[0], h_one[0], 1, 0)
+    for q in range(1, 4):
+        turned = turned + matmul(d_qkv[q], h_one[q], 1, 0)
+    grad[:, :cols] = turned.T
+    one = sums_one[...] + side_one[...].astype(wide)
+    two = sums_two[...] + side_two[...].astype(wide)
+    sums = jnp.concatenate([one[0:2], two[0:2], jnp.zeros((124, width), wide)], axis=0).T
+    grad[:, cols:] = sums[:, :HEAD_DIM]
+    scatter_slots(grad, keep_out, send_out, slice(0, cols + HEAD_DIM))
+
+
+def pair_kernel(keep, got, *outs):
+    for k, out in enumerate(outs):
+        out[...] = (keep[k].astype(wide) + got[k].astype(wide)).astype(low)
+
+
+def total_kernel(a, b, c, d, out):
+    out[...] = (a[...].astype(wide) + b[...].astype(wide) + c[...].astype(wide) + d[...].astype(wide)).astype(low)
+
+
+def scatter_over(keep, send):
+    shape = keep.shape[1:]
+    parts = pl.pallas_call(pair_kernel, out_shape=shapes(*[(shape, low)] * keep.shape[0]))(keep, swap_fsdp(send, 1))
+    found = [parts[0]] + [swap_fsdp(parts[k], 2 * k) for k in range(1, keep.shape[0])]
+    return pl.pallas_call(total_kernel, out_shape=jax.ShapeDtypeStruct(shape, low))(*found)
+
+
+def finish_mlp_kernel(own, far, up_out, down_out):
+    rank = lax.axis_index("ctx")
+    units = own.shape[1] // 2
+    a, b = own[...].astype(wide), far[...].astype(wide)
+    lower, upper = jnp.where(rank == 0, a, b), jnp.where(rank == 0, b, a)
+    up_out[:, :units] = lower[:, :units]
+    up_out[:, units:] = upper[:, :units]
+    down_out[:, :units] = lower[:, units:]
+    down_out[:, units:] = upper[:, units:]
+
+
+def finish_attn_kernel(own, far, own_proj, far_proj, q_out, k_out, v_out, o_out, g0, g1, g2, g3):
+    rank = lax.axis_index("ctx")
+    cols = v_out.shape[1]
+    rows = own.shape[0]
+    a, b = own[...].astype(wide), far[...].astype(wide)
+    even, odd = jnp.where(rank == 0, a, b), jnp.where(rank == 0, b, a)
+    q_out[...] = woven_heads(even[:, :cols], odd[:, :cols])
+    k_out[...] = woven_heads(even[:, cols : 2 * cols], odd[:, cols : 2 * cols])
+    v_out[...] = even[:, 2 * cols : 3 * cols]
+    c, d = own_proj[...].astype(wide), far_proj[...].astype(wide)
+    o_out[...] = woven_heads(jnp.where(rank == 0, c, d), jnp.where(rank == 0, d, c))
+    both = a[:, 512:640] + b[:, 512:640]
+    gains = jnp.concatenate([both, jnp.zeros((128 - rows, 128), wide)], axis=0).T
+    for i, out in enumerate((g0, g1, g2, g3)):
+        out[...] = gains[64 + i : 65 + i, :rows]
+
+
+def store_rows(out, first, value):
+    pieces = value.shape[1] // 128
+    for j in range(pieces):
+        out[pl.ds(first * pieces + j, value.shape[0], stride=pieces), :] = value[:, j * 128 : (j + 1) * 128]
+
+
+def out_kernel(resid, own, beside, out):
+    side = lax.axis_index("tp")
+    span = own.shape[0]
+    store_rows(out, side * span, resid[0] + own[...].astype(wide))
+    store_rows(out, (1 - side) * span, resid[1] + beside[...].astype(wide))
+
+
+def input_grad_kernel(x, own, beside, d_own, d_beside, gains, out):
+    side = lax.axis_index("tp")
+    span = own.shape[0]
+    for k, (d_one, d_resid) in enumerate(((own, d_own), (beside, d_beside))):
+        unit, inverse = row_norm(x[k].astype(wide))
+        value = d_resid[...] + norm_back(d_one[...].astype(wide), unit, inverse, gains[0:1, :])
+        store_rows(out, (side if k == 0 else 1 - side) * span, value)
+
+
+def first_grad_kernel(d_first, far, out):
+    rank, side = lax.axis_index("ctx"), lax.axis_index("tp")
+    span = d_first.shape[2]
+
+    @pl.when(rank == 0)
+    def _():
+        out[...] = far[...].astype(wide)
+
+    @pl.when(rank == 1)
+    def _():
+        out[:, :span] = jnp.where(side == 0, d_first[0], d_first[1])
+        out[:, span:] = jnp.where(side == 0, d_first[1], d_first[0])
+
+
+def first_send_kernel(d_first, out):
+    side = lax.axis_index("tp")
+    span = d_first.shape[2]
+    out[:, :span] = jnp.where(side == 0, d_first[2], d_first[3]).astype(low)
+    out[:, span:] = jnp.where(side == 0, d_first[3], d_first[2]).astype(low)
+
+
+def sum_kernel(keep, got, out):
+    out[...] = (keep[1].astype(wide) + got[1].astype(wide)).astype(low)
+
+
+def close_kernel(keep, got, far, out):
+    out[...] = (keep[0].astype(wide) + got[0].astype(wide) + far[...].astype(wide)).astype(low)
+
+
+def local_split(
+    hidden_in,
+    first_values,
+    span_table,
+    w_query,
+    w_key,
+    w_value,
+    w_out,
+    w_up,
+    w_down,
+    gain_attn,
+    shift_attn,
+    gain_mlp,
+    shift_mlp,
+    cotangent,
+):
+    rows, seqs, width = hidden_in.shape
+    span = rows // 2
+    shard = w_query.shape[0]
+    cols = w_query.shape[1] // 2
+    units = w_up.shape[1] // 2
+    pairs = lax.axis_size("fsdp") // 2
+    smem = pl.BlockSpec(memory_space=pltpu.SMEM)
+    vmem = pl.BlockSpec(memory_space=pltpu.VMEM)
+    side = lax.axis_index("tp")
+
+    def quarter_spec(c, turn=lambda q: q, s=span):
+        return pl.BlockSpec((1, s, c), lambda q: (turn(q), 0, 0))
+
+    def whole_spec(*shape):
+        return pl.BlockSpec(shape, lambda q: (0,) * len(shape))
+
+    def own_quarter(block):
+        return lax.dynamic_slice_in_dim(block, side * span, span)
+
+    hidden = hidden_in.reshape(rows, width)
+    cot = cotangent.reshape(rows, width)
+    first = first_values.reshape(rows, cols).T
+
+    across = swap_ctx(own_quarter(hidden))
+    gains_in = [g.reshape(1, shard) for g in (gain_attn, shift_attn, gain_mlp, shift_mlp)]
+    attn_shard = pl.pallas_call(pack_attn_kernel, out_shape=jax.ShapeDtypeStruct((shard, 640), low))(
+        w_query, w_key, w_value, *gains_in
+    )
+    attn_blocks = gather_blocks(attn_shard)
+    across2 = swap_tp(across)
+    first_far = lax.ppermute(first, "ctx", [(0, 1)])
+    up_shard, down_shard = pl.pallas_call(
+        pack_late_kernel, out_shape=shapes(((shard, 2 * cols + units), low), ((shard, units), low))
+    )(w_out, w_up, w_down)
+    up_blocks = gather_blocks(up_shard)
+    cot_across = swap_ctx(own_quarter(cot))
+    cot_across2 = swap_tp(cot_across)
+    down_blocks = gather_blocks(down_shard)
+
+    x4, h_one, w_qkv, gains, qkv, mix, low_mix, lse = pl.pallas_call(
+        attn_kernel,
+        in_specs=[smem] + [vmem] * 13,
+        out_shape=shapes(
+            ((4, span, width), low), ((4, span, width), low), ((width, 640), low), ((8, width), wide),
+            ((4, 3 * cols, span), low), ((4, cols, span), wide), ((4, cols, span), low), ((4, 8, span), wide),
+        ),
+        scratch_shapes=[pltpu.VMEM((4, span, HEAD_DIM), low)],
+    )(span_table, hidden, across, across2, *attn_blocks, first, first_far)
+
+    mix_side = swap_tp(low_mix)
+    mix_far = swap_ctx(low_mix)
+    wo_half, wu = pl.pallas_call(place_up_kernel, out_shape=shapes(((width, 2 * cols), low), ((width, units), low)))(
+        *up_blocks
+    )
+    wo_side = swap_tp(wo_half)
+    mix_side_far = swap_tp(mix_far)
+    wd, cot4 = pl.pallas_call(
+        place_down_kernel, out_shape=shapes(((width, units), low), ((4, span, width), low))
+    )(*down_blocks, cot, cot_across, cot_across2)
+
+    half_spec = pl.BlockSpec((1, span, width), lambda q: (q // 2, 0, 0))
+    resid, act, h_two, d_upper, two_keep, two_send = pl.pallas_call(
+        mlp_kernel,
+        grid=(4,),
+        in_specs=[
+            quarter_spec(width),
+            quarter_spec(span, s=cols),
+            quarter_spec(span, lambda q: (q + 2) % 4, cols),
+            quarter_spec(span, lambda q: q + 1 - 2 * (q % 2), cols),
+            quarter_spec(span, lambda q: 3 - q, cols),
+            whole_spec(width, 2 * cols),
+            whole_spec(width, 2 * cols),
+            whole_spec(width, units),
+            whole_spec(width, units),
+            whole_spec(8, width),
+            quarter_spec(width),
+        ],
+        out_specs=[
+            quarter_spec(width, lambda q: jnp.minimum(q, 1)),
+            quarter_spec(units),
+            quarter_spec(width),
+            quarter_spec(units),
+            half_spec,
+            half_spec,
+        ],
+        out_shape=shapes(
+            ((2, span, width), wide), ((4, span, units), low), ((4, span, width), low), ((4, span, units), low),
+            ((2, span, width), low), ((2, span, width), low),
+        ),
+    )(x4, low_mix, mix_far, mix_side, mix_side_far, wo_half, wo_side, wu, wd, gains, cot4)
+
+    two_got = swap_tp(two_send)
+    tile = jax.ShapeDtypeStruct((span, width), low)
+    two_far = swap_ctx(pl.pallas_call(sum_kernel, out_shape=tile)(two_keep, two_got))
+    mlp_keep, mlp_send, out_keep, out_send = pl.pallas_call(
+        mlp_grad_kernel,
+        out_shape=shapes(
+            ((pairs, shard, 2 * units), low), ((pairs, shard, 2 * units), low), ((2, span, width), low), ((2, span, width), low)
+        ),
+        scratch_shapes=[pltpu.VMEM((width, units), wide)],
+    )(cot4, act, h_two, d_upper, wd)
+    d_resid, branch, sums_two = pl.pallas_call(
+        branch_kernel,
+        out_shape=shapes(((span, width), wide), ((span, width), low), ((8, width), wide)),
+    )(two_keep, two_got, two_far, resid, cot4, gains)
+    branch_far = swap_ctx(branch)
+    branch_side = swap_tp(branch)
+    d_resid_beside = swap_tp(d_resid)
+    sums_two_side = swap_tp(sums_two.astype(low))
+    branch_side_far = swap_tp(branch_far)
+    mlp_total = scatter_over(mlp_keep, mlp_send)
+
+    d_qkv, d_first, proj_keep, proj_send = pl.pallas_call(
+        attn_back_kernel,
+        in_specs=[smem] + [vmem] * 9,
+        out_shape=shapes(
+            ((4, 3 * cols, span), low), ((4, cols, span), wide), ((pairs, shard, cols), low), ((pairs, shard, cols), low)
+        ),
+        scratch_shapes=[
+            pltpu.VMEM((4, cols, span), low),
+            pltpu.VMEM((4, span, HEAD_DIM), low),
+            pltpu.VMEM((4, span, HEAD_DIM), low),
+            pltpu.VMEM((4, HEAD_DIM, span), wide),
+            pltpu.VMEM((width, cols), wide),
+        ],
+    )(span_table, branch, branch_side, branch_far, branch_side_far, wo_half, qkv, mix, lse, low_mix)
+
+    one_keep, one_send, sums_one = pl.pallas_call(
+        d_one_kernel,
+        grid=(4,),
+        in_specs=[quarter_spec(span, s=3 * cols), whole_spec(width, 640), quarter_spec(width)],
+        out_specs=[half_spec, half_spec, whole_spec(8, width)],
+        out_shape=shapes(((2, span, width), low), ((2, span, width), low), ((8, width), wide)),
+    )(d_qkv, w_qkv, x4)
+    sums_one_side = swap_tp(sums_one.astype(low))
+    one_got = swap_tp(one_send)
+    one_far = swap_ctx(pl.pallas_call(sum_kernel, out_shape=tile)(one_keep, one_got))
+    last_keep, last_send = pl.pallas_call(
+        attn_grad_kernel,
+        out_shape=shapes(((pairs, shard, 640), low), ((pairs, shard, 640), low)),
+        scratch_shapes=[pltpu.VMEM((width, 640), wide)],
+    )(d_qkv, h_one, sums_one, sums_two, sums_one_side, sums_two_side)
+    proj_total = scatter_over(proj_keep, proj_send)
+    last_total = scatter_over(last_keep, last_send)
+
+    out_got = swap_tp(out_send)
+    out_far = swap_ctx(pl.pallas_call(sum_kernel, out_shape=tile)(out_keep, out_got))
+    out_sum = pl.pallas_call(close_kernel, out_shape=tile)(out_keep, out_got, out_far)
+    flat = jax.ShapeDtypeStruct((rows * width // 128, 128), wide)
+    out_rows = pl.pallas_call(out_kernel, out_shape=flat)(resid, out_sum, swap_tp(out_sum))
+
+    one_sum = pl.pallas_call(close_kernel, out_shape=tile)(one_keep, one_got, one_far)
+    d_input = pl.pallas_call(input_grad_kernel, out_shape=flat)(
+        x4, one_sum, swap_tp(one_sum), d_resid, d_resid_beside, gains
+    )
+
+    first_sent = pl.pallas_call(first_send_kernel, out_shape=jax.ShapeDtypeStruct((cols, rows), low))(d_first)
+    grad_first = pl.pallas_call(first_grad_kernel, out_shape=jax.ShapeDtypeStruct((cols, rows), wide))(
+        d_first, lax.ppermute(first_sent, "ctx", [(1, 0)])
+    )
+
+    grad_up, grad_down = pl.pallas_call(finish_mlp_kernel, out_shape=shapes(*[((shard, 2 * units), wide)] * 2))(
+        mlp_total, swap_ctx(mlp_total)
+    )
+    grads = pl.pallas_call(
+        finish_attn_kernel,
+        out_shape=shapes(
+            ((shard, 2 * cols), wide), ((shard, 2 * cols), wide), ((shard, cols), wide), ((shard, 2 * cols), wide),
+            *[((1, shard), wide)] * 4,
+        ),
+    )(last_total, swap_ctx(last_total), proj_total, swap_ctx(proj_total))
+    return (
+        out_rows.reshape(rows, seqs, width),
+        d_input.reshape(rows, seqs, width),
+        grad_first.T.reshape(rows, seqs, cols),
+        grads[0],
+        grads[1],
+        grads[2],
+        grads[3],
+        grad_up,
+        grad_down,
+        *[g.reshape(shard) for g in grads[4:]],
+    )
+
+
 def solution(mesh):
+    local = local_split if mesh.shape["ctx"] == 2 and mesh.shape["tp"] == 2 else local_ring
+    rows, heads, wide_rows = P("ctx", "fsdp", None), P("ctx", "fsdp", "tp"), P("fsdp", "tp")
     return jax.shard_map(
         local,
         mesh=mesh,
-        in_specs=(
-            P("ctx", "fsdp", None),
-            P("ctx", "fsdp", "tp"),
-            P(),
-            P("fsdp", "tp"),
-            P("fsdp", "tp"),
-            P("fsdp", "tp"),
-            P("fsdp", "tp"),
-            P("fsdp", "tp"),
-            P("fsdp", "tp"),
-            P("fsdp"),
-            P("fsdp"),
-            P("fsdp"),
-            P("fsdp"),
-            P("ctx", "fsdp", None),
-        ),
-        out_specs=(
-            P("ctx", "fsdp", None),
-            P("ctx", "fsdp", None),
-            P("ctx", "fsdp", "tp"),
-            P("fsdp", "tp"),
-            P("fsdp", "tp"),
-            P("fsdp", "tp"),
-            P("fsdp", "tp"),
-            P("fsdp", "tp"),
-            P("fsdp", "tp"),
-            P("fsdp"),
-            P("fsdp"),
-            P("fsdp"),
-            P("fsdp"),
-        ),
+        in_specs=(rows, heads, P()) + (wide_rows,) * 6 + (P("fsdp"),) * 4 + (rows,),
+        out_specs=(rows, rows, heads) + (wide_rows,) * 6 + (P("fsdp"),) * 4,
         check_vma=False,
     )

time: 912 us -> 260 us (0.29)
  waiting for transfers between devices: 521 us -> 72.2 us
  blocking collectives: 199 us -> 0 us
  Pallas kernels: 0 us -> 109 us
  matrix products: 73.1 us -> 0 us
  starting transfers between devices: 9.23 us -> 61.2 us
  other arithmetic: 41.2 us -> 0.01 us
  local copies, waits for them, and re-layouts: 43.8 us -> 15.1 us
  between operations: 17.6 us -> 1.12 us
    reduce_scatter x5 -> x0, waiting for transfers between devices: 281 us -> none  [the longest x1 72.2 us: local(): lax.psum_scatter(grad_up.astype(jnp.bfloat16), 'fsdp', scatter_dimension=...]
    all_gather x6 -> x0, blocking collectives: 144 us -> none  [the longest x1 31.6 us: local(): lax.all_gather(w_query, 'fsdp', axis=0, tiled=True)]
    pallas_call x0 -> x28, Pallas kernels: none -> 109 us  [the longest x1 13.9 us: local_split(): pl.pallas_call(mlp_kernel, grid=(4,), in_specs=[quarter_spec(width), quar...]
    all_gather x2 -> x0, waiting for transfers between devices: 80.8 us -> none  [the longest x1 47.5 us: local(): lax.all_gather(w_down, 'fsdp', axis=0, tiled=True)]
    dot_general x32 -> x0, matrix products: 73.1 us -> none  [the longest x6 17.1 us: contract_rows(): lax.dot_general(left, right, (((0,), (0,)), ((), ())), preferred_element_...]
    unnamed x13 -> x0, waiting for transfers between devices: 62 us -> none
    psum x4 -> x0, waiting for transfers between devices: 53.3 us -> none  [the longest x1 28.2 us: local(): lax.psum(shared[5].astype(jnp.bfloat16), 'ctx').astype(jnp.float32)]
    ppermute x8 -> x60, starting transfers between devices: 8.1 us -> 61.2 us  [the longest x33 43 us: swap_fsdp(): return lax.ppermute(value, 'fsdp', [(i, i ^ flip) for i in range(count)])]
  transfers between devices with their start and end apart: 20 -> 60, of which waited for: 19 -> 23; matrix products, arithmetic and copies ran while one was open for 8% -> 0% of each run, Pallas kernels for 0% -> 33%
where the time goes in v1:
time: 260 us; the launch traced here: 259 us
  Pallas kernels  109 us (42%)
  waiting for transfers between devices  72.2 us (28%)
  starting transfers between devices  61.2 us (24%)
  local copies, waits for them, and re-layouts  15.1 us (6%)
    ppermute x33, waiting for transfers between devices, swap_fsdp(): return lax.ppermute(value, 'fsdp', [(i, i ^ flip) for i in range(count)])  56.6 us
    ppermute x33, starting transfers between devices, swap_fsdp(): return lax.ppermute(value, 'fsdp', [(i, i ^ flip) for i in range(count)])  43 us
    unnamed x118, local copies, waits for them, and re-layouts  13.9 us
    pallas_call x1, Pallas kernels, local_split(): pl.pallas_call(mlp_kernel, grid=(4,), in_specs=[quarter_spec(width), quar...  13.9 us
    ppermute x10, starting transfers between devices, swap_ctx(): return lax.ppermute(value, 'ctx', [(0, 1), (1, 0)])  12.8 us
    pallas_call x1, Pallas kernels, local_split(): pl.pallas_call(attn_back_kernel, in_specs=[smem] + [vmem] * 9, out_shape=...  12.4 us
    pallas_call x1, Pallas kernels, local_split(): pl.pallas_call(attn_kernel, in_specs=[smem] + [vmem] * 13, out_shape=shap...  11.4 us
    ppermute x10, waiting for transfers between devices, swap_ctx(): return lax.ppermute(value, 'ctx', [(0, 1), (1, 0)])  10.5 us
  transfers between devices with their start and end apart: 60, of which 23 were waited for; matrix products, arithmetic and copies ran while one was open for 0% of the time, Pallas kernels for 33%

profile of v1, /device:TPU:0, one launch (start us, length us, event | category | flops | bytes accessed | tf_op | source)
XLA Modules:
  0.0 259.0 jit_solution(15967803812622609019)
XLA Ops:
  1.8 3.1 %collective-permute-start = (bf16[256,768]{1,0:T(8,128)(2,1)S(1)}, bf16[256,768]{1,0:T(8,128)(2,1)S(1)}, u32[]{:S(2)}, u32[]{:S(2)}) collective-permute-start(bf16[256,768]{1,0:T(8,128)(2,1)S(1)} %dynamic-slice_bitcast_fusion.1), channel_id=1, source_target_pairs={{0,2},{2,0},{1,3},{3,1},{4,6},{6,4},{5,7},{7,5},{8,10},{10,8},{9,1... | collective-permute-start | bytes 1179656 | tf_op jit(solution)/shard_map/ppermute | solution.py:345
  4.8 1.8 shard_map.237.b0
  6.6 3.6 %collective-permute-start.7 = (bf16[96,640]{1,0:T(8,128)(2,1)}, bf16[96,640]{1,0:T(8,128)(2,1)S(1)}, u32[]{:S(2)}, u32[]{:S(2)}) collective-permute-start(bf16[96,640]{1,0:T(8,128)(2,1)} %shard_map.237.b0), channel_id=1, source_target_pairs={{0,24},{4,28},{8,16},{12,20},{16,8},{20,12},{24,0},{28,4},{1,25},{... | collective-permute-start | bytes 368648 | tf_op jit(solution)/shard_map/ppermute | solution.py:337
  11.0 1.5 collective-permute-start.2
  12.5 2.4 collective-permute-done.7.b6
  14.9 2.2 collective-permute-start.9
  17.1 1.9 shard_map.239
  19.1 1.5 collective-permute-done.5.b4
  20.6 2.5 collective-permute-start.18
  23.0 2.3 collective-permute-start.16
  25.9 1.6 collective-permute-start.8
  27.5 3.5 %collective-permute-done.18.b6 = bf16[96,1152]{1,0:T(8,128)(2,1)S(1)} collective-permute-done((bf16[96,1152]{1,0:T(8,128)(2,1)}, bf16[96,1152]{1,0:T(8,128)(2,1)S(1)}, u32[]{:S(2)}, u32[]{:S(2)}) %collective-permute-start.18) | collective-permute-done | bytes 221216 | tf_op jit(solution)/shard_map/ppermute | solution.py:337
  31.0 1.5 collective-permute-start.6
  32.5 10.2 %collective-permute-done.16.b4 = bf16[96,1152]{1,0:T(8,128)(2,1)S(1)} collective-permute-done((bf16[96,1152]{1,0:T(8,128)(2,1)}, bf16[96,1152]{1,0:T(8,128)(2,1)S(1)}, u32[]{:S(2)}, u32[]{:S(2)}) %collective-permute-start.16) | collective-permute-done | bytes 221216 | tf_op jit(solution)/shard_map/ppermute | solution.py:337
  42.7 1.3 collective-permute-start.4
  44.7 1.3 collective-permute-start.19
  46.8 2.1 collective-permute-done.4.b3
  49.6 1.3 collective-permute-start.15
  51.7 11.4 %shard_map.238 = (bf16[4,256,768]{2,1,0:T(8,128)(2,1)}, bf16[4,256,768]{2,1,0:T(8,128)(2,1)}, bf16[768,640]{1,0:T(8,128)(2,1)}, f32[8,768]{1,0:T(8,128)}, bf16[4...) custom-call(s32[2,2]{1,0:T(2,128)} %table.3, ...), custom_call_target="tpu_custom_call" | custom-call | tf_op jit(solution)/shard_map/pallas_call | solution.py:824
  63.1 1.5 collective-permute-start.10
  66.4 2.5 collective-permute-start.22
  68.9 2.9 %shard_map.240 = (bf16[768,384]{1,0:T(8,128)(2,1)}, bf16[768,768]{1,0:T(8,128)(2,1)}) custom-call(bf16[96,1152]{1,0:T(8,128)(2,1)} %get-tuple-element.73.b0, bf16[96,1152]{1,0:T(8,128)(2,1)} %copy-done.32, bf16[96,1152]{1,0:T(8,128)(2,1)} %copy-done.31, bf16[96,1152]{1,0:T(8,128)(2,1)} %collective-permute-done.15.b3, bf16[96,1152]{1,0:T(8,128)(2,1)} %copy-done.30, ...), custom_call_target="tpu_custom_call" | custom-call | tf_op jit(solution)/shard_map/pallas_call | solution.py:836
  71.9 3.6 %collective-permute-done.24.b4 = bf16[96,768]{1,0:T(8,128)(2,1)S(1)} collective-permute-done((bf16[96,768]{1,0:T(8,128)(2,1)}, bf16[96,768]{1,0:T(8,128)(2,1)S(1)}, u32[]{:S(2)}, u32[]{:S(2)}) %collective-permute-start.24) | collective-permute-done | bytes 147488 | tf_op jit(solution)/shard_map/ppermute | solution.py:337
  77.7 3.2 %collective-permute-done.21.b1 = bf16[96,768]{1,0:T(8,128)(2,1)S(1)} collective-permute-done((bf16[96,768]{1,0:T(8,128)(2,1)}, bf16[96,768]{1,0:T(8,128)(2,1)S(1)}, u32[]{:S(2)}, u32[]{:S(2)}) %collective-permute-start.21) | collective-permute-done | bytes 147488 | tf_op jit(solution)/shard_map/ppermute | solution.py:337
  83.5 4.4 %collective-permute-done.25.b5 = bf16[96,768]{1,0:T(8,128)(2,1)S(1)} collective-permute-done((bf16[96,768]{1,0:T(8,128)(2,1)}, bf16[96,768]{1,0:T(8,128)(2,1)S(1)}, u32[]{:S(2)}, u32[]{:S(2)}) %collective-permute-start.25) | collective-permute-done | bytes 147488 | tf_op jit(solution)/shard_map/ppermute | solution.py:337
  88.8 4.4 %collective-permute-done.23.b3 = bf16[96,768]{1,0:T(8,128)(2,1)S(1)} collective-permute-done((bf16[96,768]{1,0:T(8,128)(2,1)}, bf16[96,768]{1,0:T(8,128)(2,1)S(1)}, u32[]{:S(2)}, u32[]{:S(2)}) %collective-permute-start.23) | collective-permute-done | bytes 147488 | tf_op jit(solution)/shard_map/ppermute | solution.py:337
  94.0 3.5 %shard_map.241 = (bf16[768,768]{1,0:T(8,128)(2,1)}, bf16[4,256,768]{2,1,0:T(8,128)(2,1)}) custom-call(bf16[96,768]{1,0:T(8,128)(2,1)} %get-tuple-element.76.b0, bf16[96,768]{1,0:T(8,128)(2,1)} %copy-done.37, bf16[96,768]{1,0:T(8,128)(2,1)} %copy-done.36, bf16[96,768]{1,0:T(8,128)(2,1)} %copy-done.40, bf16[96,768]{1,0:T(8,128)(2,1)} %copy-done.35, ...), custom_call_target="tpu_custom_call" | custom-call | tf_op jit(solution)/shard_map/pallas_call | solution.py:841
  98.6 13.9 %shard_map.242 = (f32[2,256,768]{2,1,0:T(8,128)}, bf16[4,256,768]{2,1,0:T(8,128)(2,1)}, bf16[4,256,768]{2,1,0:T(8,128)(2,1)}, bf16[4,256,768]{2,1,0:T(8,128)(2,1...) custom-call(bf16[4,256,768]{2,1,0:T(8,128)(2,1)} %get-tuple-element.71.x, ...), custom_call_target="tpu_custom_call" | custom-call | tf_op jit(solution)/shard_map/pallas_call | solution.py:846
  112.5 2.5 collective-permute-done.33.got
  115.9 2.2 shard_map.247
  119.0 10.5 %collective-permute-done.34.far = bf16[256,768]{1,0:T(8,128)(2,1)S(1)} collective-permute-done((bf16[256,768]{1,0:T(8,128)(2,1)}, bf16[256,768]{1,0:T(8,128)(2,1)S(1)}, u32[]{:S(2)}, u32[]{:S(2)}) %collective-permute-start.34) | collective-permute-done | bytes 393248 | tf_op jit(solution)/shard_map/ppermute | solution.py:345
  130.2 4.2 %shard_map.248 = (f32[256,768]{1,0:T(8,128)}, bf16[256,768]{1,0:T(8,128)(2,1)}, f32[8,768]{1,0:T(8,128)}) custom-call(bf16[2,256,768]{2,1,0:T(8,128)(2,1)} %get-tuple-element.86.keep, bf16[2,256,768]{2,1,0:T(8,128)(2,1)} %copy-done, bf16[256,768]{1,0:T(8,128)(2,1)} %copy-done.19, f32[2,256,768]{2,1,0:T(8,128)} %get-tuple-element.80.resid, ...), custom_call_target="tpu_custom_call" | custom-call | tf_op jit(solution)/shard_map/pallas_call | solution.py:886
  135.3 8.9 %shard_map.243 = (bf16[4,96,1536]{2,1,0:T(8,128)(2,1)}, bf16[4,96,1536]{2,1,0:T(8,128)(2,1)}, bf16[2,256,768]{2,1,0:T(8,128)(2,1)}, bf16[2,256,768]{2,1,0:T(8,128)(2,1)}) custom-call(bf16[4,256,768]{2,1,0:T(8,128)(2,1)} %get-tuple-element.79.cot, bf16[4,256,768]{2,1,0:T(8,128)(2,1)} %get-tuple-element.81.act, bf16[4,256,768]{2,1,0:T(8,128)(2,1)} %get-tuple-element.82.h_two, ...), custom_call_target="tpu_custom_call" | custom-call | tf_op jit(solution)/shard_map/pallas_call | solution.py:879
  148.3 12.4 %shard_map.249 = (bf16[4,576,256]{2,1,0:T(8,128)(2,1)}, f32[4,192,256]{2,1,0:T(8,128)}, bf16[4,96,192]{2,1,0:T(8,128)(2,1)}, bf16[4,96,192]{2,1,0:T(8,128)(2,1)}) custom-call(s32[2,2]{1,0:T(2,128)} %table.3, bf16[256,768]{1,0:T(8,128)(2,1)} %get-tuple-element.88.br0, bf16[256,768]{1,0:T(8,128)(2,1)} %copy-done.17, bf16[256,768]{1,0:T(8,128)(2,1)} %copy-done.16, ...), custom_call_target="tpu_custom_call" | custom-call | tf_op jit(solution)/shard_map/pallas_call | solution.py:897
  160.7 6.3 %shard_map.250 = (bf16[2,256,768]{2,1,0:T(8,128)(2,1)}, bf16[2,256,768]{2,1,0:T(8,128)(2,1)}, f32[8,768]{1,0:T(8,128)}) custom-call(bf16[4,576,256]{2,1,0:T(8,128)(2,1)} %get-tuple-element.92.d_qkv, bf16[768,640]{1,0:T(8,128)(2,1)} %get-tuple-element.93.w, bf16[4,256,768]{2,1,0:T(8,128)(2,1)} %get-tuple-element.71.x), custom_call_target="tpu_custom_call" | custom-call | tf_op jit(solution)/shard_map/pallas_call | solution.py:912
  168.0 2.2 shard_map.244
  172.4 2.7 %shard_map.262 = (bf16[96,1536]{1,0:T(8,128)(2,1)}, bf16[96,1536]{1,0:T(8,128)(2,1)}, bf16[96,1536]{1,0:T(8,128)(2,1)}, bf16[96,1536]{1,0:T(8,128)(2,1)}) custom-call(bf16[4,96,1536]{2,1,0:T(8,128)(2,1)} %get-tuple-element.117.keep, bf16[4,96,1536]{2,1,0:T(8,128)(2,1)} %copy-done.5), custom_call_target="tpu_custom_call" | custom-call | tf_op jit(solution)/shard_map/pallas_call | solution.py:685
  175.1 2.0 collective-permute-start.56
  179.0 4.1 %shard_map.256 = (bf16[4,96,640]{2,1,0:T(8,128)(2,1)}, bf16[4,96,640]{2,1,0:T(8,128)(2,1)}) custom-call(bf16[4,576,256]{2,1,0:T(8,128)(2,1)} %get-tuple-element.92.d_qkv, bf16[4,256,768]{2,1,0:T(8,128)(2,1)} %get-tuple-element.98.h_one, f32[8,768]{1,0:T(8,128)} %get-tuple-element.99.sums_one, f32[8,768]{1,0:T(8,128)} %get-tuple-element.100.sums_two, ...), custom_call_target="tpu_custom_call" | custom-call | tf_op jit(solution)/shard_map/pallas_call | solution.py:922
  185.8 2.2 shard_map.251
  189.7 2.4 shard_map.245.own
  192.1 8.2 %collective-permute-done.57.c = bf16[96,1536]{1,0:T(8,128)(2,1)} collective-permute-done((bf16[96,1536]{1,0:T(8,128)(2,1)}, bf16[96,1536]{1,0:T(8,128)(2,1)}, u32[]{:S(2)}, u32[]{:S(2)}) %collective-permute-start.57) | collective-permute-done | bytes 294944 | tf_op jit(solution)/shard_map/ppermute | solution.py:337
  200.3 1.6 collective-permute-start.58
  202.8 2.0 shard_map.257
  205.5 2.4 shard_map.252.own
  208.2 1.7 shard_map.259
  209.9 2.4 collective-permute-done.58.d
  212.2 1.9 collective-permute-start.51
  215.4 2.1 shard_map.263.own
  218.5 1.3 collective-permute-done.52.c
  220.6 2.2 collective-permute-start.48
  222.8 1.9 shard_map.254
  224.7 5.4 %collective-permute-done.47.c = bf16[96,640]{1,0:T(8,128)(2,1)S(1)} collective-permute-done((bf16[96,640]{1,0:T(8,128)(2,1)}, bf16[96,640]{1,0:T(8,128)(2,1)S(1)}, u32[]{:S(2)}, u32[]{:S(2)}) %collective-permute-start.47) | collective-permute-done | bytes 122912 | tf_op jit(solution)/shard_map/ppermute | solution.py:337
  230.0 1.3 collective-permute-start.42
  231.4 2.3 collective-permute-start.53
  233.7 1.8 shard_map.258.own
  235.4 2.1 collective-permute-done.53.d
  237.5 2.6 %collective-permute-start.49 = (bf16[96,640]{1,0:T(8,128)(2,1)}, bf16[96,640]{1,0:T(8,128)(2,1)S(1)}, u32[]{:S(2)}, u32[]{:S(2)}) collective-permute-start(bf16[96,640]{1,0:T(8,128)(2,1)} %shard_map.258.own), channel_id=1, source_target_pairs={{0,2},{2,0},{1,3},{3,1},{4,6},{6,4},{5,7},{7,5},{8,10},{10,8},{9,1... | collective-permute-start | bytes 368648 | tf_op jit(solution)/shard_map/ppermute | solution.py:345
  240.2 1.5 shard_map.260.own_proj
  242.4 2.9 %shard_map.246 = f32[3072,128]{1,0:T(8,128)} custom-call(f32[2,256,768]{2,1,0:T(8,128)} %get-tuple-element.80.resid, bf16[256,768]{1,0:T(8,128)(2,1)} %shard_map.245.own, bf16[256,768]{1,0:T(8,128)(2,1)} %copy-done.24), custom_call_target="tpu_custom_call" | custom-call | tf_op jit(solution)/shard_map/pallas_call | solution.py:934
  245.2 2.1 shard_map.264
  248.0 1.9 shard_map.255
  251.2 1.9 shard_map.261
  254.7 4.3 %shard_map.253 = f32[3072,128]{1,0:T(8,128)} custom-call(bf16[4,256,768]{2,1,0:T(8,128)(2,1)} %get-tuple-element.71.x, bf16[256,768]{1,0:T(8,128)(2,1)} %shard_map.252.own, bf16[256,768]{1,0:T(8,128)(2,1)} %copy-done.25, f32[256,768]{1,0:T(8,128)} %get-tuple-element.96.d_own, f32[256,768]{1,0:T(8,128)} %copy-done.7, f32[8,768]{1,0:T(8,128)} %get-tuple-element.78.gains), custom_call_target="tpu_custom_call" | custom-call | tf_op jit(solution)/shard_map/pallas_call | solution.py:937
  (206 shorter events, 41.1 us)
Async XLA Ops:
  0.6 50.2 %copy-start.3 = (bf16[512,1,768]{2,0,1:T(8,128)(2,1)S(1)}, bf16[512,1,768]{2,0,1:T(8,128)(2,1)}, u32[]{:S(2)}) copy-start(bf16[512,1,768]{2,0,1:T(8,128)(2,1)} %param.27) | copy-start | bytes 2359300
  1.8 24.1 %collective-permute-start = (bf16[256,768]{1,0:T(8,128)(2,1)S(1)}, bf16[256,768]{1,0:T(8,128)(2,1)S(1)}, u32[]{:S(2)}, u32[]{:S(2)}) collective-permute-start(bf16[256,768]{1,0:T(8,128)(2,1)S(1)} %dynamic-slice_bitcast_fusion.1), channel_id=1, source_target_pairs={{0,2},{2,0},{1,3},{3,1},{4,6},{6,4},{5,7},{7,5},{8,10},{10,8},{9,1... | collective-permute-start | bytes 1179656 | tf_op jit(solution)/shard_map/ppermute | solution.py:345
  6.6 8.3 %collective-permute-start.7 = (bf16[96,640]{1,0:T(8,128)(2,1)}, bf16[96,640]{1,0:T(8,128)(2,1)S(1)}, u32[]{:S(2)}, u32[]{:S(2)}) collective-permute-start(bf16[96,640]{1,0:T(8,128)(2,1)} %shard_map.237.b0), channel_id=1, source_target_pairs={{0,24},{4,28},{8,16},{12,20},{16,8},{20,12},{24,0},{28,4},{1,25},{... | collective-permute-start | bytes 368648 | tf_op jit(solution)/shard_map/ppermute | solution.py:337
  10.2 10.3 %collective-permute-start.5 = (bf16[96,640]{1,0:T(8,128)(2,1)}, bf16[96,640]{1,0:T(8,128)(2,1)S(1)}, u32[]{:S(2)}, u32[]{:S(2)}) collective-permute-start(bf16[96,640]{1,0:T(8,128)(2,1)} %shard_map.237.b0), channel_id=1, source_target_pairs={{0,16},{4,20},{8,24},{12,28},{16,0},{20,4},{24,8},{28,12},{1,17},{... | collective-permute-start | bytes 368648 | tf_op jit(solution)/shard_map/ppermute | solution.py:337
  10.3 12.8 %collective-permute-start.3 = (bf16[96,640]{1,0:T(8,128)(2,1)}, bf16[96,640]{1,0:T(8,128)(2,1)S(1)}, u32[]{:S(2)}, u32[]{:S(2)}) collective-permute-start(bf16[96,640]{1,0:T(8,128)(2,1)} %shard_map.237.b0), channel_id=1, source_target_pairs={{0,8},{4,12},{8,0},{12,4},{16,24},{20,28},{24,16},{28,20},{1,9},{5... | collective-permute-start | bytes 368648 | tf_op jit(solution)/shard_map/ppermute | solution.py:337
  11.0 14.3 %collective-permute-start.2 = (bf16[96,640]{1,0:T(8,128)(2,1)}, bf16[96,640]{1,0:T(8,128)(2,1)S(1)}, u32[]{:S(2)}, u32[]{:S(2)}) collective-permute-start(bf16[96,640]{1,0:T(8,128)(2,1)} %shard_map.237.b0), channel_id=1, source_target_pairs={{0,4},{4,0},{8,12},{12,8},{16,20},{20,16},{24,28},{28,24},{1,5},{5... | collective-permute-start | bytes 368648 | tf_op jit(solution)/shard_map/ppermute | solution.py:337
  14.9 34.0 %copy-start.44 = (bf16[96,640]{1,0:T(8,128)(2,1)}, bf16[96,640]{1,0:T(8,128)(2,1)S(1)}, u32[]{:S(2)}) copy-start(bf16[96,640]{1,0:T(8,128)(2,1)S(1)} %collective-permute-done.7.b6) | copy-start | bytes 368644
  14.9 11.0 %collective-permute-start.9 = (bf16[192,512]{1,0:T(8,128)(2,1)}, bf16[192,512]{1,0:T(8,128)(2,1)S(1)}, u32[]{:S(2)}, u32[]{:S(2)}) collective-permute-start(bf16[192,512]{1,0:T(8,128)(2,1)} %bitcast.27), channel_id=1, source_target_pairs={{0,2},{1,3},{4,6},{5,7},{8,10},{9,11},{12,14},{13,15},{16,18},{17,... | collective-permute-start | bytes 589832 | tf_op jit(solution)/shard_map/ppermute | solution.py:815
  20.6 28.3 %copy-start.45 = (bf16[96,640]{1,0:T(8,128)(2,1)}, bf16[96,640]{1,0:T(8,128)(2,1)S(1)}, u32[]{:S(2)}) copy-start(bf16[96,640]{1,0:T(8,128)(2,1)S(1)} %collective-permute-done.5.b4) | copy-start | bytes 368644
  20.6 10.4 %collective-permute-start.18 = (bf16[96,1152]{1,0:T(8,128)(2,1)}, bf16[96,1152]{1,0:T(8,128)(2,1)S(1)}, u32[]{:S(2)}, u32[]{:S(2)}) collective-permute-start(bf16[96,1152]{1,0:T(8,128)(2,1)} %get-tuple-element.73.b0), channel_id=1, source_target_pairs={{0,24},{4,28},{8,16},{12,20},{16,8},{20,12},{24,0},{28,4},{1,25},{... | collective-permute-start | bytes 663560 | tf_op jit(solution)/shard_map/ppermute | solution.py:337
  23.0 19.7 %collective-permute-start.16 = (bf16[96,1152]{1,0:T(8,128)(2,1)}, bf16[96,1152]{1,0:T(8,128)(2,1)S(1)}, u32[]{:S(2)}, u32[]{:S(2)}) collective-permute-start(bf16[96,1152]{1,0:T(8,128)(2,1)} %get-tuple-element.73.b0), channel_id=1, source_target_pairs={{0,16},{4,20},{8,24},{12,28},{16,0},{20,4},{24,8},{28,12},{1,17},{... | collective-permute-start | bytes 663560 | tf_op jit(solution)/shard_map/ppermute | solution.py:337
  25.3 18.6 %collective-permute-start.14 = (bf16[96,1152]{1,0:T(8,128)(2,1)}, bf16[96,1152]{1,0:T(8,128)(2,1)S(1)}, u32[]{:S(2)}, u32[]{:S(2)}) collective-permute-start(bf16[96,1152]{1,0:T(8,128)(2,1)} %get-tuple-element.73.b0), channel_id=1, source_target_pairs={{0,8},{4,12},{8,0},{12,4},{16,24},{20,28},{24,16},{28,20},{1,9},{5... | collective-permute-start | bytes 663560 | tf_op jit(solution)/shard_map/ppermute | solution.py:337
  25.9 25.0 %collective-permute-start.1 = (bf16[256,768]{1,0:T(8,128)(2,1)S(1)}, bf16[256,768]{1,0:T(8,128)(2,1)S(1)}, u32[]{:S(2)}, u32[]{:S(2)}) collective-permute-start(bf16[256,768]{1,0:T(8,128)(2,1)S(1)} %collective-permute-done.across), channel_id=1, source_target_pairs={{0,1},{1,0},{2,3},{3,2},{4,5},{5,4},{6,7},{7,6},{8,9},{9,8},{10,11... | collective-permute-start | bytes 1179656 | tf_op jit(solution)/shard_map/ppermute | solution.py:341
  25.9 18.8 %collective-permute-start.8 = (bf16[96,640]{1,0:T(8,128)(2,1)S(1)}, bf16[96,640]{1,0:T(8,128)(2,1)S(1)}, u32[]{:S(2)}, u32[]{:S(2)}) collective-permute-start(bf16[96,640]{1,0:T(8,128)(2,1)S(1)} %collective-permute-done.7.b6), channel_id=1, source_target_pairs={{0,4},{4,0},{8,12},{12,8},{16,20},{20,16},{24,28},{28,24},{1,5},{5... | collective-permute-start | bytes 368648 | tf_op jit(solution)/shard_map/ppermute | solution.py:337
  31.0 32.1 %copy-start.29 = (bf16[96,1152]{1,0:T(8,128)(2,1)}, bf16[96,1152]{1,0:T(8,128)(2,1)S(1)}, u32[]{:S(2)}) copy-start(bf16[96,1152]{1,0:T(8,128)(2,1)S(1)} %collective-permute-done.18.b6) | copy-start | bytes 663556
  31.0 15.0 %collective-permute-start.6 = (bf16[96,640]{1,0:T(8,128)(2,1)S(1)}, bf16[96,640]{1,0:T(8,128)(2,1)S(1)}, u32[]{:S(2)}, u32[]{:S(2)}) collective-permute-start(bf16[96,640]{1,0:T(8,128)(2,1)S(1)} %collective-permute-done.5.b4), channel_id=1, source_target_pairs={{0,4},{4,0},{8,12},{12,8},{16,20},{20,16},{24,28},{28,24},{1,5},{5... | collective-permute-start | bytes 368648 | tf_op jit(solution)/shard_map/ppermute | solution.py:337
  42.7 6.2 %collective-permute-start.4 = (bf16[96,640]{1,0:T(8,128)(2,1)S(1)}, bf16[96,640]{1,0:T(8,128)(2,1)S(1)}, u32[]{:S(2)}, u32[]{:S(2)}) collective-permute-start(bf16[96,640]{1,0:T(8,128)(2,1)S(1)} %collective-permute-done.3.b2), channel_id=1, source_target_pairs={{0,4},{4,0},{8,12},{12,8},{16,20},{20,16},{24,28},{28,24},{1,5},{5... | collective-permute-start | bytes 368648 | tf_op jit(solution)/shard_map/ppermute | solution.py:337
  44.0 19.1 %collective-permute-start.13 = (bf16[96,1152]{1,0:T(8,128)(2,1)}, bf16[96,1152]{1,0:T(8,128)(2,1)S(1)}, u32[]{:S(2)}, u32[]{:S(2)}) collective-permute-start(bf16[96,1152]{1,0:T(8,128)(2,1)} %get-tuple-element.73.b0), channel_id=1, source_target_pairs={{0,4},{4,0},{8,12},{12,8},{16,20},{20,16},{24,28},{28,24},{1,5},{5... | collective-permute-start | bytes 663560 | tf_op jit(solution)/shard_map/ppermute | solution.py:337
  44.7 19.8 %collective-permute-start.19 = (bf16[96,1152]{1,0:T(8,128)(2,1)S(1)}, bf16[96,1152]{1,0:T(8,128)(2,1)}, u32[]{:S(2)}, u32[]{:S(2)}) collective-permute-start(bf16[96,1152]{1,0:T(8,128)(2,1)S(1)} %collective-permute-done.18.b6), channel_id=1, source_target_pairs={{0,4},{4,0},{8,12},{12,8},{16,20},{20,16},{24,28},{28,24},{1,5},{5... | collective-permute-start | bytes 663560 | tf_op jit(solution)/shard_map/ppermute | solution.py:337
  46.0 19.7 %collective-permute-start.17 = (bf16[96,1152]{1,0:T(8,128)(2,1)S(1)}, bf16[96,1152]{1,0:T(8,128)(2,1)}, u32[]{:S(2)}, u32[]{:S(2)}) collective-permute-start(bf16[96,1152]{1,0:T(8,128)(2,1)S(1)} %collective-permute-done.16.b4), channel_id=1, source_target_pairs={{0,4},{4,0},{8,12},{12,8},{16,20},{20,16},{24,28},{28,24},{1,5},{5... | collective-permute-start | bytes 663560 | tf_op jit(solution)/shard_map/ppermute | solution.py:337
  49.6 16.8 %collective-permute-start.15 = (bf16[96,1152]{1,0:T(8,128)(2,1)S(1)}, bf16[96,1152]{1,0:T(8,128)(2,1)}, u32[]{:S(2)}, u32[]{:S(2)}) collective-permute-start(bf16[96,1152]{1,0:T(8,128)(2,1)S(1)} %collective-permute-done.14.b2), channel_id=1, source_target_pairs={{0,4},{4,0},{8,12},{12,8},{16,20},{20,16},{24,28},{28,24},{1,5},{5... | collective-permute-start | bytes 663560 | tf_op jit(solution)/shard_map/ppermute | solution.py:337
  50.9 26.7 %collective-permute-start.28 = (bf16[256,768]{1,0:T(8,128)(2,1)S(1)}, bf16[256,768]{1,0:T(8,128)(2,1)S(1)}, u32[]{:S(2)}, u32[]{:S(2)}) collective-permute-start(bf16[256,768]{1,0:T(8,128)(2,1)S(1)} %dynamic-slice_bitcast_fusion), channel_id=1, source_target_pairs={{0,2},{2,0},{1,3},{3,1},{4,6},{6,4},{5,7},{7,5},{8,10},{10,8},{9,1... | collective-permute-start | bytes 1179656 | tf_op jit(solution)/shard_map/ppermute | solution.py:345
  63.1 17.9 %collective-permute-start.10 = (bf16[4,192,256]{2,1,0:T(8,128)(2,1)}, bf16[4,192,256]{2,1,0:T(8,128)(2,1)S(1)}, u32[]{:S(2)}, u32[]{:S(2)}) collective-permute-start(bf16[4,192,256]{2,1,0:T(8,128)(2,1)} %get-tuple-element.72.mix0.low_mix), channel_id=1, source_target_pairs={{0,2},{2,0},{1,3},{3,1},{4,6},{6,4},{5,7},{7,5},{8,10},{10,8},{9,1... | collective-permute-start | bytes 1179656 | tf_op jit(solution)/shard_map/ppermute | solution.py:345
  64.5 7.4 %collective-permute-start.26 = (bf16[96,768]{1,0:T(8,128)(2,1)}, bf16[96,768]{1,0:T(8,128)(2,1)}, u32[]{:S(2)}, u32[]{:S(2)}) collective-permute-start(bf16[96,768]{1,0:T(8,128)(2,1)} %get-tuple-element.76.b0), channel_id=1, source_target_pairs={{0,24},{4,28},{8,16},{12,20},{16,8},{20,12},{24,0},{28,4},{1,25},{... | collective-permute-start | bytes 442376 | tf_op jit(solution)/shard_map/ppermute | solution.py:337
  65.7 9.8 %collective-permute-start.24 = (bf16[96,768]{1,0:T(8,128)(2,1)}, bf16[96,768]{1,0:T(8,128)(2,1)S(1)}, u32[]{:S(2)}, u32[]{:S(2)}) collective-permute-start(bf16[96,768]{1,0:T(8,128)(2,1)} %get-tuple-element.76.b0), channel_id=1, source_target_pairs={{0,16},{4,20},{8,24},{12,28},{16,0},{20,4},{24,8},{28,12},{1,17},{... | collective-permute-start | bytes 442376 | tf_op jit(solution)/shard_map/ppermute | solution.py:337
  66.4 10.1 %collective-permute-start.22 = (bf16[96,768]{1,0:T(8,128)(2,1)}, bf16[96,768]{1,0:T(8,128)(2,1)S(1)}, u32[]{:S(2)}, u32[]{:S(2)}) collective-permute-start(bf16[96,768]{1,0:T(8,128)(2,1)} %get-tuple-element.76.b0), channel_id=1, source_target_pairs={{0,8},{4,12},{8,0},{12,4},{16,24},{20,28},{24,16},{28,20},{1,9},{5... | collective-permute-start | bytes 442376 | tf_op jit(solution)/shard_map/ppermute | solution.py:337
  71.9 25.6 %collective-permute-start.20 = (bf16[768,384]{1,0:T(8,128)(2,1)}, bf16[768,384]{1,0:T(8,128)(2,1)S(1)}, u32[]{:S(2)}, u32[]{:S(2)}) collective-permute-start(bf16[768,384]{1,0:T(8,128)(2,1)} %get-tuple-element.74.wo_own.wo), channel_id=1, source_target_pairs={{0,1},{1,0},{2,3},{3,2},{4,5},{5,4},{6,7},{7,6},{8,9},{9,8},{10,11... | collective-permute-start | bytes 1769480 | tf_op jit(solution)/shard_map/ppermute | solution.py:341
  75.5 5.4 %collective-permute-start.21 = (bf16[96,768]{1,0:T(8,128)(2,1)}, bf16[96,768]{1,0:T(8,128)(2,1)S(1)}, u32[]{:S(2)}, u32[]{:S(2)}) collective-permute-start(bf16[96,768]{1,0:T(8,128)(2,1)} %get-tuple-element.76.b0), channel_id=1, source_target_pairs={{0,4},{4,0},{8,12},{12,8},{16,20},{20,16},{24,28},{28,24},{1,5},{5... | collective-permute-start | bytes 442376 | tf_op jit(solution)/shard_map/ppermute | solution.py:337
  76.5 6.0 %collective-permute-start.27 = (bf16[96,768]{1,0:T(8,128)(2,1)}, bf16[96,768]{1,0:T(8,128)(2,1)S(1)}, u32[]{:S(2)}, u32[]{:S(2)}) collective-permute-start(bf16[96,768]{1,0:T(8,128)(2,1)} %collective-permute-done.26.b6), channel_id=1, source_target_pairs={{0,4},{4,0},{8,12},{12,8},{16,20},{20,16},{24,28},{28,24},{1,5},{5... | collective-permute-start | bytes 442376 | tf_op jit(solution)/shard_map/ppermute | solution.py:337
  77.6 15.6 %collective-permute-start.29 = (bf16[256,768]{1,0:T(8,128)(2,1)S(1)}, bf16[256,768]{1,0:T(8,128)(2,1)S(1)}, u32[]{:S(2)}, u32[]{:S(2)}) collective-permute-start(bf16[256,768]{1,0:T(8,128)(2,1)S(1)} %collective-permute-done.28.across), channel_id=1, source_target_pairs={{0,1},{1,0},{2,3},{3,2},{4,5},{5,4},{6,7},{7,6},{8,9},{9,8},{10,11... | collective-permute-start | bytes 1179656 | tf_op jit(solution)/shard_map/ppermute | solution.py:341
  80.9 16.6 %collective-permute-start.11 = (bf16[4,192,256]{2,1,0:T(8,128)(2,1)S(1)}, bf16[4,192,256]{2,1,0:T(8,128)(2,1)S(1)}, u32[]{:S(2)}, u32[]{:S(2)}) collective-permute-start(bf16[4,192,256]{2,1,0:T(8,128)(2,1)S(1)} %copy-done.4), channel_id=1, source_target_pairs={{0,1},{1,0},{2,3},{3,2},{4,5},{5,4},{6,7},{7,6},{8,9},{9,8},{10,11... | collective-permute-start | bytes 1179656 | tf_op jit(solution)/shard_map/ppermute | solution.py:341
  80.9 16.6 %collective-permute-start.12 = (bf16[4,192,256]{2,1,0:T(8,128)(2,1)S(1)}, bf16[4,192,256]{2,1,0:T(8,128)(2,1)S(1)}, u32[]{:S(2)}, u32[]{:S(2)}) collective-permute-start(bf16[4,192,256]{2,1,0:T(8,128)(2,1)S(1)} %collective-permute-done.10.mix1), channel_id=1, source_target_pairs={{0,1},{1,0},{2,3},{3,2},{4,5},{5,4},{6,7},{7,6},{8,9},{9,8},{10,11... | collective-permute-start | bytes 1179656 | tf_op jit(solution)/shard_map/ppermute | solution.py:341
  82.5 5.4 %collective-permute-start.25 = (bf16[96,768]{1,0:T(8,128)(2,1)}, bf16[96,768]{1,0:T(8,128)(2,1)S(1)}, u32[]{:S(2)}, u32[]{:S(2)}) collective-permute-start(bf16[96,768]{1,0:T(8,128)(2,1)} %copy-done.35), channel_id=1, source_target_pairs={{0,4},{4,0},{8,12},{12,8},{16,20},{20,16},{24,28},{28,24},{1,5},{5... | collective-permute-start | bytes 442376 | tf_op jit(solution)/shard_map/ppermute | solution.py:337
  87.8 5.4 %collective-permute-start.23 = (bf16[96,768]{1,0:T(8,128)(2,1)}, bf16[96,768]{1,0:T(8,128)(2,1)S(1)}, u32[]{:S(2)}, u32[]{:S(2)}) collective-permute-start(bf16[96,768]{1,0:T(8,128)(2,1)} %copy-done.36), channel_id=1, source_target_pairs={{0,4},{4,0},{8,12},{12,8},{16,20},{20,16},{24,28},{28,24},{1,5},{5... | collective-permute-start | bytes 442376 | tf_op jit(solution)/shard_map/ppermute | solution.py:337
  112.4 2.6 collective-permute-start.33
  118.1 11.4 %collective-permute-start.34 = (bf16[256,768]{1,0:T(8,128)(2,1)}, bf16[256,768]{1,0:T(8,128)(2,1)S(1)}, u32[]{:S(2)}, u32[]{:S(2)}) collective-permute-start(bf16[256,768]{1,0:T(8,128)(2,1)} %shard_map.247), channel_id=1, source_target_pairs={{0,2},{2,0},{1,3},{3,1},{4,6},{6,4},{5,7},{7,5},{8,10},{10,8},{9,1... | collective-permute-start | bytes 1179656 | tf_op jit(solution)/shard_map/ppermute | solution.py:345
  134.4 10.8 %collective-permute-start.36 = (bf16[256,768]{1,0:T(8,128)(2,1)}, bf16[256,768]{1,0:T(8,128)(2,1)S(1)}, u32[]{:S(2)}, u32[]{:S(2)}) collective-permute-start(bf16[256,768]{1,0:T(8,128)(2,1)} %get-tuple-element.88.br0), channel_id=1, source_target_pairs={{0,2},{2,0},{1,3},{3,1},{4,6},{6,4},{5,7},{7,5},{8,10},{10,8},{9,1... | collective-permute-start | bytes 1179656 | tf_op jit(solution)/shard_map/ppermute | solution.py:345
  144.3 27.1 %collective-permute-start.55 = (bf16[4,96,1536]{2,1,0:T(8,128)(2,1)}, bf16[4,96,1536]{2,1,0:T(8,128)(2,1)S(1)}, u32[]{:S(2)}, u32[]{:S(2)}) collective-permute-start(bf16[4,96,1536]{2,1,0:T(8,128)(2,1)} %get-tuple-element.118), channel_id=1, source_target_pairs={{0,4},{4,0},{8,12},{12,8},{16,20},{20,16},{24,28},{28,24},{1,5},{5... | collective-permute-start | bytes 3538952 | tf_op jit(solution)/shard_map/ppermute | solution.py:337
  145.2 1.7 collective-permute-start.35
  145.3 2.3 collective-permute-start.37
  145.8 21.4 %collective-permute-start.30 = (bf16[2,256,768]{2,1,0:T(8,128)(2,1)}, bf16[2,256,768]{2,1,0:T(8,128)(2,1)S(1)}, u32[]{:S(2)}, u32[]{:S(2)}) collective-permute-start(bf16[2,256,768]{2,1,0:T(8,128)(2,1)} %get-tuple-element.85), channel_id=1, source_target_pairs={{0,1},{1,0},{2,3},{3,2},{4,5},{5,4},{6,7},{7,6},{8,9},{9,8},{10,11... | collective-permute-start | bytes 2359304 | tf_op jit(solution)/shard_map/ppermute | solution.py:341
  167.0 17.9 %collective-permute-start.38 = (bf16[2,256,768]{2,1,0:T(8,128)(2,1)}, bf16[2,256,768]{2,1,0:T(8,128)(2,1)S(1)}, u32[]{:S(2)}, u32[]{:S(2)}) collective-permute-start(bf16[2,256,768]{2,1,0:T(8,128)(2,1)} %get-tuple-element.95), channel_id=1, source_target_pairs={{0,1},{1,0},{2,3},{3,2},{4,5},{5,4},{6,7},{7,6},{8,9},{9,8},{10,11... | collective-permute-start | bytes 2359304 | tf_op jit(solution)/shard_map/ppermute | solution.py:341
  170.2 18.7 %collective-permute-start.31 = (bf16[256,768]{1,0:T(8,128)(2,1)}, bf16[256,768]{1,0:T(8,128)(2,1)S(1)}, u32[]{:S(2)}, u32[]{:S(2)}) collective-permute-start(bf16[256,768]{1,0:T(8,128)(2,1)} %shard_map.244), channel_id=1, source_target_pairs={{0,2},{2,0},{1,3},{3,1},{4,6},{6,4},{5,7},{7,5},{8,10},{10,8},{9,1... | collective-permute-start | bytes 1179656 | tf_op jit(solution)/shard_map/ppermute | solution.py:345
  175.1 16.9 %collective-permute-start.56 = (bf16[96,1536]{1,0:T(8,128)(2,1)}, bf16[96,1536]{1,0:T(8,128)(2,1)S(1)}, u32[]{:S(2)}, u32[]{:S(2)}) collective-permute-start(bf16[96,1536]{1,0:T(8,128)(2,1)} %get-tuple-element.120), channel_id=1, source_target_pairs={{0,8},{4,12},{8,0},{12,4},{16,24},{20,28},{24,16},{28,20},{1,9},{5... | collective-permute-start | bytes 884744 | tf_op jit(solution)/shard_map/ppermute | solution.py:337
  177.1 1.2 collective-permute-start.44
  177.1 1.3 collective-permute-start.43
  183.2 18.7 %collective-permute-start.45 = (bf16[4,96,640]{2,1,0:T(8,128)(2,1)}, bf16[4,96,640]{2,1,0:T(8,128)(2,1)S(1)}, u32[]{:S(2)}, u32[]{:S(2)}) collective-permute-start(bf16[4,96,640]{2,1,0:T(8,128)(2,1)} %get-tuple-element.102), channel_id=1, source_target_pairs={{0,4},{4,0},{8,12},{12,8},{16,20},{20,16},{24,28},{28,24},{1,5},{5... | collective-permute-start | bytes 1474568 | tf_op jit(solution)/shard_map/ppermute | solution.py:337
  184.2 16.0 %collective-permute-start.57 = (bf16[96,1536]{1,0:T(8,128)(2,1)}, bf16[96,1536]{1,0:T(8,128)(2,1)}, u32[]{:S(2)}, u32[]{:S(2)}) collective-permute-start(bf16[96,1536]{1,0:T(8,128)(2,1)} %get-tuple-element.121), channel_id=1, source_target_pairs={{0,16},{4,20},{8,24},{12,28},{16,0},{20,4},{24,8},{28,12},{1,17},{... | collective-permute-start | bytes 884744 | tf_op jit(solution)/shard_map/ppermute | solution.py:337
  188.0 16.8 %collective-permute-start.39 = (bf16[256,768]{1,0:T(8,128)(2,1)}, bf16[256,768]{1,0:T(8,128)(2,1)S(1)}, u32[]{:S(2)}, u32[]{:S(2)}) collective-permute-start(bf16[256,768]{1,0:T(8,128)(2,1)} %shard_map.251), channel_id=1, source_target_pairs={{0,2},{2,0},{1,3},{3,1},{4,6},{6,4},{5,7},{7,5},{8,10},{10,8},{9,1... | collective-permute-start | bytes 1179656 | tf_op jit(solution)/shard_map/ppermute | solution.py:345
  188.9 64.2 %collective-permute-start.41 = (f32[256,768]{1,0:T(8,128)S(1)}, f32[256,768]{1,0:T(8,128)S(1)}, u32[]{:S(2)}, u32[]{:S(2)}) collective-permute-start(f32[256,768]{1,0:T(8,128)S(1)} %copy-done.6), channel_id=1, source_target_pairs={{0,1},{1,0},{2,3},{3,2},{4,5},{5,4},{6,7},{7,6},{8,9},{9,8},{10,11... | collective-permute-start | bytes 2359304 | tf_op jit(solution)/shard_map/ppermute | solution.py:341
  192.1 22.1 %collective-permute-start.32 = (bf16[256,768]{1,0:T(8,128)(2,1)}, bf16[256,768]{1,0:T(8,128)(2,1)S(1)}, u32[]{:S(2)}, u32[]{:S(2)}) collective-permute-start(bf16[256,768]{1,0:T(8,128)(2,1)} %shard_map.245.own), channel_id=1, source_target_pairs={{0,1},{1,0},{2,3},{3,2},{4,5},{5,4},{6,7},{7,6},{8,9},{9,8},{10,11... | collective-permute-start | bytes 1179656 | tf_op jit(solution)/shard_map/ppermute | solution.py:341
  200.3 12.0 %collective-permute-start.58 = (bf16[96,1536]{1,0:T(8,128)(2,1)}, bf16[96,1536]{1,0:T(8,128)(2,1)S(1)}, u32[]{:S(2)}, u32[]{:S(2)}) collective-permute-start(bf16[96,1536]{1,0:T(8,128)(2,1)} %get-tuple-element.122), channel_id=1, source_target_pairs={{0,24},{4,28},{8,16},{12,20},{16,8},{20,12},{24,0},{28,4},{1,25},{... | collective-permute-start | bytes 884744 | tf_op jit(solution)/shard_map/ppermute | solution.py:337
  201.8 6.3 %collective-permute-start.50 = (bf16[4,96,192]{2,1,0:T(8,128)(2,1)}, bf16[4,96,192]{2,1,0:T(8,128)(2,1)}, u32[]{:S(2)}, u32[]{:S(2)}) collective-permute-start(bf16[4,96,192]{2,1,0:T(8,128)(2,1)} %get-tuple-element.108), channel_id=1, source_target_pairs={{0,4},{4,0},{8,12},{12,8},{16,20},{20,16},{24,28},{28,24},{1,5},{5... | collective-permute-start | bytes 442376 | tf_op jit(solution)/shard_map/ppermute | solution.py:337
  204.8 15.8 %collective-permute-start.46 = (bf16[96,640]{1,0:T(8,128)(2,1)}, bf16[96,640]{1,0:T(8,128)(2,1)}, u32[]{:S(2)}, u32[]{:S(2)}) collective-permute-start(bf16[96,640]{1,0:T(8,128)(2,1)} %get-tuple-element.104), channel_id=1, source_target_pairs={{0,8},{4,12},{8,0},{12,4},{16,24},{20,28},{24,16},{28,20},{1,9},{5... | collective-permute-start | bytes 368648 | tf_op jit(solution)/shard_map/ppermute | solution.py:337
  208.2 45.0 %collective-permute-start.40 = (bf16[256,768]{1,0:T(8,128)(2,1)}, bf16[256,768]{1,0:T(8,128)(2,1)S(1)}, u32[]{:S(2)}, u32[]{:S(2)}) collective-permute-start(bf16[256,768]{1,0:T(8,128)(2,1)} %shard_map.252.own), channel_id=1, source_target_pairs={{0,1},{1,0},{2,3},{3,2},{4,5},{5,4},{6,7},{7,6},{8,9},{9,8},{10,11... | collective-permute-start | bytes 1179656 | tf_op jit(solution)/shard_map/ppermute | solution.py:341
  212.2 5.2 %collective-permute-start.51 = (bf16[96,192]{1,0:T(8,128)(2,1)}, bf16[96,192]{1,0:T(8,128)(2,1)S(1)}, u32[]{:S(2)}, u32[]{:S(2)}) collective-permute-start(bf16[96,192]{1,0:T(8,128)(2,1)} %get-tuple-element.110), channel_id=1, source_target_pairs={{0,8},{4,12},{8,0},{12,4},{16,24},{20,28},{24,16},{28,20},{1,9},{5... | collective-permute-start | bytes 110600 | tf_op jit(solution)/shard_map/ppermute | solution.py:337
  214.1 5.7 %collective-permute-start.52 = (bf16[96,192]{1,0:T(8,128)(2,1)}, bf16[96,192]{1,0:T(8,128)(2,1)S(1)}, u32[]{:S(2)}, u32[]{:S(2)}) collective-permute-start(bf16[96,192]{1,0:T(8,128)(2,1)} %get-tuple-element.111), channel_id=1, source_target_pairs={{0,16},{4,20},{8,24},{12,28},{16,0},{20,4},{24,8},{28,12},{1,17},{... | collective-permute-start | bytes 110600 | tf_op jit(solution)/shard_map/ppermute | solution.py:337
  217.5 24.2 %collective-permute-start.59 = (bf16[96,1536]{1,0:T(8,128)(2,1)}, bf16[96,1536]{1,0:T(8,128)(2,1)S(1)}, u32[]{:S(2)}, u32[]{:S(2)}) collective-permute-start(bf16[96,1536]{1,0:T(8,128)(2,1)} %shard_map.263.own), channel_id=1, source_target_pairs={{0,2},{2,0},{1,3},{3,1},{4,6},{6,4},{5,7},{7,5},{8,10},{10,8},{9,1... | collective-permute-start | bytes 884744 | tf_op jit(solution)/shard_map/ppermute | solution.py:345
  219.8 10.2 %collective-permute-start.47 = (bf16[96,640]{1,0:T(8,128)(2,1)}, bf16[96,640]{1,0:T(8,128)(2,1)S(1)}, u32[]{:S(2)}, u32[]{:S(2)}) collective-permute-start(bf16[96,640]{1,0:T(8,128)(2,1)} %get-tuple-element.105), channel_id=1, source_target_pairs={{0,16},{4,20},{8,24},{12,28},{16,0},{20,4},{24,8},{28,12},{1,17},{... | collective-permute-start | bytes 368648 | tf_op jit(solution)/shard_map/ppermute | solution.py:337
  220.6 10.7 %collective-permute-start.48 = (bf16[96,640]{1,0:T(8,128)(2,1)}, bf16[96,640]{1,0:T(8,128)(2,1)S(1)}, u32[]{:S(2)}, u32[]{:S(2)}) collective-permute-start(bf16[96,640]{1,0:T(8,128)(2,1)} %get-tuple-element.106), channel_id=1, source_target_pairs={{0,24},{4,28},{8,16},{12,20},{16,8},{20,12},{24,0},{28,4},{1,25},{... | collective-permute-start | bytes 368648 | tf_op jit(solution)/shard_map/ppermute | solution.py:337
  230.0 17.3 %collective-permute-start.42 = (bf16[192,512]{1,0:T(8,128)(2,1)}, bf16[192,512]{1,0:T(8,128)(2,1)S(1)}, u32[]{:S(2)}, u32[]{:S(2)}) collective-permute-start(bf16[192,512]{1,0:T(8,128)(2,1)} %shard_map.254), channel_id=1, source_target_pairs={{2,0},{3,1},{6,4},{7,5},{10,8},{11,9},{14,12},{15,13},{18,16},{19,... | collective-permute-start | bytes 589832 | tf_op jit(solution)/shard_map/ppermute | solution.py:943
  231.4 6.2 %collective-permute-start.53 = (bf16[96,192]{1,0:T(8,128)(2,1)}, bf16[96,192]{1,0:T(8,128)(2,1)S(1)}, u32[]{:S(2)}, u32[]{:S(2)}) collective-permute-start(bf16[96,192]{1,0:T(8,128)(2,1)} %get-tuple-element.112), channel_id=1, source_target_pairs={{0,24},{4,28},{8,16},{12,20},{16,8},{20,12},{24,0},{28,4},{1,25},{... | collective-permute-start | bytes 110600 | tf_op jit(solution)/shard_map/ppermute | solution.py:337
  237.5 12.5 %collective-permute-start.49 = (bf16[96,640]{1,0:T(8,128)(2,1)}, bf16[96,640]{1,0:T(8,128)(2,1)S(1)}, u32[]{:S(2)}, u32[]{:S(2)}) collective-permute-start(bf16[96,640]{1,0:T(8,128)(2,1)} %shard_map.258.own), channel_id=1, source_target_pairs={{0,2},{2,0},{1,3},{3,1},{4,6},{6,4},{5,7},{7,5},{8,10},{10,8},{9,1... | collective-permute-start | bytes 368648 | tf_op jit(solution)/shard_map/ppermute | solution.py:345
  241.7 8.3 %collective-permute-start.54 = (bf16[96,192]{1,0:T(8,128)(2,1)}, bf16[96,192]{1,0:T(8,128)(2,1)S(1)}, u32[]{:S(2)}, u32[]{:S(2)}) collective-permute-start(bf16[96,192]{1,0:T(8,128)(2,1)} %shard_map.260.own_proj), channel_id=1, source_target_pairs={{0,2},{2,0},{1,3},{3,1},{4,6},{6,4},{5,7},{7,5},{8,10},{10,8},{9,1... | collective-permute-start | bytes 110600 | tf_op jit(solution)/shard_map/ppermute | solution.py:345
  (55 other events, 414.3 us)

commit v2 on v1

--- a/solution.py
+++ b/solution.py
@@ -345,14 +345,16 @@
     return lax.ppermute(value, "ctx", [(0, 1), (1, 0)])
 
 
-def gather_blocks(shard):
-    count = lax.axis_size("fsdp")
-    blocks = {0: shard}
-    for k in range(1, count // 2):
-        blocks[2 * k] = swap_fsdp(shard, 2 * k)
-    for k in range(count // 2):
-        blocks[2 * k + 1] = swap_fsdp(blocks[2 * k], 1)
-    return [blocks[m] for m in range(count)]
+def after(value, *others):
+    return lax.optimization_barrier((value, others))[0]
+
+
+def gather_columns(shard):
+    return [shard] + [swap_fsdp(shard, 2 * k) for k in range(1, lax.axis_size("fsdp") // 2)]
+
+
+def gather_pairs(near):
+    return [block for mine in near for block in (mine, swap_fsdp(mine, 1))]
 
 
 def matmul(left, right, left_dim, right_dim):
@@ -390,16 +392,16 @@
     out[...] = jnp.concatenate([pick(wq), pick(wk), wv[...].astype(wide), gains, pad], axis=1).astype(low)
 
 
-def pack_late_kernel(wo, wu, wd, out_up, out_down):
+def pack_late_kernel(wo, wu, wd, out):
     rank = lax.axis_index("ctx")
     cols, units = wo.shape[1], wu.shape[1] // 2
     block = wo[...].astype(wide)
     even, odd = parity_heads(block, 0), parity_heads(block, 1)
     own = jnp.where(rank == 0, even, odd)
     other = jnp.where(rank == 0, odd, even)
-    out_up[:, :cols] = jnp.concatenate([own, other], axis=1).astype(low)
-    out_up[:, cols:] = jnp.where(rank == 0, wu[:, :units], wu[:, units:])
-    out_down[...] = jnp.where(rank == 0, wd[:, :units], wd[:, units:])
+    out[:, :cols] = jnp.concatenate([own, other], axis=1).astype(low)
+    out[:, cols : cols + units] = jnp.where(rank == 0, wu[:, :units], wu[:, units:])
+    out[:, cols + units :] = jnp.where(rank == 0, wd[:, :units], wd[:, units:])
 
 
 def place_blocks(blocks, store):
@@ -422,10 +424,10 @@
     return [sum(jnp.where(held[q] == p, q, 0) for q in range(4)) for p in range(4)]
 
 
-def attn_kernel(table, hid, across, across2, b0, b1, b2, b3, b4, b5, b6, b7, first, first_far,
+def attn_kernel(table, hid, pair, pair2, b0, b1, b2, b3, b4, b5, b6, b7, first, first_far,
                 x_out, h_out, w_out, gains_out, qkv_out, mix_out, low_out, lse_out, keys_scr):
     rank, side = lax.axis_index("ctx"), lax.axis_index("tp")
-    span = across.shape[0]
+    span = pair.shape[1]
     cols = first.shape[0]
     heads = cols // HEAD_DIM
 
@@ -438,8 +440,8 @@
     gain, shift = gains[0:1], gains[1:2]
     x_out[0] = hid[pl.ds(pl.multiple_of(side * span, span), span), :]
     x_out[1] = hid[pl.ds(pl.multiple_of((1 - side) * span, span), span), :]
-    x_out[2] = across[...]
-    x_out[3] = across2[...]
+    x_out[2] = pair[0]
+    x_out[3] = pair2[0]
     step = 64
 
     def norm_chunk(i, carry):
@@ -489,28 +491,21 @@
             lse_out[order[qp], h : h + 1, :] = top + jnp.log(total)
 
 
-def place_up_kernel(b0, b1, b2, b3, b4, b5, b6, b7, wo_out, wu_out):
-    cols = wo_out.shape[1]
+def place_late_kernel(b0, b1, b2, b3, b4, b5, b6, b7, cot, pair, pair2, wo_out, wu_out, wd_out, cot_out):
+    side = lax.axis_index("tp")
+    span = pair.shape[1]
+    cols, units = wo_out.shape[1], wu_out.shape[1]
 
     def store(where, block):
         wo_out[where, :] = block[:, :cols]
-        wu_out[where, :] = block[:, cols:]
-
-    place_blocks((b0, b1, b2, b3, b4, b5, b6, b7), store)
-
-
-def place_down_kernel(b0, b1, b2, b3, b4, b5, b6, b7, cot, across, across2, wd_out, cot_out):
-    side = lax.axis_index("tp")
-    span = across.shape[0]
-
-    def store(where, block):
-        wd_out[where, :] = block[...]
+        wu_out[where, :] = block[:, cols : cols + units]
+        wd_out[where, :] = block[:, cols + units :]
 
     place_blocks((b0, b1, b2, b3, b4, b5, b6, b7), store)
     cot_out[0] = cot[pl.ds(pl.multiple_of(side * span, span), span), :]
     cot_out[1] = cot[pl.ds(pl.multiple_of((1 - side) * span, span), span), :]
-    cot_out[2] = across[...]
-    cot_out[3] = across2[...]
+    cot_out[2] = pair[1]
+    cot_out[3] = pair2[1]
 
 
 def mlp_kernel(x, mix0, mix1, mix2, mix3, wo_own, wo_side, wu, wd, gains, cot,
@@ -587,20 +582,16 @@
     low_out[...] = d_resid.astype(low)
 
 
-def attn_back_kernel(table, br0, br1, br2, br3, wo, qkv, mix, lse, low_mix, d_out, d_first, keep_out, send_out,
-                     dm_scr, keys_scr, values_scr, dq_scr, grad):
+def attn_back_kernel(table, br0, br1, br2, br3, wo, qkv, mix, lse, d_out, d_first,
+                     dm_scr, keys_scr, values_scr, dq_scr):
     rank = lax.axis_index("ctx")
     span = qkv.shape[2]
     cols = mix.shape[1]
     heads = cols // HEAD_DIM
     wo_turned = wo[:, :cols].T
     branches = (br0, br1, br2, br3)
-    turned = jnp.zeros((cols, wo.shape[0]), wide)
     for q in range(4):
         dm_scr[q] = matmul(wo_turned, branches[q][...], 1, 1).astype(low)
-        turned = turned + matmul(low_mix[q], branches[q][...], 1, 0)
-    grad[...] = turned.T
-    scatter_slots(grad, keep_out, send_out, slice(0, cols))
     order = quarter_of_place(table)
     below = lax.broadcasted_iota(jnp.int32, (span, span), 0) <= lax.broadcasted_iota(jnp.int32, (span, span), 1)
     root = low(HEAD_DIM ** -0.5)
@@ -635,7 +626,7 @@
             d_out[order[qp], mine, :] = (dq_scr[qp] * HEAD_DIM ** -0.5).astype(low)
 
 
-def d_one_kernel(d_qkv, w, x, keep_out, send_out, sums_out):
+def d_one_kernel(d_qkv, w, x, sums_two, keep_out, send_out, sums_out):
     q = pl.program_id(0)
     wide_cols = d_qkv.shape[1]
     part = matmul(d_qkv[0].T, w[:, :wide_cols], 1, 1)
@@ -643,7 +634,7 @@
 
     @pl.when(q == 0)
     def _():
-        sums_out[...] = jnp.zeros_like(sums_out)
+        sums_out[...] = jnp.concatenate([jnp.zeros_like(sums_two), sums_two[...]], axis=0)[6:14]
 
     sums_out[0:1, :] += jnp.sum(part * unit, axis=0, keepdims=True)
     sums_out[1:2, :] += jnp.sum(part, axis=0, keepdims=True)
@@ -657,18 +648,23 @@
         send_out[0] = part.astype(low)
 
 
-def attn_grad_kernel(d_qkv, h_one, sums_one, sums_two, side_one, side_two, keep_out, send_out, grad):
-    cols = d_qkv.shape[1]
-    width = h_one.shape[2]
+def attn_grad_kernel(d_qkv, h_one, keep_out, send_out, grad):
     turned = matmul(d_qkv[0], h_one[0], 1, 0)
     for q in range(1, 4):
         turned = turned + matmul(d_qkv[q], h_one[q], 1, 0)
-    grad[:, :cols] = turned.T
-    one = sums_one[...] + side_one[...].astype(wide)
-    two = sums_two[...] + side_two[...].astype(wide)
-    sums = jnp.concatenate([one[0:2], two[0:2], jnp.zeros((124, width), wide)], axis=0).T
-    grad[:, cols:] = sums[:, :HEAD_DIM]
-    scatter_slots(grad, keep_out, send_out, slice(0, cols + HEAD_DIM))
+    grad[...] = turned.T
+    scatter_slots(grad, keep_out, send_out, slice(None))
+
+
+def proj_grad_kernel(low_mix, br0, br1, br2, br3, sums, sums_side, keep_out, send_out, grad):
+    cols = low_mix.shape[1]
+    turned = matmul(low_mix[0], br0[...], 1, 0)
+    for q, branch in ((1, br1), (2, br2), (3, br3)):
+        turned = turned + matmul(low_mix[q], branch[...], 1, 0)
+    gains = sums[...] + sums_side[...].astype(wide)
+    pad = jnp.zeros((HEAD_DIM - gains.shape[0], gains.shape[1]), wide)
+    grad[...] = jnp.concatenate([turned, gains, pad], axis=0).T
+    scatter_slots(grad, keep_out, send_out, slice(None))
 
 
 def pair_kernel(keep, got, *outs):
@@ -676,15 +672,14 @@
         out[...] = (keep[k].astype(wide) + got[k].astype(wide)).astype(low)
 
 
-def total_kernel(a, b, c, d, out):
-    out[...] = (a[...].astype(wide) + b[...].astype(wide) + c[...].astype(wide) + d[...].astype(wide)).astype(low)
-
-
-def scatter_over(keep, send):
+def add(*parts):
+    return sum(part.astype(wide) for part in parts).astype(low)
+
+
+def scatter_over(keep, got):
     shape = keep.shape[1:]
-    parts = pl.pallas_call(pair_kernel, out_shape=shapes(*[(shape, low)] * keep.shape[0]))(keep, swap_fsdp(send, 1))
-    found = [parts[0]] + [swap_fsdp(parts[k], 2 * k) for k in range(1, keep.shape[0])]
-    return pl.pallas_call(total_kernel, out_shape=jax.ShapeDtypeStruct(shape, low))(*found)
+    parts = pl.pallas_call(pair_kernel, out_shape=shapes(*[(shape, low)] * keep.shape[0]))(keep, got)
+    return add(parts[0], *[swap_fsdp(parts[k], 2 * k) for k in range(1, keep.shape[0])])
 
 
 def finish_mlp_kernel(own, far, up_out, down_out):
@@ -708,8 +703,9 @@
     k_out[...] = woven_heads(even[:, cols : 2 * cols], odd[:, cols : 2 * cols])
     v_out[...] = even[:, 2 * cols : 3 * cols]
     c, d = own_proj[...].astype(wide), far_proj[...].astype(wide)
-    o_out[...] = woven_heads(jnp.where(rank == 0, c, d), jnp.where(rank == 0, d, c))
-    both = a[:, 512:640] + b[:, 512:640]
+    even, odd = jnp.where(rank == 0, c, d), jnp.where(rank == 0, d, c)
+    o_out[...] = woven_heads(even[:, :cols], odd[:, :cols])
+    both = c[:, 128:256] + d[:, 128:256]
     gains = jnp.concatenate([both, jnp.zeros((128 - rows, 128), wide)], axis=0).T
     for i, out in enumerate((g0, g1, g2, g3)):
         out[...] = gains[64 + i : 65 + i, :rows]
@@ -756,14 +752,6 @@
     span = d_first.shape[2]
     out[:, :span] = jnp.where(side == 0, d_first[2], d_first[3]).astype(low)
     out[:, span:] = jnp.where(side == 0, d_first[3], d_first[2]).astype(low)
-
-
-def sum_kernel(keep, got, out):
-    out[...] = (keep[1].astype(wide) + got[1].astype(wide)).astype(low)
-
-
-def close_kernel(keep, got, far, out):
-    out[...] = (keep[0].astype(wide) + got[0].astype(wide) + far[...].astype(wide)).astype(low)
 
 
 def local_split(
@@ -798,28 +786,25 @@
     def whole_spec(*shape):
         return pl.BlockSpec(shape, lambda q: (0,) * len(shape))
 
-    def own_quarter(block):
-        return lax.dynamic_slice_in_dim(block, side * span, span)
-
     hidden = hidden_in.reshape(rows, width)
     cot = cotangent.reshape(rows, width)
     first = first_values.reshape(rows, cols).T
 
-    across = swap_ctx(own_quarter(hidden))
+    own_pair = jnp.stack([lax.dynamic_slice_in_dim(block, side * span, span) for block in (hidden, cot)])
     gains_in = [g.reshape(1, shard) for g in (gain_attn, shift_attn, gain_mlp, shift_mlp)]
     attn_shard = pl.pallas_call(pack_attn_kernel, out_shape=jax.ShapeDtypeStruct((shard, 640), low))(
         w_query, w_key, w_value, *gains_in
     )
-    attn_blocks = gather_blocks(attn_shard)
-    across2 = swap_tp(across)
+    pair = swap_ctx(after(own_pair, attn_shard))
+    near = gather_columns(attn_shard)
+    attn_blocks = gather_pairs(near)
+    w_late = after((w_out, w_up, w_down), attn_shard)
+    late_shard = pl.pallas_call(
+        pack_late_kernel, out_shape=jax.ShapeDtypeStruct((shard, 2 * cols + 2 * units), low)
+    )(*w_late)
+    late_near = gather_columns(late_shard)
     first_far = lax.ppermute(first, "ctx", [(0, 1)])
-    up_shard, down_shard = pl.pallas_call(
-        pack_late_kernel, out_shape=shapes(((shard, 2 * cols + units), low), ((shard, units), low))
-    )(w_out, w_up, w_down)
-    up_blocks = gather_blocks(up_shard)
-    cot_across = swap_ctx(own_quarter(cot))
-    cot_across2 = swap_tp(cot_across)
-    down_blocks = gather_blocks(down_shard)
+    pair2 = swap_tp(after(pair, *attn_blocks))
 
     x4, h_one, w_qkv, gains, qkv, mix, low_mix, lse = pl.pallas_call(
         attn_kernel,
@@ -829,18 +814,17 @@
             ((4, 3 * cols, span), low), ((4, cols, span), wide), ((4, cols, span), low), ((4, 8, span), wide),
         ),
         scratch_shapes=[pltpu.VMEM((4, span, HEAD_DIM), low)],
-    )(span_table, hidden, across, across2, *attn_blocks, first, first_far)
-
+    )(span_table, hidden, pair, pair2, *attn_blocks, first, first_far)
+
+    mix_far = swap_ctx(low_mix)
     mix_side = swap_tp(low_mix)
-    mix_far = swap_ctx(low_mix)
-    wo_half, wu = pl.pallas_call(place_up_kernel, out_shape=shapes(((width, 2 * cols), low), ((width, units), low)))(
-        *up_blocks
-    )
+    late_blocks = gather_pairs([late_near[0]] + [after(block, lse) for block in late_near[1:]])
+    wo_half, wu, wd, cot4 = pl.pallas_call(
+        place_late_kernel,
+        out_shape=shapes(((width, 2 * cols), low), ((width, units), low), ((width, units), low), ((4, span, width), low)),
+    )(*late_blocks, cot, pair, pair2)
     wo_side = swap_tp(wo_half)
     mix_side_far = swap_tp(mix_far)
-    wd, cot4 = pl.pallas_call(
-        place_down_kernel, out_shape=shapes(((width, units), low), ((4, span, width), low))
-    )(*down_blocks, cot, cot_across, cot_across2)
 
     half_spec = pl.BlockSpec((1, span, width), lambda q: (q // 2, 0, 0))
     resid, act, h_two, d_upper, two_keep, two_send = pl.pallas_call(
@@ -874,8 +858,7 @@
     )(x4, low_mix, mix_far, mix_side, mix_side_far, wo_half, wo_side, wu, wd, gains, cot4)
 
     two_got = swap_tp(two_send)
-    tile = jax.ShapeDtypeStruct((span, width), low)
-    two_far = swap_ctx(pl.pallas_call(sum_kernel, out_shape=tile)(two_keep, two_got))
+    two_far = swap_ctx(add(two_keep[1], two_got[1]))
     mlp_keep, mlp_send, out_keep, out_send = pl.pallas_call(
         mlp_grad_kernel,
         out_shape=shapes(
@@ -886,54 +869,58 @@
     d_resid, branch, sums_two = pl.pallas_call(
         branch_kernel,
         out_shape=shapes(((span, width), wide), ((span, width), low), ((8, width), wide)),
-    )(two_keep, two_got, two_far, resid, cot4, gains)
+    )(two_keep, two_got, after(two_far, mlp_keep), resid, cot4, gains)
     branch_far = swap_ctx(branch)
     branch_side = swap_tp(branch)
     d_resid_beside = swap_tp(d_resid)
-    sums_two_side = swap_tp(sums_two.astype(low))
     branch_side_far = swap_tp(branch_far)
-    mlp_total = scatter_over(mlp_keep, mlp_send)
-
-    d_qkv, d_first, proj_keep, proj_send = pl.pallas_call(
+    branches = (branch, branch_side, branch_far, branch_side_far)
+
+    flat = jax.ShapeDtypeStruct((rows * width // 128, 128), wide)
+    out_got = swap_tp(out_send)
+    out_half = add(out_keep[1], out_got[1])
+    out_far = swap_ctx(out_half)
+    out_sum = add(out_keep[0], out_got[0], out_far)
+    out_rows = pl.pallas_call(out_kernel, out_shape=flat)(resid, out_sum, swap_tp(out_sum))
+    mlp_total = scatter_over(mlp_keep, swap_fsdp(mlp_send, 1))
+
+    d_qkv, d_first = pl.pallas_call(
         attn_back_kernel,
-        in_specs=[smem] + [vmem] * 9,
-        out_shape=shapes(
-            ((4, 3 * cols, span), low), ((4, cols, span), wide), ((pairs, shard, cols), low), ((pairs, shard, cols), low)
-        ),
+        in_specs=[smem] + [vmem] * 8,
+        out_shape=shapes(((4, 3 * cols, span), low), ((4, cols, span), wide)),
         scratch_shapes=[
             pltpu.VMEM((4, cols, span), low),
             pltpu.VMEM((4, span, HEAD_DIM), low),
             pltpu.VMEM((4, span, HEAD_DIM), low),
             pltpu.VMEM((4, HEAD_DIM, span), wide),
-            pltpu.VMEM((width, cols), wide),
         ],
-    )(span_table, branch, branch_side, branch_far, branch_side_far, wo_half, qkv, mix, lse, low_mix)
-
-    one_keep, one_send, sums_one = pl.pallas_call(
+    )(span_table, *branches, after(wo_half, out_half), qkv, mix, lse)
+
+    last_keep, last_send = pl.pallas_call(
+        attn_grad_kernel,
+        out_shape=shapes(((pairs, shard, 3 * cols), low), ((pairs, shard, 3 * cols), low)),
+        scratch_shapes=[pltpu.VMEM((width, 3 * cols), wide)],
+    )(d_qkv, h_one)
+    one_keep, one_send, sums = pl.pallas_call(
         d_one_kernel,
         grid=(4,),
-        in_specs=[quarter_spec(span, s=3 * cols), whole_spec(width, 640), quarter_spec(width)],
+        in_specs=[quarter_spec(span, s=3 * cols), whole_spec(width, 640), quarter_spec(width), whole_spec(8, width)],
         out_specs=[half_spec, half_spec, whole_spec(8, width)],
         out_shape=shapes(((2, span, width), low), ((2, span, width), low), ((8, width), wide)),
-    )(d_qkv, w_qkv, x4)
-    sums_one_side = swap_tp(sums_one.astype(low))
+    )(after(d_qkv, last_send), w_qkv, x4, sums_two)
     one_got = swap_tp(one_send)
-    one_far = swap_ctx(pl.pallas_call(sum_kernel, out_shape=tile)(one_keep, one_got))
-    last_keep, last_send = pl.pallas_call(
-        attn_grad_kernel,
-        out_shape=shapes(((pairs, shard, 640), low), ((pairs, shard, 640), low)),
-        scratch_shapes=[pltpu.VMEM((width, 640), wide)],
-    )(d_qkv, h_one, sums_one, sums_two, sums_one_side, sums_two_side)
-    proj_total = scatter_over(proj_keep, proj_send)
-    last_total = scatter_over(last_keep, last_send)
-
-    out_got = swap_tp(out_send)
-    out_far = swap_ctx(pl.pallas_call(sum_kernel, out_shape=tile)(out_keep, out_got))
-    out_sum = pl.pallas_call(close_kernel, out_shape=tile)(out_keep, out_got, out_far)
-    flat = jax.ShapeDtypeStruct((rows * width // 128, 128), wide)
-    out_rows = pl.pallas_call(out_kernel, out_shape=flat)(resid, out_sum, swap_tp(out_sum))
-
-    one_sum = pl.pallas_call(close_kernel, out_shape=tile)(one_keep, one_got, one_far)
+    sums_side = swap_tp(sums.astype(low))
+    one_far = swap_ctx(add(one_keep[1], one_got[1]))
+    last_got = swap_fsdp(last_send, 1)
+    last_total = scatter_over(last_keep, last_got)
+    proj_keep, proj_send = pl.pallas_call(
+        proj_grad_kernel,
+        out_shape=shapes(((pairs, shard, 256), low), ((pairs, shard, 256), low)),
+        scratch_shapes=[pltpu.VMEM((width, 256), wide)],
+    )(after(low_mix, last_got), *branches, sums, sums_side)
+    proj_total = scatter_over(proj_keep, swap_fsdp(proj_send, 1))
+
+    one_sum = add(one_keep[0], one_got[0], one_far)
     d_input = pl.pallas_call(input_grad_kernel, out_shape=flat)(
         x4, one_sum, swap_tp(one_sum), d_resid, d_resid_beside, gains
     )

time: 260 us -> 249 us (0.958)
  Pallas kernels: 109 us -> 94.1 us
  waiting for transfers between devices: 72.2 us -> 80.8 us
  other arithmetic: 0.01 us -> 8.33 us
  starting transfers between devices: 61.2 us -> 53.5 us
  local copies, waits for them, and re-layouts: 15.1 us -> 10.5 us
    pallas_call x13 -> x5, Pallas kernels: 41.6 us -> 26.2 us  [the longest x1 11.8 us: local_split(): pl.pallas_call(attn_back_kernel, in_specs=[smem] + [vmem] * 8, out_shape=...]
    convert_element_type x2 -> x9, other arithmetic: 0.01 us -> 8.25 us  [the longest x8 7.51 us: add(): return sum((part.astype(wide) for part in parts)).astype(low)]
    ppermute x33 -> x26, starting transfers between devices: 43 us -> 37.2 us  [swap_fsdp(): return lax.ppermute(value, 'fsdp', [(i, i ^ flip) for i in range(count)])]
    unnamed x118 -> x96, local copies, waits for them, and re-layouts: 13.9 us -> 9.3 us
    ppermute x1, waiting for transfers between devices: 0.01 us -> 3.65 us  [local_split(): first_far = lax.ppermute(first, 'ctx', [(0, 1)])]
    ppermute x10 -> x9, waiting for transfers between devices: 10.5 us -> 13.4 us  [swap_ctx(): return lax.ppermute(value, 'ctx', [(0, 1), (1, 0)])]
    ppermute x10 -> x9, starting transfers between devices: 12.8 us -> 10.5 us  [swap_ctx(): return lax.ppermute(value, 'ctx', [(0, 1), (1, 0)])]
    ppermute x33 -> x26, waiting for transfers between devices: 56.6 us -> 58.1 us  [swap_fsdp(): return lax.ppermute(value, 'fsdp', [(i, i ^ flip) for i in range(count)])]
  transfers between devices with their start and end apart: 60 -> 50, of which waited for: 23 -> 20; matrix products, arithmetic and copies ran while one was open for 0% -> 3% of each run, Pallas kernels for 33% -> 30%
where the time goes in v2:
time: 249 us; the launch traced here: 248 us
  Pallas kernels  94.1 us (38%)
  waiting for transfers between devices  80.8 us (32%)
  starting transfers between devices  53.5 us (21%)
  local copies, waits for them, and re-layouts  10.5 us (4%)
  other arithmetic  8.33 us (3%)
    ppermute x26, waiting for transfers between devices, swap_fsdp(): return lax.ppermute(value, 'fsdp', [(i, i ^ flip) for i in range(count)])  58.1 us
    ppermute x26, starting transfers between devices, swap_fsdp(): return lax.ppermute(value, 'fsdp', [(i, i ^ flip) for i in range(count)])  37.2 us
    pallas_call x1, Pallas kernels, local_split(): pl.pallas_call(mlp_kernel, grid=(4,), in_specs=[quarter_spec(width), quar...  13.9 us
    ppermute x9, waiting for transfers between devices, swap_ctx(): return lax.ppermute(value, 'ctx', [(0, 1), (1, 0)])  13.4 us
    pallas_call x1, Pallas kernels, local_split(): pl.pallas_call(attn_back_kernel, in_specs=[smem] + [vmem] * 8, out_shape=...  11.8 us
    pallas_call x1, Pallas kernels, local_split(): pl.pallas_call(attn_kernel, in_specs=[smem] + [vmem] * 13, out_shape=shap...  11.6 us
    ppermute x9, starting transfers between devices, swap_ctx(): return lax.ppermute(value, 'ctx', [(0, 1), (1, 0)])  10.5 us
    unnamed x96, local copies, waits for them, and re-layouts  9.3 us
  transfers between devices with their start and end apart: 50, of which 20 were waited for; matrix products, arithmetic and copies ran while one was open for 3% of the time, Pallas kernels for 30%

profile of v2, /device:TPU:0, one launch (start us, length us, event | category | flops | bytes accessed | tf_op | source)
XLA Modules:
  0.0 248.4 jit_solution(13090896975311298596)
XLA Ops:
  0.6 1.2 dynamic-slice_bitcast_fusion
  1.9 1.8 shard_map.237.b0
  3.7 3.0 %collective-permute-start = (bf16[2,256,768]{2,1,0:T(8,128)(2,1)S(1)}, bf16[2,256,768]{2,1,0:T(8,128)(2,1)S(1)}, u32[]{:S(2)}, u32[]{:S(2)}) collective-permute-start(bf16[2,256,768]{2,1,0:T(8,128)(2,1)S(1)} %pad_maximum_fusion), channel_id=1, source_target_pairs={{0,2},{2,0},{1,3},{3,1},{4,6},{6,4},{5,7},{7,5},{8,10},{10,8},{9,1... | collective-permute-start | bytes 2359304 | tf_op jit(solution)/shard_map/ppermute | solution.py:345
  6.7 3.6 %collective-permute-start.6 = (bf16[96,640]{1,0:T(8,128)(2,1)}, bf16[96,640]{1,0:T(8,128)(2,1)S(1)}, u32[]{:S(2)}, u32[]{:S(2)}) collective-permute-start(bf16[96,640]{1,0:T(8,128)(2,1)} %shard_map.237.b0), channel_id=1, source_target_pairs={{0,24},{4,28},{8,16},{12,20},{16,8},{20,12},{24,0},{28,4},{1,25},{... | collective-permute-start | bytes 368648 | tf_op jit(solution)/shard_map/ppermute | solution.py:337
  11.1 1.5 collective-permute-start.1
  12.6 2.4 collective-permute-done.6.b6
  15.0 1.5 collective-permute-start.7
  16.5 4.1 %collective-permute-done.4.b4 = bf16[96,640]{1,0:T(8,128)(2,1)S(1)} collective-permute-done((bf16[96,640]{1,0:T(8,128)(2,1)}, bf16[96,640]{1,0:T(8,128)(2,1)S(1)}, u32[]{:S(2)}, u32[]{:S(2)}) %collective-permute-start.4) | collective-permute-done | bytes 122912 | tf_op jit(solution)/shard_map/ppermute | solution.py:337
  20.7 1.5 collective-permute-start.5
  22.7 3.7 %collective-permute-done.5.b5 = bf16[96,640]{1,0:T(8,128)(2,1)S(1)} collective-permute-done((bf16[96,640]{1,0:T(8,128)(2,1)S(1)}, bf16[96,640]{1,0:T(8,128)(2,1)S(1)}, u32[]{:S(2)}, u32[]{:S(2)}) %collective-permute-start.5) | collective-permute-done | bytes 122912 | tf_op jit(solution)/shard_map/ppermute | solution.py:337
  26.4 1.3 collective-permute-done.3.b3
  28.3 2.3 shard_map.239.b0
  30.6 1.8 collective-permute-start.18
  32.5 2.5 collective-permute-start.14
  35.0 2.4 collective-permute-start.9
  37.4 3.6 %collective-permute-done.9.first_far = bf16[192,512]{1,0:T(8,128)(2,1)S(1)} collective-permute-done((bf16[192,512]{1,0:T(8,128)(2,1)S(1)}, bf16[192,512]{1,0:T(8,128)(2,1)S(1)}, u32[]{:S(2)}, u32[]{:S(2)}) %collective-permute-start.9) | collective-permute-done | bytes 196640 | tf_op jit(solution)/shard_map/ppermute | solution.py:806
  41.1 1.5 collective-permute-start.13
  43.5 11.6 %shard_map.238 = (bf16[4,256,768]{2,1,0:T(8,128)(2,1)}, bf16[4,256,768]{2,1,0:T(8,128)(2,1)}, bf16[768,640]{1,0:T(8,128)(2,1)}, f32[8,768]{1,0:T(8,128)}, bf16[4...) custom-call(s32[2,2]{1,0:T(2,128)} %table.3, ...), custom_call_target="tpu_custom_call" | custom-call | tf_op jit(solution)/shard_map/pallas_call | solution.py:809
  55.1 10.0 %collective-permute-done.16.b4 = bf16[96,1920]{1,0:T(8,128)(2,1)S(1)} collective-permute-done((bf16[96,1920]{1,0:T(8,128)(2,1)}, bf16[96,1920]{1,0:T(8,128)(2,1)S(1)}, u32[]{:S(2)}, u32[]{:S(2)}) %collective-permute-start.16) | collective-permute-done | bytes 368672 | tf_op jit(solution)/shard_map/ppermute | solution.py:337
  65.2 1.6 collective-permute-start.15
  67.2 1.5 collective-permute-start.19
  69.2 7.4 %collective-permute-done.15.b3 = bf16[96,1920]{1,0:T(8,128)(2,1)S(1)} collective-permute-done((bf16[96,1920]{1,0:T(8,128)(2,1)S(1)}, bf16[96,1920]{1,0:T(8,128)(2,1)S(1)}, u32[]{:S(2)}, u32[]{:S(2)}) %collective-permute-start.15) | collective-permute-done | bytes 368672 | tf_op jit(solution)/shard_map/ppermute | solution.py:337
  76.7 7.9 %collective-permute-done.17.b5 = bf16[96,1920]{1,0:T(8,128)(2,1)S(1)} collective-permute-done((bf16[96,1920]{1,0:T(8,128)(2,1)S(1)}, bf16[96,1920]{1,0:T(8,128)(2,1)S(1)}, u32[]{:S(2)}, u32[]{:S(2)}) %collective-permute-start.17) | collective-permute-done | bytes 368672 | tf_op jit(solution)/shard_map/ppermute | solution.py:337
  84.6 6.3 %collective-permute-done.19.b7 = bf16[96,1920]{1,0:T(8,128)(2,1)S(1)} collective-permute-done((bf16[96,1920]{1,0:T(8,128)(2,1)S(1)}, bf16[96,1920]{1,0:T(8,128)(2,1)S(1)}, u32[]{:S(2)}, u32[]{:S(2)}) %collective-permute-start.19) | collective-permute-done | bytes 368672 | tf_op jit(solution)/shard_map/ppermute | solution.py:337
  91.6 4.9 %shard_map.240 = (bf16[768,384]{1,0:T(8,128)(2,1)}, bf16[768,768]{1,0:T(8,128)(2,1)}, bf16[768,768]{1,0:T(8,128)(2,1)}, bf16[4,256,768]{2,1,0:T(8,128)(2,1)}) custom-call(bf16[96,1920]{1,0:T(8,128)(2,1)} %shard_map.239.b0, bf16[96,1920]{1,0:T(8,128)(2,1)} %copy-done.25, bf16[96,1920]{1,0:T(8,128)(2,1)} %copy-done.24, bf16[96,1920]{1,0:T(8,128)(2,1)} %copy-done.26, ...), custom_call_target="tpu_custom_call" | custom-call | tf_op jit(solution)/shard_map/pallas_call | solution.py:822
  97.1 2.2 collective-permute-done.11.mix2
  100.8 13.9 %shard_map.241 = (f32[2,256,768]{2,1,0:T(8,128)}, bf16[4,256,768]{2,1,0:T(8,128)(2,1)}, bf16[4,256,768]{2,1,0:T(8,128)(2,1)}, bf16[4,256,768]{2,1,0:T(8,128)(2,1...) custom-call(bf16[4,256,768]{2,1,0:T(8,128)(2,1)} %get-tuple-element.83.x, ...), custom_call_target="tpu_custom_call" | custom-call | tf_op jit(solution)/shard_map/pallas_call | solution.py:830
  114.9 2.4 collective-permute-done.24.got
  117.2 1.3 fusion.3
  119.1 8.9 %shard_map.242 = (bf16[4,96,1536]{2,1,0:T(8,128)(2,1)}, bf16[4,96,1536]{2,1,0:T(8,128)(2,1)}, bf16[2,256,768]{2,1,0:T(8,128)(2,1)}, bf16[2,256,768]{2,1,0:T(8,128)(2,1)}) custom-call(bf16[4,256,768]{2,1,0:T(8,128)(2,1)} %get-tuple-element.96.cot, bf16[4,256,768]{2,1,0:T(8,128)(2,1)} %get-tuple-element.98.act, bf16[4,256,768]{2,1,0:T(8,128)(2,1)} %get-tuple-element.99.h_two, ...), custom_call_target="tpu_custom_call" | custom-call | tf_op jit(solution)/shard_map/pallas_call | solution.py:862
  128.1 1.8 collective-permute-done.25.far
  130.5 4.3 %shard_map.244 = (f32[256,768]{1,0:T(8,128)}, bf16[256,768]{1,0:T(8,128)(2,1)}, f32[8,768]{1,0:T(8,128)}) custom-call(bf16[2,256,768]{2,1,0:T(8,128)(2,1)} %get-tuple-element.103.keep, bf16[2,256,768]{2,1,0:T(8,128)(2,1)} %copy-done.2, bf16[256,768]{1,0:T(8,128)(2,1)} %copy-done.19, f32[2,256,768]{2,1,0:T(8,128)} %get-tuple-element.97.resid, ...), custom_call_target="tpu_custom_call" | custom-call | tf_op jit(solution)/shard_map/pallas_call | solution.py:869
  135.3 1.5 collective-permute-start.45
  136.8 8.5 %collective-permute-done.27.br2 = bf16[256,768]{1,0:T(8,128)(2,1)S(1)} collective-permute-done((bf16[256,768]{1,0:T(8,128)(2,1)}, bf16[256,768]{1,0:T(8,128)(2,1)S(1)}, u32[]{:S(2)}, u32[]{:S(2)}) %collective-permute-start.27) | collective-permute-done | bytes 393248 | tf_op jit(solution)/shard_map/ppermute | solution.py:345
  145.3 1.2 fusion.2
  147.8 11.8 %shard_map.245 = (bf16[4,576,256]{2,1,0:T(8,128)(2,1)}, f32[4,192,256]{2,1,0:T(8,128)}) custom-call(s32[2,2]{1,0:T(2,128)} %table.3, bf16[256,768]{1,0:T(8,128)(2,1)} %get-tuple-element.107.br0, bf16[256,768]{1,0:T(8,128)(2,1)} %copy-done.5, bf16[256,768]{1,0:T(8,128)(2,1)} %copy-done.4, bf16[256,768]{1,0:T(8,128)(2,1)} %copy-done.6, ...), custom_call_target="tpu_custom_call" | custom-call | tf_op jit(solution)/shard_map/pallas_call | solution.py:887
  159.6 4.4 %shard_map.246 = (bf16[4,96,576]{2,1,0:T(8,128)(2,1)}, bf16[4,96,576]{2,1,0:T(8,128)(2,1)}) custom-call(bf16[4,576,256]{2,1,0:T(8,128)(2,1)} %get-tuple-element.114.d_qkv, bf16[4,256,768]{2,1,0:T(8,128)(2,1)} %get-tuple-element.112.h_one), custom_call_target="tpu_custom_call" | custom-call | tf_op jit(solution)/shard_map/pallas_call | solution.py:899
  164.0 6.0 %shard_map.247 = (bf16[2,256,768]{2,1,0:T(8,128)(2,1)}, bf16[2,256,768]{2,1,0:T(8,128)(2,1)}, f32[8,768]{1,0:T(8,128)}) custom-call(bf16[4,576,256]{2,1,0:T(8,128)(2,1)} %get-tuple-element.114.d_qkv, bf16[768,640]{1,0:T(8,128)(2,1)} %get-tuple-element.115.w, bf16[4,256,768]{2,1,0:T(8,128)(2,1)} %get-tuple-element.83.x, f32[8,768]{1,0:T(8,128)} %get-tuple-element.116.sums_two), custom_call_target="tpu_custom_call" | custom-call | tf_op jit(solution)/shard_map/pallas_call | solution.py:904
  170.2 1.5 collective-permute-start.34
  173.7 2.7 %shard_map.255 = (bf16[96,1536]{1,0:T(8,128)(2,1)}, bf16[96,1536]{1,0:T(8,128)(2,1)}, bf16[96,1536]{1,0:T(8,128)(2,1)}, bf16[96,1536]{1,0:T(8,128)(2,1)}) custom-call(bf16[4,96,1536]{2,1,0:T(8,128)(2,1)} %get-tuple-element.105.keep, bf16[4,96,1536]{2,1,0:T(8,128)(2,1)} %copy-done.9), custom_call_target="tpu_custom_call" | custom-call | tf_op jit(solution)/shard_map/pallas_call | solution.py:681
  176.4 2.5 %collective-permute-start.47 = (bf16[96,1536]{1,0:T(8,128)(2,1)}, bf16[96,1536]{1,0:T(8,128)(2,1)}, u32[]{:S(2)}, u32[]{:S(2)}) collective-permute-start(bf16[96,1536]{1,0:T(8,128)(2,1)} %get-tuple-element.141), channel_id=1, source_target_pairs={{0,16},{4,20},{8,24},{12,28},{16,0},{20,4},{24,8},{28,12},{1,17},{... | collective-permute-start | bytes 884744 | tf_op jit(solution)/shard_map/ppermute | solution.py:337
  179.6 3.1 %collective-permute-done.22 = bf16[256,768]{1,0:T(8,128)(2,1)S(1)} collective-permute-done((bf16[256,768]{1,0:T(8,128)(2,1)S(1)}, bf16[256,768]{1,0:T(8,128)(2,1)S(1)}, u32[]{:S(2)}, u32[]{:S(2)}) %collective-permute-start.22) | collective-permute-done | bytes 393248 | tf_op jit(solution)/shard_map/ppermute | solution.py:345
  183.5 2.0 collective-permute-start.48
  185.5 1.3 fusion.1.own
  187.4 2.9 %shard_map.252 = (bf16[4,96,256]{2,1,0:T(8,128)(2,1)}, bf16[4,96,256]{2,1,0:T(8,128)(2,1)}) custom-call(bf16[4,192,256]{2,1,0:T(8,128)(2,1)} %get-tuple-element.126.mix0.low_mix, bf16[256,768]{1,0:T(8,128)(2,1)} %get-tuple-element.107.br0, bf16[256,768]{1,0:T(8,128)(2,1)} %copy-done.5, bf16[256,768]{1,0:T(8,128)(2,1)} %copy-done.4, ...), custom_call_target="tpu_custom_call" | custom-call | tf_op jit(solution)/shard_map/pallas_call | solution.py:916
  191.6 8.5 %collective-permute-done.47 = bf16[96,1536]{1,0:T(8,128)(2,1)} collective-permute-done((bf16[96,1536]{1,0:T(8,128)(2,1)}, bf16[96,1536]{1,0:T(8,128)(2,1)}, u32[]{:S(2)}, u32[]{:S(2)}) %collective-permute-start.47) | collective-permute-done | bytes 294944 | tf_op jit(solution)/shard_map/ppermute | solution.py:337
  201.1 1.4 add_convert_fusion.3.own
  202.5 1.9 shard_map.249
  204.5 2.0 shard_map.251
  206.4 4.7 %collective-permute-start.35 = (bf16[96,576]{1,0:T(8,128)(2,1)}, bf16[96,576]{1,0:T(8,128)(2,1)}, u32[]{:S(2)}, u32[]{:S(2)}) collective-permute-start(bf16[96,576]{1,0:T(8,128)(2,1)} %get-tuple-element.123), channel_id=1, source_target_pairs={{0,8},{4,12},{8,0},{12,4},{16,24},{20,28},{24,16},{28,20},{1,9},{5... | collective-permute-start | bytes 331784 | tf_op jit(solution)/shard_map/ppermute | solution.py:337
  211.8 1.7 shard_map.253
  213.5 1.9 collective-permute-start.37
  216.5 1.1 fusion.own
  217.7 1.1 collective-permute-start.49
  218.8 4.5 %collective-permute-done.36 = bf16[96,576]{1,0:T(8,128)(2,1)} collective-permute-done((bf16[96,576]{1,0:T(8,128)(2,1)}, bf16[96,576]{1,0:T(8,128)(2,1)}, u32[]{:S(2)}, u32[]{:S(2)}) %collective-permute-start.36) | collective-permute-done | bytes 110624 | tf_op jit(solution)/shard_map/ppermute | solution.py:337
  223.3 2.0 collective-permute-start.43
  226.3 1.9 collective-permute-done.42
  228.2 1.3 collective-permute-start.33
  229.5 2.7 %collective-permute-start.38 = (bf16[96,576]{1,0:T(8,128)(2,1)S(1)}, bf16[96,576]{1,0:T(8,128)(2,1)S(1)}, u32[]{:S(2)}, u32[]{:S(2)}) collective-permute-start(bf16[96,576]{1,0:T(8,128)(2,1)S(1)} %add_convert_fusion.4.own), channel_id=1, source_target_pairs={{0,2},{2,0},{1,3},{3,1},{4,6},{6,4},{5,7},{7,5},{8,10},{10,8},{9,1... | collective-permute-start | bytes 331784 | tf_op jit(solution)/shard_map/ppermute | solution.py:345
  232.4 2.9 %shard_map.243 = f32[3072,128]{1,0:T(8,128)} custom-call(f32[2,256,768]{2,1,0:T(8,128)} %get-tuple-element.97.resid, bf16[256,768]{1,0:T(8,128)(2,1)} %copy-done.7, bf16[256,768]{1,0:T(8,128)(2,1)} %collective-permute-done.23.beside), custom_call_target="tpu_custom_call" | custom-call | tf_op jit(solution)/shard_map/pallas_call | solution.py:884
  235.3 2.1 shard_map.256
  238.3 1.9 shard_map.250
  241.5 1.9 shard_map.254
  244.1 4.3 %shard_map.248 = f32[3072,128]{1,0:T(8,128)} custom-call(bf16[4,256,768]{2,1,0:T(8,128)(2,1)} %get-tuple-element.83.x, bf16[256,768]{1,0:T(8,128)(2,1)} %copy-done.8, bf16[256,768]{1,0:T(8,128)(2,1)} %copy-done.21, f32[256,768]{1,0:T(8,128)} %get-tuple-element.119.d_own, f32[256,768]{1,0:T(8,128)} %collective-permute-done.32.d_beside, ...), custom_call_target="tpu_custom_call" | custom-call | tf_op jit(solution)/shard_map/pallas_call | solution.py:924
  (163 shorter events, 22.5 us)
Async XLA Ops:
  1.8 33.2 %copy-start.30 = (bf16[512,1,192]{0,2,1:T(8,128)(2,1)S(1)}, bf16[512,1,192]{0,2,1:T(8,128)(2,1)}, u32[]{:S(2)}) copy-start(bf16[512,1,192]{0,2,1:T(8,128)(2,1)} %param.15) | copy-start | bytes 589828
  3.7 23.9 %collective-permute-start = (bf16[2,256,768]{2,1,0:T(8,128)(2,1)S(1)}, bf16[2,256,768]{2,1,0:T(8,128)(2,1)S(1)}, u32[]{:S(2)}, u32[]{:S(2)}) collective-permute-start(bf16[2,256,768]{2,1,0:T(8,128)(2,1)S(1)} %pad_maximum_fusion), channel_id=1, source_target_pairs={{0,2},{2,0},{1,3},{3,1},{4,6},{6,4},{5,7},{7,5},{8,10},{10,8},{9,1... | collective-permute-start | bytes 2359304 | tf_op jit(solution)/shard_map/ppermute | solution.py:345
  6.7 8.3 %collective-permute-start.6 = (bf16[96,640]{1,0:T(8,128)(2,1)}, bf16[96,640]{1,0:T(8,128)(2,1)S(1)}, u32[]{:S(2)}, u32[]{:S(2)}) collective-permute-start(bf16[96,640]{1,0:T(8,128)(2,1)} %shard_map.237.b0), channel_id=1, source_target_pairs={{0,24},{4,28},{8,16},{12,20},{16,8},{20,12},{24,0},{28,4},{1,25},{... | collective-permute-start | bytes 368648 | tf_op jit(solution)/shard_map/ppermute | solution.py:337
  10.3 10.3 %collective-permute-start.4 = (bf16[96,640]{1,0:T(8,128)(2,1)}, bf16[96,640]{1,0:T(8,128)(2,1)S(1)}, u32[]{:S(2)}, u32[]{:S(2)}) collective-permute-start(bf16[96,640]{1,0:T(8,128)(2,1)} %shard_map.237.b0), channel_id=1, source_target_pairs={{0,16},{4,20},{8,24},{12,28},{16,0},{20,4},{24,8},{28,12},{1,17},{... | collective-permute-start | bytes 368648 | tf_op jit(solution)/shard_map/ppermute | solution.py:337
  10.3 11.8 %collective-permute-start.2 = (bf16[96,640]{1,0:T(8,128)(2,1)}, bf16[96,640]{1,0:T(8,128)(2,1)S(1)}, u32[]{:S(2)}, u32[]{:S(2)}) collective-permute-start(bf16[96,640]{1,0:T(8,128)(2,1)} %shard_map.237.b0), channel_id=1, source_target_pairs={{0,8},{4,12},{8,0},{12,4},{16,24},{20,28},{24,16},{28,20},{1,9},{5... | collective-permute-start | bytes 368648 | tf_op jit(solution)/shard_map/ppermute | solution.py:337
  11.1 11.6 %collective-permute-start.1 = (bf16[96,640]{1,0:T(8,128)(2,1)}, bf16[96,640]{1,0:T(8,128)(2,1)S(1)}, u32[]{:S(2)}, u32[]{:S(2)}) collective-permute-start(bf16[96,640]{1,0:T(8,128)(2,1)} %shard_map.237.b0), channel_id=1, source_target_pairs={{0,4},{4,0},{8,12},{12,8},{16,20},{20,16},{24,28},{28,24},{1,5},{5... | collective-permute-start | bytes 368648 | tf_op jit(solution)/shard_map/ppermute | solution.py:337
  15.0 22.4 %copy-start.35 = (bf16[96,640]{1,0:T(8,128)(2,1)}, bf16[96,640]{1,0:T(8,128)(2,1)S(1)}, u32[]{:S(2)}) copy-start(bf16[96,640]{1,0:T(8,128)(2,1)S(1)} %collective-permute-done.6.b6) | copy-start | bytes 368644
  15.0 7.7 %collective-permute-start.7 = (bf16[96,640]{1,0:T(8,128)(2,1)S(1)}, bf16[96,640]{1,0:T(8,128)(2,1)S(1)}, u32[]{:S(2)}, u32[]{:S(2)}) collective-permute-start(bf16[96,640]{1,0:T(8,128)(2,1)S(1)} %collective-permute-done.6.b6), channel_id=1, source_target_pairs={{0,4},{4,0},{8,12},{12,8},{16,20},{20,16},{24,28},{28,24},{1,5},{5... | collective-permute-start | bytes 368648 | tf_op jit(solution)/shard_map/ppermute | solution.py:337
  20.6 16.8 %copy-start.36 = (bf16[96,640]{1,0:T(8,128)(2,1)}, bf16[96,640]{1,0:T(8,128)(2,1)S(1)}, u32[]{:S(2)}) copy-start(bf16[96,640]{1,0:T(8,128)(2,1)S(1)} %collective-permute-done.4.b4) | copy-start | bytes 368644
  20.7 5.7 %collective-permute-start.5 = (bf16[96,640]{1,0:T(8,128)(2,1)S(1)}, bf16[96,640]{1,0:T(8,128)(2,1)S(1)}, u32[]{:S(2)}, u32[]{:S(2)}) collective-permute-start(bf16[96,640]{1,0:T(8,128)(2,1)S(1)} %collective-permute-done.4.b4), channel_id=1, source_target_pairs={{0,4},{4,0},{8,12},{12,8},{16,20},{20,16},{24,28},{28,24},{1,5},{5... | collective-permute-start | bytes 368648 | tf_op jit(solution)/shard_map/ppermute | solution.py:337
  22.1 15.3 %copy-start.37 = (bf16[96,640]{1,0:T(8,128)(2,1)}, bf16[96,640]{1,0:T(8,128)(2,1)S(1)}, u32[]{:S(2)}) copy-start(bf16[96,640]{1,0:T(8,128)(2,1)S(1)} %collective-permute-done.2.b2) | copy-start | bytes 368644
  22.1 5.5 %collective-permute-start.3 = (bf16[96,640]{1,0:T(8,128)(2,1)S(1)}, bf16[96,640]{1,0:T(8,128)(2,1)S(1)}, u32[]{:S(2)}, u32[]{:S(2)}) collective-permute-start(bf16[96,640]{1,0:T(8,128)(2,1)S(1)} %collective-permute-done.2.b2), channel_id=1, source_target_pairs={{0,4},{4,0},{8,12},{12,8},{16,20},{20,16},{24,28},{28,24},{1,5},{5... | collective-permute-start | bytes 368648 | tf_op jit(solution)/shard_map/ppermute | solution.py:337
  28.3 14.3 %copy-start = (bf16[2,256,768]{2,1,0:T(8,128)(2,1)}, bf16[2,256,768]{2,1,0:T(8,128)(2,1)S(1)}, u32[]{:S(2)}) copy-start(bf16[2,256,768]{2,1,0:T(8,128)(2,1)S(1)} %collective-permute-done.pair) | copy-start | bytes 2359300
  28.3 14.3 %collective-permute-start.8 = (bf16[2,256,768]{2,1,0:T(8,128)(2,1)S(1)}, bf16[2,256,768]{2,1,0:T(8,128)(2,1)S(1)}, u32[]{:S(2)}, u32[]{:S(2)}) collective-permute-start(bf16[2,256,768]{2,1,0:T(8,128)(2,1)S(1)} %collective-permute-done.pair), channel_id=1, source_target_pairs={{0,1},{1,0},{2,3},{3,2},{4,5},{5,4},{6,7},{7,6},{8,9},{9,8},{10,11... | collective-permute-start | bytes 2359304 | tf_op jit(solution)/shard_map/ppermute | solution.py:341
  30.6 24.5 %collective-permute-start.18 = (bf16[96,1920]{1,0:T(8,128)(2,1)}, bf16[96,1920]{1,0:T(8,128)(2,1)S(1)}, u32[]{:S(2)}, u32[]{:S(2)}) collective-permute-start(bf16[96,1920]{1,0:T(8,128)(2,1)} %shard_map.239.b0), channel_id=1, source_target_pairs={{0,24},{4,28},{8,16},{12,20},{16,8},{20,12},{24,0},{28,4},{1,25},{... | collective-permute-start | bytes 1105928 | tf_op jit(solution)/shard_map/ppermute | solution.py:337
  32.4 32.7 %collective-permute-start.16 = (bf16[96,1920]{1,0:T(8,128)(2,1)}, bf16[96,1920]{1,0:T(8,128)(2,1)S(1)}, u32[]{:S(2)}, u32[]{:S(2)}) collective-permute-start(bf16[96,1920]{1,0:T(8,128)(2,1)} %shard_map.239.b0), channel_id=1, source_target_pairs={{0,16},{4,20},{8,24},{12,28},{16,0},{20,4},{24,8},{28,12},{1,17},{... | collective-permute-start | bytes 1105928 | tf_op jit(solution)/shard_map/ppermute | solution.py:337
  32.5 32.6 %collective-permute-start.14 = (bf16[96,1920]{1,0:T(8,128)(2,1)}, bf16[96,1920]{1,0:T(8,128)(2,1)S(1)}, u32[]{:S(2)}, u32[]{:S(2)}) collective-permute-start(bf16[96,1920]{1,0:T(8,128)(2,1)} %shard_map.239.b0), channel_id=1, source_target_pairs={{0,8},{4,12},{8,0},{12,4},{16,24},{20,28},{24,16},{28,20},{1,9},{5... | collective-permute-start | bytes 1105928 | tf_op jit(solution)/shard_map/ppermute | solution.py:337
  35.0 6.1 %collective-permute-start.9 = (bf16[192,512]{1,0:T(8,128)(2,1)S(1)}, bf16[192,512]{1,0:T(8,128)(2,1)S(1)}, u32[]{:S(2)}, u32[]{:S(2)}) collective-permute-start(bf16[192,512]{1,0:T(8,128)(2,1)S(1)} %bitcast.42), channel_id=1, source_target_pairs={{0,2},{1,3},{4,6},{5,7},{8,10},{9,11},{12,14},{13,15},{16,18},{17,... | collective-permute-start | bytes 589832 | tf_op jit(solution)/shard_map/ppermute | solution.py:806
  41.1 28.1 %collective-permute-start.13 = (bf16[96,1920]{1,0:T(8,128)(2,1)}, bf16[96,1920]{1,0:T(8,128)(2,1)S(1)}, u32[]{:S(2)}, u32[]{:S(2)}) collective-permute-start(bf16[96,1920]{1,0:T(8,128)(2,1)} %shard_map.239.b0), channel_id=1, source_target_pairs={{0,4},{4,0},{8,12},{12,8},{16,20},{20,16},{24,28},{28,24},{1,5},{5... | collective-permute-start | bytes 1105928 | tf_op jit(solution)/shard_map/ppermute | solution.py:337
  55.1 35.8 %copy-start.22 = (bf16[96,1920]{1,0:T(8,128)(2,1)}, bf16[96,1920]{1,0:T(8,128)(2,1)S(1)}, u32[]{:S(2)}) copy-start(bf16[96,1920]{1,0:T(8,128)(2,1)S(1)} %collective-permute-done.18.b6) | copy-start | bytes 1105924
  65.1 25.7 %copy-start.23 = (bf16[96,1920]{1,0:T(8,128)(2,1)}, bf16[96,1920]{1,0:T(8,128)(2,1)S(1)}, u32[]{:S(2)}) copy-start(bf16[96,1920]{1,0:T(8,128)(2,1)S(1)} %collective-permute-done.16.b4) | copy-start | bytes 1105924
  65.1 25.7 %copy-start.24 = (bf16[96,1920]{1,0:T(8,128)(2,1)}, bf16[96,1920]{1,0:T(8,128)(2,1)S(1)}, u32[]{:S(2)}) copy-start(bf16[96,1920]{1,0:T(8,128)(2,1)S(1)} %collective-permute-done.14.b2) | copy-start | bytes 1105924
  65.2 11.5 %collective-permute-start.15 = (bf16[96,1920]{1,0:T(8,128)(2,1)S(1)}, bf16[96,1920]{1,0:T(8,128)(2,1)S(1)}, u32[]{:S(2)}, u32[]{:S(2)}) collective-permute-start(bf16[96,1920]{1,0:T(8,128)(2,1)S(1)} %collective-permute-done.14.b2), channel_id=1, source_target_pairs={{0,4},{4,0},{8,12},{12,8},{16,20},{20,16},{24,28},{28,24},{1,5},{5... | collective-permute-start | bytes 1105928 | tf_op jit(solution)/shard_map/ppermute | solution.py:337
  66.7 17.9 %collective-permute-start.17 = (bf16[96,1920]{1,0:T(8,128)(2,1)S(1)}, bf16[96,1920]{1,0:T(8,128)(2,1)S(1)}, u32[]{:S(2)}, u32[]{:S(2)}) collective-permute-start(bf16[96,1920]{1,0:T(8,128)(2,1)S(1)} %collective-permute-done.16.b4), channel_id=1, source_target_pairs={{0,4},{4,0},{8,12},{12,8},{16,20},{20,16},{24,28},{28,24},{1,5},{5... | collective-permute-start | bytes 1105928 | tf_op jit(solution)/shard_map/ppermute | solution.py:337
  67.2 23.6 %collective-permute-start.19 = (bf16[96,1920]{1,0:T(8,128)(2,1)S(1)}, bf16[96,1920]{1,0:T(8,128)(2,1)S(1)}, u32[]{:S(2)}, u32[]{:S(2)}) collective-permute-start(bf16[96,1920]{1,0:T(8,128)(2,1)S(1)} %collective-permute-done.18.b6), channel_id=1, source_target_pairs={{0,4},{4,0},{8,12},{12,8},{16,20},{20,16},{24,28},{28,24},{1,5},{5... | collective-permute-start | bytes 1105928 | tf_op jit(solution)/shard_map/ppermute | solution.py:337
  68.7 28.3 %collective-permute-start.10 = (bf16[4,192,256]{2,1,0:T(8,128)(2,1)}, bf16[4,192,256]{2,1,0:T(8,128)(2,1)S(1)}, u32[]{:S(2)}, u32[]{:S(2)}) collective-permute-start(bf16[4,192,256]{2,1,0:T(8,128)(2,1)} %get-tuple-element.126.mix0.low_mix), channel_id=1, source_target_pairs={{0,2},{2,0},{1,3},{3,1},{4,6},{6,4},{5,7},{7,5},{8,10},{10,8},{9,1... | collective-permute-start | bytes 1179656 | tf_op jit(solution)/shard_map/ppermute | solution.py:345
  69.2 21.6 %copy-start.25 = (bf16[96,1920]{1,0:T(8,128)(2,1)}, bf16[96,1920]{1,0:T(8,128)(2,1)S(1)}, u32[]{:S(2)}) copy-start(bf16[96,1920]{1,0:T(8,128)(2,1)S(1)} %collective-permute-done.13.b1) | copy-start | bytes 1105924
  76.7 14.2 %copy-start.26 = (bf16[96,1920]{1,0:T(8,128)(2,1)}, bf16[96,1920]{1,0:T(8,128)(2,1)S(1)}, u32[]{:S(2)}) copy-start(bf16[96,1920]{1,0:T(8,128)(2,1)S(1)} %collective-permute-done.15.b3) | copy-start | bytes 1105924
  96.5 3.3 %collective-permute-start.20 = (bf16[768,384]{1,0:T(8,128)(2,1)}, bf16[768,384]{1,0:T(8,128)(2,1)S(1)}, u32[]{:S(2)}, u32[]{:S(2)}) collective-permute-start(bf16[768,384]{1,0:T(8,128)(2,1)} %get-tuple-element.108.wo_own.wo), channel_id=1, source_target_pairs={{0,1},{1,0},{2,3},{3,2},{4,5},{5,4},{6,7},{7,6},{8,9},{9,8},{10,11... | collective-permute-start | bytes 1769480 | tf_op jit(solution)/shard_map/ppermute | solution.py:341
  96.5 2.8 %collective-permute-start.11 = (bf16[4,192,256]{2,1,0:T(8,128)(2,1)S(1)}, bf16[4,192,256]{2,1,0:T(8,128)(2,1)S(1)}, u32[]{:S(2)}, u32[]{:S(2)}) collective-permute-start(bf16[4,192,256]{2,1,0:T(8,128)(2,1)S(1)} %copy-done.3), channel_id=1, source_target_pairs={{0,1},{1,0},{2,3},{3,2},{4,5},{5,4},{6,7},{7,6},{8,9},{9,8},{10,11... | collective-permute-start | bytes 1179656 | tf_op jit(solution)/shard_map/ppermute | solution.py:341
  97.0 2.8 %collective-permute-start.12 = (bf16[4,192,256]{2,1,0:T(8,128)(2,1)S(1)}, bf16[4,192,256]{2,1,0:T(8,128)(2,1)S(1)}, u32[]{:S(2)}, u32[]{:S(2)}) collective-permute-start(bf16[4,192,256]{2,1,0:T(8,128)(2,1)S(1)} %collective-permute-done.10.mix1), channel_id=1, source_target_pairs={{0,1},{1,0},{2,3},{3,2},{4,5},{5,4},{6,7},{7,6},{8,9},{9,8},{10,11... | collective-permute-start | bytes 1179656 | tf_op jit(solution)/shard_map/ppermute | solution.py:341
  114.7 2.6 %collective-permute-start.24 = (bf16[2,256,768]{2,1,0:T(8,128)(2,1)}, bf16[2,256,768]{2,1,0:T(8,128)(2,1)S(1)}, u32[]{:S(2)}, u32[]{:S(2)}) collective-permute-start(bf16[2,256,768]{2,1,0:T(8,128)(2,1)} %get-tuple-element.104), channel_id=1, source_target_pairs={{0,1},{1,0},{2,3},{3,2},{4,5},{5,4},{6,7},{7,6},{8,9},{9,8},{10,11... | collective-permute-start | bytes 2359304 | tf_op jit(solution)/shard_map/ppermute | solution.py:341
  118.6 11.2 %collective-permute-start.25 = (bf16[256,768]{1,0:T(8,128)(2,1)S(1)}, bf16[256,768]{1,0:T(8,128)(2,1)S(1)}, u32[]{:S(2)}, u32[]{:S(2)}) collective-permute-start(bf16[256,768]{1,0:T(8,128)(2,1)S(1)} %fusion.3), channel_id=1, source_target_pairs={{0,2},{2,0},{1,3},{3,1},{4,6},{6,4},{5,7},{7,5},{8,10},{10,8},{9,1... | collective-permute-start | bytes 1179656 | tf_op jit(solution)/shard_map/ppermute | solution.py:345
  128.0 17.3 %collective-permute-start.21 = (bf16[2,256,768]{2,1,0:T(8,128)(2,1)}, bf16[2,256,768]{2,1,0:T(8,128)(2,1)}, u32[]{:S(2)}, u32[]{:S(2)}) collective-permute-start(bf16[2,256,768]{2,1,0:T(8,128)(2,1)} %get-tuple-element.102), channel_id=1, source_target_pairs={{0,1},{1,0},{2,3},{3,2},{4,5},{5,4},{6,7},{7,6},{8,9},{9,8},{10,11... | collective-permute-start | bytes 2359304 | tf_op jit(solution)/shard_map/ppermute | solution.py:341
  130.5 14.8 %copy-start.12 = (bf16[2,256,768]{2,1,0:T(8,128)(2,1)S(1)}, bf16[2,256,768]{2,1,0:T(8,128)(2,1)}, u32[]{:S(2)}) copy-start(bf16[2,256,768]{2,1,0:T(8,128)(2,1)} %get-tuple-element.101) | copy-start | bytes 2359300
  134.8 10.5 %collective-permute-start.27 = (bf16[256,768]{1,0:T(8,128)(2,1)}, bf16[256,768]{1,0:T(8,128)(2,1)S(1)}, u32[]{:S(2)}, u32[]{:S(2)}) collective-permute-start(bf16[256,768]{1,0:T(8,128)(2,1)} %get-tuple-element.107.br0), channel_id=1, source_target_pairs={{0,2},{2,0},{1,3},{3,1},{4,6},{6,4},{5,7},{7,5},{8,10},{10,8},{9,1... | collective-permute-start | bytes 1179656 | tf_op jit(solution)/shard_map/ppermute | solution.py:345
  135.3 37.3 %collective-permute-start.45 = (bf16[4,96,1536]{2,1,0:T(8,128)(2,1)}, bf16[4,96,1536]{2,1,0:T(8,128)(2,1)S(1)}, u32[]{:S(2)}, u32[]{:S(2)}) collective-permute-start(bf16[4,96,1536]{2,1,0:T(8,128)(2,1)} %get-tuple-element.138), channel_id=1, source_target_pairs={{0,4},{4,0},{8,12},{12,8},{16,20},{20,16},{24,28},{28,24},{1,5},{5... | collective-permute-start | bytes 3538952 | tf_op jit(solution)/shard_map/ppermute | solution.py:337
  136.8 9.8 %collective-permute-start.26 = (bf16[256,768]{1,0:T(8,128)(2,1)}, bf16[256,768]{1,0:T(8,128)(2,1)S(1)}, u32[]{:S(2)}, u32[]{:S(2)}) collective-permute-start(bf16[256,768]{1,0:T(8,128)(2,1)} %get-tuple-element.107.br0), channel_id=1, source_target_pairs={{0,1},{1,0},{2,3},{3,2},{4,5},{5,4},{6,7},{7,6},{8,9},{9,8},{10,11... | collective-permute-start | bytes 1179656 | tf_op jit(solution)/shard_map/ppermute | solution.py:341
  145.3 1.7 collective-permute-start.28
  170.0 20.3 %collective-permute-start.29 = (bf16[2,256,768]{2,1,0:T(8,128)(2,1)}, bf16[2,256,768]{2,1,0:T(8,128)(2,1)S(1)}, u32[]{:S(2)}, u32[]{:S(2)}) collective-permute-start(bf16[2,256,768]{2,1,0:T(8,128)(2,1)} %get-tuple-element.118), channel_id=1, source_target_pairs={{0,1},{1,0},{2,3},{3,2},{4,5},{5,4},{6,7},{7,6},{8,9},{9,8},{10,11... | collective-permute-start | bytes 2359304 | tf_op jit(solution)/shard_map/ppermute | solution.py:341
  170.2 15.3 %collective-permute-start.34 = (bf16[4,96,576]{2,1,0:T(8,128)(2,1)}, bf16[4,96,576]{2,1,0:T(8,128)(2,1)}, u32[]{:S(2)}, u32[]{:S(2)}) collective-permute-start(bf16[4,96,576]{2,1,0:T(8,128)(2,1)} %get-tuple-element.113), channel_id=1, source_target_pairs={{0,4},{4,0},{8,12},{12,8},{16,20},{20,16},{24,28},{28,24},{1,5},{5... | collective-permute-start | bytes 1327112 | tf_op jit(solution)/shard_map/ppermute | solution.py:337
  171.6 11.1 %collective-permute-start.22 = (bf16[256,768]{1,0:T(8,128)(2,1)S(1)}, bf16[256,768]{1,0:T(8,128)(2,1)S(1)}, u32[]{:S(2)}, u32[]{:S(2)}) collective-permute-start(bf16[256,768]{1,0:T(8,128)(2,1)S(1)} %fusion.2), channel_id=1, source_target_pairs={{0,2},{2,0},{1,3},{3,1},{4,6},{6,4},{5,7},{7,5},{8,10},{10,8},{9,1... | collective-permute-start | bytes 1179656 | tf_op jit(solution)/shard_map/ppermute | solution.py:345
  176.4 14.6 %collective-permute-start.46 = (bf16[96,1536]{1,0:T(8,128)(2,1)}, bf16[96,1536]{1,0:T(8,128)(2,1)}, u32[]{:S(2)}, u32[]{:S(2)}) collective-permute-start(bf16[96,1536]{1,0:T(8,128)(2,1)} %get-tuple-element.140), channel_id=1, source_target_pairs={{0,8},{4,12},{8,0},{12,4},{16,24},{20,28},{24,16},{28,20},{1,9},{5... | collective-permute-start | bytes 884744 | tf_op jit(solution)/shard_map/ppermute | solution.py:337
  176.4 23.7 %collective-permute-start.47 = (bf16[96,1536]{1,0:T(8,128)(2,1)}, bf16[96,1536]{1,0:T(8,128)(2,1)}, u32[]{:S(2)}, u32[]{:S(2)}) collective-permute-start(bf16[96,1536]{1,0:T(8,128)(2,1)} %get-tuple-element.141), channel_id=1, source_target_pairs={{0,16},{4,20},{8,24},{12,28},{16,0},{20,4},{24,8},{28,12},{1,17},{... | collective-permute-start | bytes 884744 | tf_op jit(solution)/shard_map/ppermute | solution.py:337
  183.5 17.6 %collective-permute-start.48 = (bf16[96,1536]{1,0:T(8,128)(2,1)}, bf16[96,1536]{1,0:T(8,128)(2,1)}, u32[]{:S(2)}, u32[]{:S(2)}) collective-permute-start(bf16[96,1536]{1,0:T(8,128)(2,1)} %get-tuple-element.142), channel_id=1, source_target_pairs={{0,24},{4,28},{8,16},{12,20},{16,8},{20,12},{24,0},{28,4},{1,25},{... | collective-permute-start | bytes 884744 | tf_op jit(solution)/shard_map/ppermute | solution.py:337
  185.5 1.3 collective-permute-start.39
  186.8 26.7 %collective-permute-start.23 = (bf16[256,768]{1,0:T(8,128)(2,1)S(1)}, bf16[256,768]{1,0:T(8,128)(2,1)}, u32[]{:S(2)}, u32[]{:S(2)}) collective-permute-start(bf16[256,768]{1,0:T(8,128)(2,1)S(1)} %fusion.1.own), channel_id=1, source_target_pairs={{0,1},{1,0},{2,3},{3,2},{4,5},{5,4},{6,7},{7,6},{8,9},{9,8},{10,11... | collective-permute-start | bytes 1179656 | tf_op jit(solution)/shard_map/ppermute | solution.py:341
  190.3 53.0 %collective-permute-start.32 = (f32[256,768]{1,0:T(8,128)S(1)}, f32[256,768]{1,0:T(8,128)}, u32[]{:S(2)}, u32[]{:S(2)}) collective-permute-start(f32[256,768]{1,0:T(8,128)S(1)} %copy-done.13), channel_id=1, source_target_pairs={{0,1},{1,0},{2,3},{3,2},{4,5},{5,4},{6,7},{7,6},{8,9},{9,8},{10,11... | collective-permute-start | bytes 2359304 | tf_op jit(solution)/shard_map/ppermute | solution.py:341
  191.0 20.2 %collective-permute-start.40 = (bf16[4,96,256]{2,1,0:T(8,128)(2,1)}, bf16[4,96,256]{2,1,0:T(8,128)(2,1)}, u32[]{:S(2)}, u32[]{:S(2)}) collective-permute-start(bf16[4,96,256]{2,1,0:T(8,128)(2,1)} %get-tuple-element.129), channel_id=1, source_target_pairs={{0,4},{4,0},{8,12},{12,8},{16,20},{20,16},{24,28},{28,24},{1,5},{5... | collective-permute-start | bytes 589832 | tf_op jit(solution)/shard_map/ppermute | solution.py:337
  200.1 15.3 %collective-permute-start.30 = (bf16[256,768]{1,0:T(8,128)(2,1)S(1)}, bf16[256,768]{1,0:T(8,128)(2,1)}, u32[]{:S(2)}, u32[]{:S(2)}) collective-permute-start(bf16[256,768]{1,0:T(8,128)(2,1)S(1)} %fusion.4), channel_id=1, source_target_pairs={{0,2},{2,0},{1,3},{3,1},{4,6},{6,4},{5,7},{7,5},{8,10},{10,8},{9,1... | collective-permute-start | bytes 1179656 | tf_op jit(solution)/shard_map/ppermute | solution.py:345
  202.5 15.2 %copy-start.10 = (bf16[96,1536]{1,0:T(8,128)(2,1)}, bf16[96,1536]{1,0:T(8,128)(2,1)S(1)}, u32[]{:S(2)}) copy-start(bf16[96,1536]{1,0:T(8,128)(2,1)S(1)} %add_convert_fusion.3.own) | copy-start | bytes 884740
  206.4 11.2 %collective-permute-start.35 = (bf16[96,576]{1,0:T(8,128)(2,1)}, bf16[96,576]{1,0:T(8,128)(2,1)}, u32[]{:S(2)}, u32[]{:S(2)}) collective-permute-start(bf16[96,576]{1,0:T(8,128)(2,1)} %get-tuple-element.123), channel_id=1, source_target_pairs={{0,8},{4,12},{8,0},{12,4},{16,24},{20,28},{24,16},{28,20},{1,9},{5... | collective-permute-start | bytes 331784 | tf_op jit(solution)/shard_map/ppermute | solution.py:337
  211.2 12.1 %collective-permute-start.36 = (bf16[96,576]{1,0:T(8,128)(2,1)}, bf16[96,576]{1,0:T(8,128)(2,1)}, u32[]{:S(2)}, u32[]{:S(2)}) collective-permute-start(bf16[96,576]{1,0:T(8,128)(2,1)} %get-tuple-element.124), channel_id=1, source_target_pairs={{0,16},{4,20},{8,24},{12,28},{16,0},{20,4},{24,8},{28,12},{1,17},{... | collective-permute-start | bytes 331784 | tf_op jit(solution)/shard_map/ppermute | solution.py:337
  213.5 18.8 %copy-start.43 = (bf16[96,256]{1,0:T(8,128)(2,1)S(1)}, bf16[96,256]{1,0:T(8,128)(2,1)}, u32[]{:S(2)}) copy-start(bf16[96,256]{1,0:T(8,128)(2,1)} %get-tuple-element.130) | copy-start | bytes 147460
  213.5 9.8 %collective-permute-start.37 = (bf16[96,576]{1,0:T(8,128)(2,1)}, bf16[96,576]{1,0:T(8,128)(2,1)S(1)}, u32[]{:S(2)}, u32[]{:S(2)}) collective-permute-start(bf16[96,576]{1,0:T(8,128)(2,1)} %get-tuple-element.125), channel_id=1, source_target_pairs={{0,24},{4,28},{8,16},{12,20},{16,8},{20,12},{24,0},{28,4},{1,25},{... | collective-permute-start | bytes 331784 | tf_op jit(solution)/shard_map/ppermute | solution.py:337
  215.4 9.8 %collective-permute-start.41 = (bf16[96,256]{1,0:T(8,128)(2,1)}, bf16[96,256]{1,0:T(8,128)(2,1)S(1)}, u32[]{:S(2)}, u32[]{:S(2)}) collective-permute-start(bf16[96,256]{1,0:T(8,128)(2,1)} %get-tuple-element.131), channel_id=1, source_target_pairs={{0,8},{4,12},{8,0},{12,4},{16,24},{20,28},{24,16},{28,20},{1,9},{5... | collective-permute-start | bytes 147464 | tf_op jit(solution)/shard_map/ppermute | solution.py:337
  217.6 17.7 %copy-start.8 = (bf16[256,768]{1,0:T(8,128)(2,1)}, bf16[256,768]{1,0:T(8,128)(2,1)S(1)}, u32[]{:S(2)}) copy-start(bf16[256,768]{1,0:T(8,128)(2,1)S(1)} %fusion.own) | copy-start | bytes 1179652
  217.7 14.6 %collective-permute-start.49 = (bf16[96,1536]{1,0:T(8,128)(2,1)S(1)}, bf16[96,1536]{1,0:T(8,128)(2,1)S(1)}, u32[]{:S(2)}, u32[]{:S(2)}) collective-permute-start(bf16[96,1536]{1,0:T(8,128)(2,1)S(1)} %add_convert_fusion.3.own), channel_id=1, source_target_pairs={{0,2},{2,0},{1,3},{3,1},{4,6},{6,4},{5,7},{7,5},{8,10},{10,8},{9,1... | collective-permute-start | bytes 884744 | tf_op jit(solution)/shard_map/ppermute | solution.py:345
  223.3 5.0 %collective-permute-start.42 = (bf16[96,256]{1,0:T(8,128)(2,1)S(1)}, bf16[96,256]{1,0:T(8,128)(2,1)S(1)}, u32[]{:S(2)}, u32[]{:S(2)}) collective-permute-start(bf16[96,256]{1,0:T(8,128)(2,1)S(1)} %copy-done.47), channel_id=1, source_target_pairs={{0,16},{4,20},{8,24},{12,28},{16,0},{20,4},{24,8},{28,12},{1,17},{... | collective-permute-start | bytes 147464 | tf_op jit(solution)/shard_map/ppermute | solution.py:337
  223.3 6.3 %collective-permute-start.43 = (bf16[96,256]{1,0:T(8,128)(2,1)S(1)}, bf16[96,256]{1,0:T(8,128)(2,1)S(1)}, u32[]{:S(2)}, u32[]{:S(2)}) collective-permute-start(bf16[96,256]{1,0:T(8,128)(2,1)S(1)} %copy-done.46), channel_id=1, source_target_pairs={{0,24},{4,28},{8,16},{12,20},{16,8},{20,12},{24,0},{28,4},{1,25},{... | collective-permute-start | bytes 147464 | tf_op jit(solution)/shard_map/ppermute | solution.py:337
  225.3 18.1 %collective-permute-start.31 = (bf16[256,768]{1,0:T(8,128)(2,1)S(1)}, bf16[256,768]{1,0:T(8,128)(2,1)S(1)}, u32[]{:S(2)}, u32[]{:S(2)}) collective-permute-start(bf16[256,768]{1,0:T(8,128)(2,1)S(1)} %fusion.own), channel_id=1, source_target_pairs={{0,1},{1,0},{2,3},{3,2},{4,5},{5,4},{6,7},{7,6},{8,9},{9,8},{10,11... | collective-permute-start | bytes 1179656 | tf_op jit(solution)/shard_map/ppermute | solution.py:341
  228.2 9.3 %collective-permute-start.33 = (bf16[192,512]{1,0:T(8,128)(2,1)}, bf16[192,512]{1,0:T(8,128)(2,1)S(1)}, u32[]{:S(2)}, u32[]{:S(2)}) collective-permute-start(bf16[192,512]{1,0:T(8,128)(2,1)} %shard_map.249), channel_id=1, source_target_pairs={{2,0},{3,1},{6,4},{7,5},{10,8},{11,9},{14,12},{15,13},{18,16},{19,... | collective-permute-start | bytes 589832 | tf_op jit(solution)/shard_map/ppermute | solution.py:930
  229.5 10.7 %collective-permute-start.38 = (bf16[96,576]{1,0:T(8,128)(2,1)S(1)}, bf16[96,576]{1,0:T(8,128)(2,1)S(1)}, u32[]{:S(2)}, u32[]{:S(2)}) collective-permute-start(bf16[96,576]{1,0:T(8,128)(2,1)S(1)} %add_convert_fusion.4.own), channel_id=1, source_target_pairs={{0,2},{2,0},{1,3},{3,1},{4,6},{6,4},{5,7},{7,5},{8,10},{10,8},{9,1... | collective-permute-start | bytes 331784 | tf_op jit(solution)/shard_map/ppermute | solution.py:345
  232.3 7.9 %collective-permute-start.44 = (bf16[96,256]{1,0:T(8,128)(2,1)S(1)}, bf16[96,256]{1,0:T(8,128)(2,1)S(1)}, u32[]{:S(2)}, u32[]{:S(2)}) collective-permute-start(bf16[96,256]{1,0:T(8,128)(2,1)S(1)} %add_convert_fusion.5.own_proj), channel_id=1, source_target_pairs={{0,2},{2,0},{1,3},{3,1},{4,6},{6,4},{5,7},{7,5},{8,10},{10,8},{9,1... | collective-permute-start | bytes 147464 | tf_op jit(solution)/shard_map/ppermute | solution.py:345
  (34 other events, 116.4 us)
